TPU v7x, 8 devices: a whole 2x2x1 slice. The times are simulated.
8 devices in a mesh: dp: 1 (over z), ep: 8 (over y, x, core).
Axes of the slice: x: 2, y: 2, z: 1, core: 2. Of those that a mesh axis runs over, the one named last changes fastest.
Arguments:
- tokens: bfloat16 [8192, 2560], P(('dp', 'ep'))
- expert_ids: int32 [8192, 6], P(('dp', 'ep'))
- gate_wts: float32 [8192, 6], P(('dp', 'ep'))
- slot_ids: int32 [8192, 6], P(('dp', 'ep'))
- w_gate: bfloat16 [64, 2560, 1536], P('ep')
- w_up: bfloat16 [64, 2560, 1536], P('ep')
- w_down: bfloat16 [64, 1536, 2560], P('ep')
Outputs:
- output: bfloat16 [8192, 2560], P(('dp', 'ep'))
All inputs are finite; a program needn't handle non-finite values.
Results may differ from a plain program's by a relative error of at most 0.001.
Values are sent between devices in bfloat16 or wider.
A program may use at most 1 GiB of HBM per device.

v0:
```python
import functools
import jax
import jax.numpy as jnp
from jax import lax
from jax.sharding import PartitionSpec as P

CAP_NUM = 3
CAP_DEN = 2


def local_share(token_block, src_shard, my_rank, w_gate, w_up, w_down, shard_cap):
    token_blk, ids_blk, gates_blk, slots_blk = token_block
    num_local = w_gate.shape[0]
    tok_dev = token_blk.shape[0]
    local_id = ids_blk - my_rank * num_local
    keep_mask = (slots_blk >= 0) & (local_id >= 0) & (local_id < num_local)
    flat_slot = jnp.where(keep_mask, local_id * shard_cap + slots_blk - src_shard * shard_cap, num_local * shard_cap).reshape(-1)
    tok_index = jnp.broadcast_to(jnp.arange(tok_dev, dtype=jnp.int32)[:, None], ids_blk.shape).reshape(-1)
    slot_token = jnp.full((num_local * shard_cap,), tok_dev, jnp.int32).at[flat_slot].set(tok_index, mode='drop')
    slot_gate = jnp.zeros((num_local * shard_cap,), jnp.float32).at[flat_slot].set(gates_blk.reshape(-1), mode='drop')
    dispatched = jnp.take(token_blk, slot_token, axis=0, mode='fill', fill_value=0).reshape(num_local, shard_cap, -1)
    h_gate = jnp.einsum('ecd,edf->ecf', dispatched, w_gate, preferred_element_type=jnp.float32)
    h_up = jnp.einsum('ecd,edf->ecf', dispatched, w_up, preferred_element_type=jnp.float32)
    hidden = (jax.nn.silu(h_gate) * h_up).astype(jnp.bfloat16)
    expert_out = jnp.einsum('ecf,efd->ecd', hidden, w_down, preferred_element_type=jnp.float32)
    weighted = (expert_out * slot_gate.reshape(num_local, shard_cap, 1)).reshape(num_local * shard_cap, -1)
    return jnp.zeros((tok_dev, token_blk.shape[1]), jnp.float32).at[slot_token].add(weighted, mode='drop')


def solution(mesh):
    group_size = mesh.shape['ep']
    next_perm = [(dev_num, (dev_num + 1) % group_size) for dev_num in range(group_size)]
    row_spec = P(('dp', 'ep'), None)
    expert_spec = P('ep', None, None)

    def per_device(tokens, expert_ids, gate_wts, slot_ids, w_gate, w_up, w_down):
        my_rank = lax.axis_index('ep')
        tok_dev, top_k = expert_ids.shape
        shard_cap = CAP_NUM * tok_dev * top_k // (CAP_DEN * w_gate.shape[0] * group_size)
        expert_share = functools.partial(local_share, my_rank=my_rank, w_gate=w_gate, w_up=w_up, w_down=w_down, shard_cap=shard_cap)
        own_block = (tokens, expert_ids, gate_wts, slot_ids)
        home_part = expert_share(own_block, my_rank)
        visitor = lax.ppermute(own_block, 'ep', next_perm)
        accum = expert_share(visitor, (my_rank - 1) % group_size)

        def pass_on(hop_num, loop_state):
            visitor, accum = loop_state
            visitor, accum = lax.ppermute((visitor, accum), 'ep', next_perm)
            return visitor, accum + expert_share(visitor, (my_rank - hop_num) % group_size)

        visitor, accum = lax.fori_loop(2, group_size, pass_on, (visitor, accum))
        accum = lax.ppermute(accum, 'ep', next_perm)
        return (accum + home_part).astype(jnp.bfloat16)

    return jax.shard_map(per_device, mesh=mesh, in_specs=(row_spec, row_spec, row_spec, row_spec, expert_spec, expert_spec, expert_spec), out_specs=row_spec, check_vma=False)
```

profile of v0, /device:TPU:0, one launch (start us, length us, event | category | flops | bytes accessed | tf_op | source)
XLA Modules:
  0.0 2020.3 jit_solution(8603405151931257566)
XLA Ops:
  7.9 23.0 %scatter_custom_fusion.6 = s32[1152]{0:T(1024)S(1)} fusion(s32[6144]{0:T(1024)S(1)} %bitcast.72, s32[6144]{0:T(1024)S(1)} %reshape.266, s32[]{:T(128)} %constant.140.clone.1), kind=kCustom, calls=%fused_computation.51 | custom fusion | bytes 4612 | tf_op jit(solution)/shard_map/scatter | solution.py:19
  52.5 26.9 %fusion.27 = f32[8,144,1536]{2,1,0:T(8,128)} fusion(bf16[8,144,2560]{2,1,0:T(8,128)(2,1)} %bitcast.66, bf16[8,2560,1536]{2,1,0:T(8,128)(2,1)} %param.15), kind=kOutput, calls=%fused_computation.61 | convolution fusion | flops 9059696640 | bytes 75890688 | tf_op jit(solution)/shard_map/ecd,edf->ecf/dot_general | solution.py:22
  80.1 23.4 %scatter_custom_fusion.3 = s32[1152]{0:T(1024)S(1)} fusion(s32[6144]{0:T(1024)S(1)} %bitcast.74, s32[6144]{0:T(1024)S(1)} %reshape.266, s32[]{:T(128)} %constant.140.clone.1), kind=kCustom, calls=%fused_computation.53 | custom fusion | bytes 4612 | tf_op jit(solution)/shard_map/scatter | solution.py:19
  149.1 26.7 %fusion.26 = f32[8,144,1536]{2,1,0:T(8,128)} fusion(bf16[8,144,2560]{2,1,0:T(8,128)(2,1)} %bitcast.68, bf16[8,2560,1536]{2,1,0:T(8,128)(2,1)} %param.15), kind=kOutput, calls=%fused_computation.60 | convolution fusion | flops 9059696640 | bytes 75890688 | tf_op jit(solution)/shard_map/ecd,edf->ecf/dot_general | solution.py:22
  175.8 26.3 %multiply_convert_fusion.12 = bf16[8,144,1536]{2,1,0:T(8,128)(2,1)S(1)} fusion(f32[8,144,1536]{2,1,0:T(8,128)} %fusion.26, bf16[8,144,2560]{2,1,0:T(8,128)(2,1)} %bitcast.69, bf16[8,2560,1536]{2,1,0:T(8,128)(2,1)} %param.16), kind=kOutput, calls=%fused_computation.29.clone.clone.clone.clone | convolution fusion | flops 9070313472 | bytes 79429632 | tf_op jit(solution)/shard_map/ecd,edf->ecf/dot_general | solution.py:23
  202.1 27.2 %broadcast_multiply_fusion.1 = f32[8,144,2560]{2,1,0:T(8,128)} fusion(f32[8,144]{1,0:T(8,128)S(1)} %copy-done.4, bf16[8,1536,2560]{2,1,0:T(8,128)(2,1)} %param.17, bf16[8,144,1536]{2,1,0:T(8,128)(2,1)S(1)} %multiply_convert_fusion.12), kind=kOutput, calls=%fused_computation.30 | convolution fusion | flops 9062645760 | bytes 78254592 | tf_op jit(solution)/shard_map/ecf,efd->ecd/dot_general | solution.py:25
  229.3 29.8 %scatter_custom_fusion.5 = f32[1024,2560]{1,0:T(8,128)} fusion(s32[1152]{0:T(1024)} %copy-done.16, f32[1152,2560]{1,0:T(8,128)} %bitcast.65, f32[]{:T(128)} %constant.139.clone.1), kind=kCustom, calls=%fused_computation.33 | custom fusion | flops 2949120 | bytes 10486272 | tf_op jit(solution)/shard_map/scatter-add | solution.py:27
  259.2 1604.6 %while.23 = (s32[]{:T(128)}, bf16[1024,2560]{1,0:T(8,128)(2,1)}, s32[1024,6]{0,1:T(8,128)S(1)}, f32[1024,6]{1,0:T(8,128)S(1)}, s32[1024,6]{0,1:T(8,128)S(1)}, /*...) while((s32[]{:T(128)}, bf16[1024,2560]{1,0:T(8,128)(2,1)}, ...), condition=%wide.region_7.9_spmd, body=%wide.region_3.0_spmd.sunk | while | flops 27198646272 | bytes 388123072 | solution.py:51
  278.8 58.3 %collective-permute-done.1 = s32[1024,6]{0,1:T(8,128)S(1)} collective-permute-done((s32[1024,6]{0,1:T(8,128)S(1)}, s32[1024,6]{0,1:T(8,128)S(1)}, u32[]{:S(2)}, u32[]{:S(2)}) %collective-permute-start.1) | collective-permute-done | bytes 24608 | tf_op jit(solution)/shard_map/while/body/eval_jaxpr/ppermute | solution.py:48
  343.4 23.0 %scatter_custom_fusion.24 = f32[1152]{0:T(1024)S(1)} fusion(s32[6144]{0:T(1024)S(1)} %bitcast.70, f32[6144]{0:T(1024)S(1)} %reshape.333, f32[]{:T(128)} %constant.139.clone.1..sunk), kind=kCustom, calls=%fused_computation.22.clone.1 | custom fusion | bytes 4612 | tf_op jit(solution)/shard_map/while/body/eval_jaxpr/scatter | solution.py:20
  414.2 26.7 %fusion.79 = f32[8,144,1536]{2,1,0:T(8,128)} fusion(bf16[8,144,2560]{2,1,0:T(8,128)(2,1)} %bitcast.62, bf16[8,2560,1536]{2,1,0:T(8,128)(2,1)} %get-tuple-element.391), kind=kOutput, calls=%fused_computation.59.clone.1 | convolution fusion | flops 9059696640 | bytes 75890688 | tf_op jit(solution)/shard_map/while/body/eval_jaxpr/ecd,edf->ecf/dot_general | solution.py:22
  440.9 26.3 %multiply_convert_fusion.14 = bf16[8,144,1536]{2,1,0:T(8,128)(2,1)S(1)} fusion(f32[8,144,1536]{2,1,0:T(8,128)} %fusion.79, bf16[8,144,2560]{2,1,0:T(8,128)(2,1)} %bitcast.63, bf16[8,2560,1536]{2,1,0:T(8,128)(2,1)} %get-tuple-element.392), kind=kOutput, calls=%fused_computation.12.clone.clone.clone.clone.1.clone.1 | convolution fusion | flops 9070313472 | bytes 79429632 | tf_op jit(solution)/shard_map/while/body/eval_jaxpr/ecd,edf->ecf/dot_general | solution.py:23
  472.3 27.0 %broadcast_multiply_fusion.3 = f32[8,144,2560]{2,1,0:T(8,128)} fusion(f32[8,144]{1,0:T(8,128)S(1)} %copy-done, bf16[8,1536,2560]{2,1,0:T(8,128)(2,1)} %get-tuple-element.393, bf16[8,144,1536]{2,1,0:T(8,128)(2,1)S(1)} %multiply_convert_fusion.14), kind=kOutput, calls=%fused_computation.13.clone.2 | convolution fusion | flops 9062645760 | bytes 78254592 | tf_op jit(solution)/shard_map/while/body/eval_jaxpr/ecf,efd->ecd/dot_general | solution.py:25
  499.3 33.1 %scatter_fusion = f32[1024,2560]{1,0:T(8,128)} fusion(f32[1024,2560]{1,0:T(8,128)} %collective-permute-done.4, s32[1152]{0:T(1024)S(1)} %copy-done.3, f32[1152,2560]{1,0:T(8,128)} %bitcast.61), kind=kCustom, calls=%fused_computation.5.clone.1 | custom fusion | flops 2949120 | bytes 35394048 | tf_op jit(solution)/shard_map/while/body/eval_jaxpr/scatter-add | solution.py:27
  543.2 58.3 %collective-permute-done.1 = s32[1024,6]{0,1:T(8,128)S(1)} collective-permute-done((s32[1024,6]{0,1:T(8,128)S(1)}, s32[1024,6]{0,1:T(8,128)S(1)}, u32[]{:S(2)}, u32[]{:S(2)}) %collective-permute-start.1) | collective-permute-done | bytes 24608 | tf_op jit(solution)/shard_map/while/body/eval_jaxpr/ppermute | solution.py:48
  607.9 23.0 %scatter_custom_fusion.24 = f32[1152]{0:T(1024)S(1)} fusion(s32[6144]{0:T(1024)S(1)} %bitcast.70, f32[6144]{0:T(1024)S(1)} %reshape.333, f32[]{:T(128)} %constant.139.clone.1..sunk), kind=kCustom, calls=%fused_computation.22.clone.1 | custom fusion | bytes 4612 | tf_op jit(solution)/shard_map/while/body/eval_jaxpr/scatter | solution.py:20
  678.6 26.7 %fusion.79 = f32[8,144,1536]{2,1,0:T(8,128)} fusion(bf16[8,144,2560]{2,1,0:T(8,128)(2,1)} %bitcast.62, bf16[8,2560,1536]{2,1,0:T(8,128)(2,1)} %get-tuple-element.391), kind=kOutput, calls=%fused_computation.59.clone.1 | convolution fusion | flops 9059696640 | bytes 75890688 | tf_op jit(solution)/shard_map/while/body/eval_jaxpr/ecd,edf->ecf/dot_general | solution.py:22
  705.3 26.3 %multiply_convert_fusion.14 = bf16[8,144,1536]{2,1,0:T(8,128)(2,1)S(1)} fusion(f32[8,144,1536]{2,1,0:T(8,128)} %fusion.79, bf16[8,144,2560]{2,1,0:T(8,128)(2,1)} %bitcast.63, bf16[8,2560,1536]{2,1,0:T(8,128)(2,1)} %get-tuple-element.392), kind=kOutput, calls=%fused_computation.12.clone.clone.clone.clone.1.clone.1 | convolution fusion | flops 9070313472 | bytes 79429632 | tf_op jit(solution)/shard_map/while/body/eval_jaxpr/ecd,edf->ecf/dot_general | solution.py:23
  736.8 27.0 %broadcast_multiply_fusion.3 = f32[8,144,2560]{2,1,0:T(8,128)} fusion(f32[8,144]{1,0:T(8,128)S(1)} %copy-done, bf16[8,1536,2560]{2,1,0:T(8,128)(2,1)} %get-tuple-element.393, bf16[8,144,1536]{2,1,0:T(8,128)(2,1)S(1)} %multiply_convert_fusion.14), kind=kOutput, calls=%fused_computation.13.clone.2 | convolution fusion | flops 9062645760 | bytes 78254592 | tf_op jit(solution)/shard_map/while/body/eval_jaxpr/ecf,efd->ecd/dot_general | solution.py:25
  763.8 33.1 %scatter_fusion = f32[1024,2560]{1,0:T(8,128)} fusion(f32[1024,2560]{1,0:T(8,128)} %collective-permute-done.4, s32[1152]{0:T(1024)S(1)} %copy-done.3, f32[1152,2560]{1,0:T(8,128)} %bitcast.61), kind=kCustom, calls=%fused_computation.5.clone.1 | custom fusion | flops 2949120 | bytes 35394048 | tf_op jit(solution)/shard_map/while/body/eval_jaxpr/scatter-add | solution.py:27
  807.7 58.3 %collective-permute-done.1 = s32[1024,6]{0,1:T(8,128)S(1)} collective-permute-done((s32[1024,6]{0,1:T(8,128)S(1)}, s32[1024,6]{0,1:T(8,128)S(1)}, u32[]{:S(2)}, u32[]{:S(2)}) %collective-permute-start.1) | collective-permute-done | bytes 24608 | tf_op jit(solution)/shard_map/while/body/eval_jaxpr/ppermute | solution.py:48
  872.3 23.0 %scatter_custom_fusion.24 = f32[1152]{0:T(1024)S(1)} fusion(s32[6144]{0:T(1024)S(1)} %bitcast.70, f32[6144]{0:T(1024)S(1)} %reshape.333, f32[]{:T(128)} %constant.139.clone.1..sunk), kind=kCustom, calls=%fused_computation.22.clone.1 | custom fusion | bytes 4612 | tf_op jit(solution)/shard_map/while/body/eval_jaxpr/scatter | solution.py:20
  943.1 26.7 %fusion.79 = f32[8,144,1536]{2,1,0:T(8,128)} fusion(bf16[8,144,2560]{2,1,0:T(8,128)(2,1)} %bitcast.62, bf16[8,2560,1536]{2,1,0:T(8,128)(2,1)} %get-tuple-element.391), kind=kOutput, calls=%fused_computation.59.clone.1 | convolution fusion | flops 9059696640 | bytes 75890688 | tf_op jit(solution)/shard_map/while/body/eval_jaxpr/ecd,edf->ecf/dot_general | solution.py:22
  969.8 26.3 %multiply_convert_fusion.14 = bf16[8,144,1536]{2,1,0:T(8,128)(2,1)S(1)} fusion(f32[8,144,1536]{2,1,0:T(8,128)} %fusion.79, bf16[8,144,2560]{2,1,0:T(8,128)(2,1)} %bitcast.63, bf16[8,2560,1536]{2,1,0:T(8,128)(2,1)} %get-tuple-element.392), kind=kOutput, calls=%fused_computation.12.clone.clone.clone.clone.1.clone.1 | convolution fusion | flops 9070313472 | bytes 79429632 | tf_op jit(solution)/shard_map/while/body/eval_jaxpr/ecd,edf->ecf/dot_general | solution.py:23
  1001.2 27.0 %broadcast_multiply_fusion.3 = f32[8,144,2560]{2,1,0:T(8,128)} fusion(f32[8,144]{1,0:T(8,128)S(1)} %copy-done, bf16[8,1536,2560]{2,1,0:T(8,128)(2,1)} %get-tuple-element.393, bf16[8,144,1536]{2,1,0:T(8,128)(2,1)S(1)} %multiply_convert_fusion.14), kind=kOutput, calls=%fused_computation.13.clone.2 | convolution fusion | flops 9062645760 | bytes 78254592 | tf_op jit(solution)/shard_map/while/body/eval_jaxpr/ecf,efd->ecd/dot_general | solution.py:25
  1028.2 33.1 %scatter_fusion = f32[1024,2560]{1,0:T(8,128)} fusion(f32[1024,2560]{1,0:T(8,128)} %collective-permute-done.4, s32[1152]{0:T(1024)S(1)} %copy-done.3, f32[1152,2560]{1,0:T(8,128)} %bitcast.61), kind=kCustom, calls=%fused_computation.5.clone.1 | custom fusion | flops 2949120 | bytes 35394048 | tf_op jit(solution)/shard_map/while/body/eval_jaxpr/scatter-add | solution.py:27
  1072.1 58.3 %collective-permute-done.1 = s32[1024,6]{0,1:T(8,128)S(1)} collective-permute-done((s32[1024,6]{0,1:T(8,128)S(1)}, s32[1024,6]{0,1:T(8,128)S(1)}, u32[]{:S(2)}, u32[]{:S(2)}) %collective-permute-start.1) | collective-permute-done | bytes 24608 | tf_op jit(solution)/shard_map/while/body/eval_jaxpr/ppermute | solution.py:48
  1136.8 23.0 %scatter_custom_fusion.24 = f32[1152]{0:T(1024)S(1)} fusion(s32[6144]{0:T(1024)S(1)} %bitcast.70, f32[6144]{0:T(1024)S(1)} %reshape.333, f32[]{:T(128)} %constant.139.clone.1..sunk), kind=kCustom, calls=%fused_computation.22.clone.1 | custom fusion | bytes 4612 | tf_op jit(solution)/shard_map/while/body/eval_jaxpr/scatter | solution.py:20
  1207.5 26.7 %fusion.79 = f32[8,144,1536]{2,1,0:T(8,128)} fusion(bf16[8,144,2560]{2,1,0:T(8,128)(2,1)} %bitcast.62, bf16[8,2560,1536]{2,1,0:T(8,128)(2,1)} %get-tuple-element.391), kind=kOutput, calls=%fused_computation.59.clone.1 | convolution fusion | flops 9059696640 | bytes 75890688 | tf_op jit(solution)/shard_map/while/body/eval_jaxpr/ecd,edf->ecf/dot_general | solution.py:22
  1234.2 26.3 %multiply_convert_fusion.14 = bf16[8,144,1536]{2,1,0:T(8,128)(2,1)S(1)} fusion(f32[8,144,1536]{2,1,0:T(8,128)} %fusion.79, bf16[8,144,2560]{2,1,0:T(8,128)(2,1)} %bitcast.63, bf16[8,2560,1536]{2,1,0:T(8,128)(2,1)} %get-tuple-element.392), kind=kOutput, calls=%fused_computation.12.clone.clone.clone.clone.1.clone.1 | convolution fusion | flops 9070313472 | bytes 79429632 | tf_op jit(solution)/shard_map/while/body/eval_jaxpr/ecd,edf->ecf/dot_general | solution.py:23
  1265.6 27.0 %broadcast_multiply_fusion.3 = f32[8,144,2560]{2,1,0:T(8,128)} fusion(f32[8,144]{1,0:T(8,128)S(1)} %copy-done, bf16[8,1536,2560]{2,1,0:T(8,128)(2,1)} %get-tuple-element.393, bf16[8,144,1536]{2,1,0:T(8,128)(2,1)S(1)} %multiply_convert_fusion.14), kind=kOutput, calls=%fused_computation.13.clone.2 | convolution fusion | flops 9062645760 | bytes 78254592 | tf_op jit(solution)/shard_map/while/body/eval_jaxpr/ecf,efd->ecd/dot_general | solution.py:25
  1292.6 33.1 %scatter_fusion = f32[1024,2560]{1,0:T(8,128)} fusion(f32[1024,2560]{1,0:T(8,128)} %collective-permute-done.4, s32[1152]{0:T(1024)S(1)} %copy-done.3, f32[1152,2560]{1,0:T(8,128)} %bitcast.61), kind=kCustom, calls=%fused_computation.5.clone.1 | custom fusion | flops 2949120 | bytes 35394048 | tf_op jit(solution)/shard_map/while/body/eval_jaxpr/scatter-add | solution.py:27
  1336.6 58.3 %collective-permute-done.1 = s32[1024,6]{0,1:T(8,128)S(1)} collective-permute-done((s32[1024,6]{0,1:T(8,128)S(1)}, s32[1024,6]{0,1:T(8,128)S(1)}, u32[]{:S(2)}, u32[]{:S(2)}) %collective-permute-start.1) | collective-permute-done | bytes 24608 | tf_op jit(solution)/shard_map/while/body/eval_jaxpr/ppermute | solution.py:48
  1401.2 23.0 %scatter_custom_fusion.24 = f32[1152]{0:T(1024)S(1)} fusion(s32[6144]{0:T(1024)S(1)} %bitcast.70, f32[6144]{0:T(1024)S(1)} %reshape.333, f32[]{:T(128)} %constant.139.clone.1..sunk), kind=kCustom, calls=%fused_computation.22.clone.1 | custom fusion | bytes 4612 | tf_op jit(solution)/shard_map/while/body/eval_jaxpr/scatter | solution.py:20
  1472.0 26.7 %fusion.79 = f32[8,144,1536]{2,1,0:T(8,128)} fusion(bf16[8,144,2560]{2,1,0:T(8,128)(2,1)} %bitcast.62, bf16[8,2560,1536]{2,1,0:T(8,128)(2,1)} %get-tuple-element.391), kind=kOutput, calls=%fused_computation.59.clone.1 | convolution fusion | flops 9059696640 | bytes 75890688 | tf_op jit(solution)/shard_map/while/body/eval_jaxpr/ecd,edf->ecf/dot_general | solution.py:22
  1498.7 26.3 %multiply_convert_fusion.14 = bf16[8,144,1536]{2,1,0:T(8,128)(2,1)S(1)} fusion(f32[8,144,1536]{2,1,0:T(8,128)} %fusion.79, bf16[8,144,2560]{2,1,0:T(8,128)(2,1)} %bitcast.63, bf16[8,2560,1536]{2,1,0:T(8,128)(2,1)} %get-tuple-element.392), kind=kOutput, calls=%fused_computation.12.clone.clone.clone.clone.1.clone.1 | convolution fusion | flops 9070313472 | bytes 79429632 | tf_op jit(solution)/shard_map/while/body/eval_jaxpr/ecd,edf->ecf/dot_general | solution.py:23
  1530.1 27.0 %broadcast_multiply_fusion.3 = f32[8,144,2560]{2,1,0:T(8,128)} fusion(f32[8,144]{1,0:T(8,128)S(1)} %copy-done, bf16[8,1536,2560]{2,1,0:T(8,128)(2,1)} %get-tuple-element.393, bf16[8,144,1536]{2,1,0:T(8,128)(2,1)S(1)} %multiply_convert_fusion.14), kind=kOutput, calls=%fused_computation.13.clone.2 | convolution fusion | flops 9062645760 | bytes 78254592 | tf_op jit(solution)/shard_map/while/body/eval_jaxpr/ecf,efd->ecd/dot_general | solution.py:25
  1557.1 33.1 %scatter_fusion = f32[1024,2560]{1,0:T(8,128)} fusion(f32[1024,2560]{1,0:T(8,128)} %collective-permute-done.4, s32[1152]{0:T(1024)S(1)} %copy-done.3, f32[1152,2560]{1,0:T(8,128)} %bitcast.61), kind=kCustom, calls=%fused_computation.5.clone.1 | custom fusion | flops 2949120 | bytes 35394048 | tf_op jit(solution)/shard_map/while/body/eval_jaxpr/scatter-add | solution.py:27
  1601.0 58.3 %collective-permute-done.1 = s32[1024,6]{0,1:T(8,128)S(1)} collective-permute-done((s32[1024,6]{0,1:T(8,128)S(1)}, s32[1024,6]{0,1:T(8,128)S(1)}, u32[]{:S(2)}, u32[]{:S(2)}) %collective-permute-start.1) | collective-permute-done | bytes 24608 | tf_op jit(solution)/shard_map/while/body/eval_jaxpr/ppermute | solution.py:48
  1736.4 26.7 %fusion.79 = f32[8,144,1536]{2,1,0:T(8,128)} fusion(bf16[8,144,2560]{2,1,0:T(8,128)(2,1)} %bitcast.62, bf16[8,2560,1536]{2,1,0:T(8,128)(2,1)} %get-tuple-element.391), kind=kOutput, calls=%fused_computation.59.clone.1 | convolution fusion | flops 9059696640 | bytes 75890688 | tf_op jit(solution)/shard_map/while/body/eval_jaxpr/ecd,edf->ecf/dot_general | solution.py:22
  1763.1 26.3 %multiply_convert_fusion.14 = bf16[8,144,1536]{2,1,0:T(8,128)(2,1)S(1)} fusion(f32[8,144,1536]{2,1,0:T(8,128)} %fusion.79, bf16[8,144,2560]{2,1,0:T(8,128)(2,1)} %bitcast.63, bf16[8,2560,1536]{2,1,0:T(8,128)(2,1)} %get-tuple-element.392), kind=kOutput, calls=%fused_computation.12.clone.clone.clone.clone.1.clone.1 | convolution fusion | flops 9070313472 | bytes 79429632 | tf_op jit(solution)/shard_map/while/body/eval_jaxpr/ecd,edf->ecf/dot_general | solution.py:23
  1794.5 27.0 %broadcast_multiply_fusion.3 = f32[8,144,2560]{2,1,0:T(8,128)} fusion(f32[8,144]{1,0:T(8,128)S(1)} %copy-done, bf16[8,1536,2560]{2,1,0:T(8,128)(2,1)} %get-tuple-element.393, bf16[8,144,1536]{2,1,0:T(8,128)(2,1)S(1)} %multiply_convert_fusion.14), kind=kOutput, calls=%fused_computation.13.clone.2 | convolution fusion | flops 9062645760 | bytes 78254592 | tf_op jit(solution)/shard_map/while/body/eval_jaxpr/ecf,efd->ecd/dot_general | solution.py:25
  1821.5 33.1 %scatter_fusion = f32[1024,2560]{1,0:T(8,128)} fusion(f32[1024,2560]{1,0:T(8,128)} %collective-permute-done.4, s32[1152]{0:T(1024)S(1)} %copy-done.3, f32[1152,2560]{1,0:T(8,128)} %bitcast.61), kind=kCustom, calls=%fused_computation.5.clone.1 | custom fusion | flops 2949120 | bytes 35394048 | tf_op jit(solution)/shard_map/while/body/eval_jaxpr/scatter-add | solution.py:27
  1863.8 26.3 %multiply_convert_fusion.4.clone.4 = bf16[8,144,1536]{2,1,0:T(8,128)(2,1)S(1)} fusion(f32[8,144,1536]{2,1,0:T(8,128)} %fusion.27, bf16[8,144,2560]{2,1,0:T(8,128)(2,1)} %bitcast.67, bf16[8,2560,1536]{2,1,0:T(8,128)(2,1)} %get-tuple-element.418), kind=kOutput, calls=%fused_computation.28.clone.clone.clone.1 | convolution fusion | flops 9070313472 | bytes 79429632 | tf_op jit(solution)/shard_map/ecd,edf->ecf/dot_general | solution.py:23
  1892.1 23.1 %scatter_custom_fusion.7 = f32[1152]{0:T(1024)S(1)} fusion(s32[6144]{0:T(1024)} %bitcast.73, f32[6144]{0:T(1024)} %reshape.274, f32[]{:T(128)} %constant.139.clone.1), kind=kCustom, calls=%fused_computation.47 | custom fusion | bytes 5120 | tf_op jit(solution)/shard_map/scatter | solution.py:20
  1915.3 27.2 %convolution_multiply_fusion = f32[8,144,2560]{2,1,0:T(8,128)} fusion(bf16[8,1536,2560]{2,1,0:T(8,128)(2,1)} %get-tuple-element.402, f32[8,144]{1,0:T(8,128)S(1)} %mul.141, bf16[8,144,1536]{2,1,0:T(8,128)(2,1)S(1)} %multiply_convert_fusion.4.clone.4), kind=kOutput, calls=%fused_computation.27 | convolution fusion | flops 9062645760 | bytes 78254592 | tf_op jit(solution)/shard_map/ecf,efd->ecd/dot_general | solution.py:25
  1942.5 37.5 %collective-permute-done.9 = f32[1024,2560]{1,0:T(8,128)} collective-permute-done((f32[1024,2560]{1,0:T(8,128)}, f32[1024,2560]{1,0:T(8,128)}, u32[]{:S(2)}, u32[]{:S(2)}) %collective-permute-start.9) | collective-permute-done | bytes 10485792 | tf_op jit(solution)/shard_map/ppermute | solution.py:52
  1980.0 33.1 %scatter_fusion.1 = f32[1024,2560]{1,0:T(8,128)} fusion(f32[1024,2560]{1,0:T(8,128)} %collective-permute-done.9, s32[1152]{0:T(1024)S(1)} %copy-done.9, f32[1152,2560]{1,0:T(8,128)} %bitcast.64), kind=kCustom, calls=%fused_computation.11 | custom fusion | flops 2949120 | bytes 35394048 | tf_op jit(solution)/shard_map/scatter-add | solution.py:27
  (301 shorter events, 527.1 us)
Async XLA Ops:
  0.0 127.6 %collective-permute-start.5 = (bf16[1024,2560]{1,0:T(8,128)(2,1)}, bf16[1024,2560]{1,0:T(8,128)(2,1)}, u32[]{:S(2)}, u32[]{:S(2)}) collective-permute-start(bf16[1024,2560]{1,0:T(8,128)(2,1)} %param.11), channel_id=1, source_target_pairs={{0,1},{1,2},{2,3},{3,4},{4,5},{5,6},{6,7},{7,0}} | collective-permute-start | bytes 15728648 | tf_op jit(solution)/shard_map/ppermute | solution.py:43
  0.9 78.5 %collective-permute-start.6 = (s32[1024,6]{0,1:T(8,128)}, s32[1024,6]{0,1:T(8,128)S(1)}, u32[]{:S(2)}, u32[]{:S(2)}) collective-permute-start(s32[1024,6]{0,1:T(8,128)} %param.12), channel_id=1, source_target_pairs={{0,1},{1,2},{2,3},{3,4},{4,5},{5,6},{6,7},{7,0}} | collective-permute-start | bytes 73736 | tf_op jit(solution)/shard_map/ppermute | solution.py:43
  4.4 42.3 %copy-start.1 = (f32[1024,6]{1,0:T(8,128)}, f32[1024,6]{1,0:T(8,128)S(1)}, u32[]{:S(2)}) copy-start(f32[1024,6]{1,0:T(8,128)S(1)} %copy.19) | copy-start | bytes 73732
  4.4 99.1 %collective-permute-start.7 = (f32[1024,6]{1,0:T(8,128)S(1)}, f32[1024,6]{1,0:T(8,128)S(1)}, u32[]{:S(2)}, u32[]{:S(2)}) collective-permute-start(f32[1024,6]{1,0:T(8,128)S(1)} %copy.19), channel_id=1, source_target_pairs={{0,1},{1,2},{2,3},{3,4},{4,5},{5,6},{6,7},{7,0}} | collective-permute-start | bytes 73736 | tf_op jit(solution)/shard_map/ppermute | solution.py:43
  4.5 74.9 %collective-permute-start.8 = (s32[1024,6]{0,1:T(8,128)}, s32[1024,6]{0,1:T(8,128)S(1)}, u32[]{:S(2)}, u32[]{:S(2)}) collective-permute-start(s32[1024,6]{0,1:T(8,128)} %param.14), channel_id=1, source_target_pairs={{0,1},{1,2},{2,3},{3,4},{4,5},{5,6},{6,7},{7,0}} | collective-permute-start | bytes 73736 | tf_op jit(solution)/shard_map/ppermute | solution.py:43
  7.9 38.9 %copy-start.17 = (s32[6144,1]{0,1:T(1,128)}, s32[6144,1]{0,1:T(1,128)S(1)}, u32[]{:S(2)}) copy-start(s32[6144,1]{0,1:T(1,128)S(1)} %compare_select_fusion.2) | copy-start | bytes 73732
  79.4 64.1 %copy-start.10 = (s32[1024,6]{0,1:T(8,128)}, s32[1024,6]{0,1:T(8,128)S(1)}, u32[]{:S(2)}) copy-start(s32[1024,6]{0,1:T(8,128)S(1)} %collective-permute-done.6) | copy-start | bytes 73732
  79.4 64.0 %copy-start.13 = (s32[1024,6]{0,1:T(8,128)}, s32[1024,6]{0,1:T(8,128)S(1)}, u32[]{:S(2)}) copy-start(s32[1024,6]{0,1:T(8,128)S(1)} %collective-permute-done.8) | copy-start | bytes 73732
  103.5 39.9 %copy-start.5 = (f32[1024,6]{1,0:T(8,128)}, f32[1024,6]{1,0:T(8,128)S(1)}, u32[]{:S(2)}) copy-start(f32[1024,6]{1,0:T(8,128)S(1)} %collective-permute-done.7) | copy-start | bytes 73732
  229.3 29.8 %copy-start.6 = (f32[1024,6]{1,0:T(8,128)S(1)}, f32[1024,6]{1,0:T(8,128)}, u32[]{:S(2)}) copy-start(f32[1024,6]{1,0:T(8,128)} %copy-done.5) | copy-start | bytes 73732
  229.3 29.8 %copy-start.11 = (s32[1024,6]{0,1:T(8,128)S(1)}, s32[1024,6]{0,1:T(8,128)}, u32[]{:S(2)}) copy-start(s32[1024,6]{0,1:T(8,128)} %copy-done.10) | copy-start | bytes 73732
  229.3 29.8 %copy-start.14 = (s32[1024,6]{0,1:T(8,128)S(1)}, s32[1024,6]{0,1:T(8,128)}, u32[]{:S(2)}) copy-start(s32[1024,6]{0,1:T(8,128)} %copy-done.13) | copy-start | bytes 73732
  276.7 116.1 %collective-permute-start = (bf16[1024,2560]{1,0:T(8,128)(2,1)}, bf16[1024,2560]{1,0:T(8,128)(2,1)}, u32[]{:S(2)}, u32[]{:S(2)}) collective-permute-start(bf16[1024,2560]{1,0:T(8,128)(2,1)} %get-tuple-element.365), channel_id=1, source_target_pairs={{0,1},{1,2},{2,3},{3,4},{4,5},{5,6},{6,7},{7,0}} | collective-permute-start | bytes 15728648 | tf_op jit(solution)/shard_map/while/body/eval_jaxpr/ppermute | solution.py:48
  276.7 60.4 %collective-permute-start.1 = (s32[1024,6]{0,1:T(8,128)S(1)}, s32[1024,6]{0,1:T(8,128)S(1)}, u32[]{:S(2)}, u32[]{:S(2)}) collective-permute-start(s32[1024,6]{0,1:T(8,128)S(1)} %get-tuple-element.366), channel_id=1, source_target_pairs={{0,1},{1,2},{2,3},{3,4},{4,5},{5,6},{6,7},{7,0}} | collective-permute-start | bytes 73736 | tf_op jit(solution)/shard_map/while/body/eval_jaxpr/ppermute | solution.py:48
  278.3 59.1 %collective-permute-start.3 = (s32[1024,6]{0,1:T(8,128)S(1)}, s32[1024,6]{0,1:T(8,128)S(1)}, u32[]{:S(2)}, u32[]{:S(2)}) collective-permute-start(s32[1024,6]{0,1:T(8,128)S(1)} %get-tuple-element.368), channel_id=1, source_target_pairs={{0,1},{1,2},{2,3},{3,4},{4,5},{5,6},{6,7},{7,0}} | collective-permute-start | bytes 73736 | tf_op jit(solution)/shard_map/while/body/eval_jaxpr/ppermute | solution.py:48
  278.3 64.7 %collective-permute-start.2 = (f32[1024,6]{1,0:T(8,128)S(1)}, f32[1024,6]{1,0:T(8,128)S(1)}, u32[]{:S(2)}, u32[]{:S(2)}) collective-permute-start(f32[1024,6]{1,0:T(8,128)S(1)} %get-tuple-element.367), channel_id=1, source_target_pairs={{0,1},{1,2},{2,3},{3,4},{4,5},{5,6},{6,7},{7,0}} | collective-permute-start | bytes 73736 | tf_op jit(solution)/shard_map/while/body/eval_jaxpr/ppermute | solution.py:48
  278.4 220.9 %collective-permute-start.4 = (f32[1024,2560]{1,0:T(8,128)}, f32[1024,2560]{1,0:T(8,128)}, u32[]{:S(2)}, u32[]{:S(2)}) collective-permute-start(f32[1024,2560]{1,0:T(8,128)} %get-tuple-element.369), channel_id=1, source_target_pairs={{0,1},{1,2},{2,3},{3,4},{4,5},{5,6},{6,7},{7,0}} | collective-permute-start | bytes 31457288 | tf_op jit(solution)/shard_map/while/body/eval_jaxpr/ppermute | solution.py:48
  472.3 27.0 %copy-start.3 = (s32[1152]{0:T(1024)S(1)}, s32[1152]{0:T(1024)}, u32[]{:S(2)}) copy-start(s32[1152]{0:T(1024)} %copy-done.2) | copy-start | bytes 13828 | tf_op jit(solution)/shard_map/while
  541.1 116.1 %collective-permute-start = (bf16[1024,2560]{1,0:T(8,128)(2,1)}, bf16[1024,2560]{1,0:T(8,128)(2,1)}, u32[]{:S(2)}, u32[]{:S(2)}) collective-permute-start(bf16[1024,2560]{1,0:T(8,128)(2,1)} %get-tuple-element.365), channel_id=1, source_target_pairs={{0,1},{1,2},{2,3},{3,4},{4,5},{5,6},{6,7},{7,0}} | collective-permute-start | bytes 15728648 | tf_op jit(solution)/shard_map/while/body/eval_jaxpr/ppermute | solution.py:48
  541.2 60.4 %collective-permute-start.1 = (s32[1024,6]{0,1:T(8,128)S(1)}, s32[1024,6]{0,1:T(8,128)S(1)}, u32[]{:S(2)}, u32[]{:S(2)}) collective-permute-start(s32[1024,6]{0,1:T(8,128)S(1)} %get-tuple-element.366), channel_id=1, source_target_pairs={{0,1},{1,2},{2,3},{3,4},{4,5},{5,6},{6,7},{7,0}} | collective-permute-start | bytes 73736 | tf_op jit(solution)/shard_map/while/body/eval_jaxpr/ppermute | solution.py:48
  541.9 60.1 %collective-permute-start.3 = (s32[1024,6]{0,1:T(8,128)S(1)}, s32[1024,6]{0,1:T(8,128)S(1)}, u32[]{:S(2)}, u32[]{:S(2)}) collective-permute-start(s32[1024,6]{0,1:T(8,128)S(1)} %get-tuple-element.368), channel_id=1, source_target_pairs={{0,1},{1,2},{2,3},{3,4},{4,5},{5,6},{6,7},{7,0}} | collective-permute-start | bytes 73736 | tf_op jit(solution)/shard_map/while/body/eval_jaxpr/ppermute | solution.py:48
  541.9 65.6 %collective-permute-start.2 = (f32[1024,6]{1,0:T(8,128)S(1)}, f32[1024,6]{1,0:T(8,128)S(1)}, u32[]{:S(2)}, u32[]{:S(2)}) collective-permute-start(f32[1024,6]{1,0:T(8,128)S(1)} %get-tuple-element.367), channel_id=1, source_target_pairs={{0,1},{1,2},{2,3},{3,4},{4,5},{5,6},{6,7},{7,0}} | collective-permute-start | bytes 73736 | tf_op jit(solution)/shard_map/while/body/eval_jaxpr/ppermute | solution.py:48
  542.8 220.9 %collective-permute-start.4 = (f32[1024,2560]{1,0:T(8,128)}, f32[1024,2560]{1,0:T(8,128)}, u32[]{:S(2)}, u32[]{:S(2)}) collective-permute-start(f32[1024,2560]{1,0:T(8,128)} %get-tuple-element.369), channel_id=1, source_target_pairs={{0,1},{1,2},{2,3},{3,4},{4,5},{5,6},{6,7},{7,0}} | collective-permute-start | bytes 31457288 | tf_op jit(solution)/shard_map/while/body/eval_jaxpr/ppermute | solution.py:48
  736.8 27.0 %copy-start.3 = (s32[1152]{0:T(1024)S(1)}, s32[1152]{0:T(1024)}, u32[]{:S(2)}) copy-start(s32[1152]{0:T(1024)} %copy-done.2) | copy-start | bytes 13828 | tf_op jit(solution)/shard_map/while
  805.6 116.1 %collective-permute-start = (bf16[1024,2560]{1,0:T(8,128)(2,1)}, bf16[1024,2560]{1,0:T(8,128)(2,1)}, u32[]{:S(2)}, u32[]{:S(2)}) collective-permute-start(bf16[1024,2560]{1,0:T(8,128)(2,1)} %get-tuple-element.365), channel_id=1, source_target_pairs={{0,1},{1,2},{2,3},{3,4},{4,5},{5,6},{6,7},{7,0}} | collective-permute-start | bytes 15728648 | tf_op jit(solution)/shard_map/while/body/eval_jaxpr/ppermute | solution.py:48
  805.6 60.4 %collective-permute-start.1 = (s32[1024,6]{0,1:T(8,128)S(1)}, s32[1024,6]{0,1:T(8,128)S(1)}, u32[]{:S(2)}, u32[]{:S(2)}) collective-permute-start(s32[1024,6]{0,1:T(8,128)S(1)} %get-tuple-element.366), channel_id=1, source_target_pairs={{0,1},{1,2},{2,3},{3,4},{4,5},{5,6},{6,7},{7,0}} | collective-permute-start | bytes 73736 | tf_op jit(solution)/shard_map/while/body/eval_jaxpr/ppermute | solution.py:48
  805.6 60.7 %collective-permute-start.3 = (s32[1024,6]{0,1:T(8,128)S(1)}, s32[1024,6]{0,1:T(8,128)S(1)}, u32[]{:S(2)}, u32[]{:S(2)}) collective-permute-start(s32[1024,6]{0,1:T(8,128)S(1)} %get-tuple-element.368), channel_id=1, source_target_pairs={{0,1},{1,2},{2,3},{3,4},{4,5},{5,6},{6,7},{7,0}} | collective-permute-start | bytes 73736 | tf_op jit(solution)/shard_map/while/body/eval_jaxpr/ppermute | solution.py:48
  805.7 66.3 %collective-permute-start.2 = (f32[1024,6]{1,0:T(8,128)S(1)}, f32[1024,6]{1,0:T(8,128)S(1)}, u32[]{:S(2)}, u32[]{:S(2)}) collective-permute-start(f32[1024,6]{1,0:T(8,128)S(1)} %get-tuple-element.367), channel_id=1, source_target_pairs={{0,1},{1,2},{2,3},{3,4},{4,5},{5,6},{6,7},{7,0}} | collective-permute-start | bytes 73736 | tf_op jit(solution)/shard_map/while/body/eval_jaxpr/ppermute | solution.py:48
  807.3 220.9 %collective-permute-start.4 = (f32[1024,2560]{1,0:T(8,128)}, f32[1024,2560]{1,0:T(8,128)}, u32[]{:S(2)}, u32[]{:S(2)}) collective-permute-start(f32[1024,2560]{1,0:T(8,128)} %get-tuple-element.369), channel_id=1, source_target_pairs={{0,1},{1,2},{2,3},{3,4},{4,5},{5,6},{6,7},{7,0}} | collective-permute-start | bytes 31457288 | tf_op jit(solution)/shard_map/while/body/eval_jaxpr/ppermute | solution.py:48
  1001.2 27.0 %copy-start.3 = (s32[1152]{0:T(1024)S(1)}, s32[1152]{0:T(1024)}, u32[]{:S(2)}) copy-start(s32[1152]{0:T(1024)} %copy-done.2) | copy-start | bytes 13828 | tf_op jit(solution)/shard_map/while
  1070.0 116.1 %collective-permute-start = (bf16[1024,2560]{1,0:T(8,128)(2,1)}, bf16[1024,2560]{1,0:T(8,128)(2,1)}, u32[]{:S(2)}, u32[]{:S(2)}) collective-permute-start(bf16[1024,2560]{1,0:T(8,128)(2,1)} %get-tuple-element.365), channel_id=1, source_target_pairs={{0,1},{1,2},{2,3},{3,4},{4,5},{5,6},{6,7},{7,0}} | collective-permute-start | bytes 15728648 | tf_op jit(solution)/shard_map/while/body/eval_jaxpr/ppermute | solution.py:48
  1070.1 60.4 %collective-permute-start.1 = (s32[1024,6]{0,1:T(8,128)S(1)}, s32[1024,6]{0,1:T(8,128)S(1)}, u32[]{:S(2)}, u32[]{:S(2)}) collective-permute-start(s32[1024,6]{0,1:T(8,128)S(1)} %get-tuple-element.366), channel_id=1, source_target_pairs={{0,1},{1,2},{2,3},{3,4},{4,5},{5,6},{6,7},{7,0}} | collective-permute-start | bytes 73736 | tf_op jit(solution)/shard_map/while/body/eval_jaxpr/ppermute | solution.py:48
  1070.1 60.7 %collective-permute-start.3 = (s32[1024,6]{0,1:T(8,128)S(1)}, s32[1024,6]{0,1:T(8,128)S(1)}, u32[]{:S(2)}, u32[]{:S(2)}) collective-permute-start(s32[1024,6]{0,1:T(8,128)S(1)} %get-tuple-element.368), channel_id=1, source_target_pairs={{0,1},{1,2},{2,3},{3,4},{4,5},{5,6},{6,7},{7,0}} | collective-permute-start | bytes 73736 | tf_op jit(solution)/shard_map/while/body/eval_jaxpr/ppermute | solution.py:48
  1070.1 66.3 %collective-permute-start.2 = (f32[1024,6]{1,0:T(8,128)S(1)}, f32[1024,6]{1,0:T(8,128)S(1)}, u32[]{:S(2)}, u32[]{:S(2)}) collective-permute-start(f32[1024,6]{1,0:T(8,128)S(1)} %get-tuple-element.367), channel_id=1, source_target_pairs={{0,1},{1,2},{2,3},{3,4},{4,5},{5,6},{6,7},{7,0}} | collective-permute-start | bytes 73736 | tf_op jit(solution)/shard_map/while/body/eval_jaxpr/ppermute | solution.py:48
  1071.7 220.9 %collective-permute-start.4 = (f32[1024,2560]{1,0:T(8,128)}, f32[1024,2560]{1,0:T(8,128)}, u32[]{:S(2)}, u32[]{:S(2)}) collective-permute-start(f32[1024,2560]{1,0:T(8,128)} %get-tuple-element.369), channel_id=1, source_target_pairs={{0,1},{1,2},{2,3},{3,4},{4,5},{5,6},{6,7},{7,0}} | collective-permute-start | bytes 31457288 | tf_op jit(solution)/shard_map/while/body/eval_jaxpr/ppermute | solution.py:48
  1265.6 27.0 %copy-start.3 = (s32[1152]{0:T(1024)S(1)}, s32[1152]{0:T(1024)}, u32[]{:S(2)}) copy-start(s32[1152]{0:T(1024)} %copy-done.2) | copy-start | bytes 13828 | tf_op jit(solution)/shard_map/while
  1334.5 116.1 %collective-permute-start = (bf16[1024,2560]{1,0:T(8,128)(2,1)}, bf16[1024,2560]{1,0:T(8,128)(2,1)}, u32[]{:S(2)}, u32[]{:S(2)}) collective-permute-start(bf16[1024,2560]{1,0:T(8,128)(2,1)} %get-tuple-element.365), channel_id=1, source_target_pairs={{0,1},{1,2},{2,3},{3,4},{4,5},{5,6},{6,7},{7,0}} | collective-permute-start | bytes 15728648 | tf_op jit(solution)/shard_map/while/body/eval_jaxpr/ppermute | solution.py:48
  1334.5 60.4 %collective-permute-start.1 = (s32[1024,6]{0,1:T(8,128)S(1)}, s32[1024,6]{0,1:T(8,128)S(1)}, u32[]{:S(2)}, u32[]{:S(2)}) collective-permute-start(s32[1024,6]{0,1:T(8,128)S(1)} %get-tuple-element.366), channel_id=1, source_target_pairs={{0,1},{1,2},{2,3},{3,4},{4,5},{5,6},{6,7},{7,0}} | collective-permute-start | bytes 73736 | tf_op jit(solution)/shard_map/while/body/eval_jaxpr/ppermute | solution.py:48
  1334.5 60.7 %collective-permute-start.3 = (s32[1024,6]{0,1:T(8,128)S(1)}, s32[1024,6]{0,1:T(8,128)S(1)}, u32[]{:S(2)}, u32[]{:S(2)}) collective-permute-start(s32[1024,6]{0,1:T(8,128)S(1)} %get-tuple-element.368), channel_id=1, source_target_pairs={{0,1},{1,2},{2,3},{3,4},{4,5},{5,6},{6,7},{7,0}} | collective-permute-start | bytes 73736 | tf_op jit(solution)/shard_map/while/body/eval_jaxpr/ppermute | solution.py:48
  1334.6 66.3 %collective-permute-start.2 = (f32[1024,6]{1,0:T(8,128)S(1)}, f32[1024,6]{1,0:T(8,128)S(1)}, u32[]{:S(2)}, u32[]{:S(2)}) collective-permute-start(f32[1024,6]{1,0:T(8,128)S(1)} %get-tuple-element.367), channel_id=1, source_target_pairs={{0,1},{1,2},{2,3},{3,4},{4,5},{5,6},{6,7},{7,0}} | collective-permute-start | bytes 73736 | tf_op jit(solution)/shard_map/while/body/eval_jaxpr/ppermute | solution.py:48
  1336.2 220.9 %collective-permute-start.4 = (f32[1024,2560]{1,0:T(8,128)}, f32[1024,2560]{1,0:T(8,128)}, u32[]{:S(2)}, u32[]{:S(2)}) collective-permute-start(f32[1024,2560]{1,0:T(8,128)} %get-tuple-element.369), channel_id=1, source_target_pairs={{0,1},{1,2},{2,3},{3,4},{4,5},{5,6},{6,7},{7,0}} | collective-permute-start | bytes 31457288 | tf_op jit(solution)/shard_map/while/body/eval_jaxpr/ppermute | solution.py:48
  1598.9 116.1 %collective-permute-start = (bf16[1024,2560]{1,0:T(8,128)(2,1)}, bf16[1024,2560]{1,0:T(8,128)(2,1)}, u32[]{:S(2)}, u32[]{:S(2)}) collective-permute-start(bf16[1024,2560]{1,0:T(8,128)(2,1)} %get-tuple-element.365), channel_id=1, source_target_pairs={{0,1},{1,2},{2,3},{3,4},{4,5},{5,6},{6,7},{7,0}} | collective-permute-start | bytes 15728648 | tf_op jit(solution)/shard_map/while/body/eval_jaxpr/ppermute | solution.py:48
  1598.9 60.4 %collective-permute-start.1 = (s32[1024,6]{0,1:T(8,128)S(1)}, s32[1024,6]{0,1:T(8,128)S(1)}, u32[]{:S(2)}, u32[]{:S(2)}) collective-permute-start(s32[1024,6]{0,1:T(8,128)S(1)} %get-tuple-element.366), channel_id=1, source_target_pairs={{0,1},{1,2},{2,3},{3,4},{4,5},{5,6},{6,7},{7,0}} | collective-permute-start | bytes 73736 | tf_op jit(solution)/shard_map/while/body/eval_jaxpr/ppermute | solution.py:48
  1599.0 60.7 %collective-permute-start.3 = (s32[1024,6]{0,1:T(8,128)S(1)}, s32[1024,6]{0,1:T(8,128)S(1)}, u32[]{:S(2)}, u32[]{:S(2)}) collective-permute-start(s32[1024,6]{0,1:T(8,128)S(1)} %get-tuple-element.368), channel_id=1, source_target_pairs={{0,1},{1,2},{2,3},{3,4},{4,5},{5,6},{6,7},{7,0}} | collective-permute-start | bytes 73736 | tf_op jit(solution)/shard_map/while/body/eval_jaxpr/ppermute | solution.py:48
  1599.0 66.3 %collective-permute-start.2 = (f32[1024,6]{1,0:T(8,128)S(1)}, f32[1024,6]{1,0:T(8,128)S(1)}, u32[]{:S(2)}, u32[]{:S(2)}) collective-permute-start(f32[1024,6]{1,0:T(8,128)S(1)} %get-tuple-element.367), channel_id=1, source_target_pairs={{0,1},{1,2},{2,3},{3,4},{4,5},{5,6},{6,7},{7,0}} | collective-permute-start | bytes 73736 | tf_op jit(solution)/shard_map/while/body/eval_jaxpr/ppermute | solution.py:48
  1600.6 220.9 %collective-permute-start.4 = (f32[1024,2560]{1,0:T(8,128)}, f32[1024,2560]{1,0:T(8,128)}, u32[]{:S(2)}, u32[]{:S(2)}) collective-permute-start(f32[1024,2560]{1,0:T(8,128)} %get-tuple-element.369), channel_id=1, source_target_pairs={{0,1},{1,2},{2,3},{3,4},{4,5},{5,6},{6,7},{7,0}} | collective-permute-start | bytes 31457288 | tf_op jit(solution)/shard_map/while/body/eval_jaxpr/ppermute | solution.py:48
  1863.8 116.3 %collective-permute-start.9 = (f32[1024,2560]{1,0:T(8,128)}, f32[1024,2560]{1,0:T(8,128)}, u32[]{:S(2)}, u32[]{:S(2)}) collective-permute-start(f32[1024,2560]{1,0:T(8,128)} %get-tuple-element.255), channel_id=1, source_target_pairs={{0,1},{1,2},{2,3},{3,4},{4,5},{5,6},{6,7},{7,0}} | collective-permute-start | bytes 31457288 | tf_op jit(solution)/shard_map/ppermute | solution.py:52
  1915.3 64.7 %copy-start.9 = (s32[1152]{0:T(1024)S(1)}, s32[1152]{0:T(1024)}, u32[]{:S(2)}) copy-start(s32[1152]{0:T(1024)} %copy-done.8) | copy-start | bytes 13828
  (35 other events, 302.5 us)
where the time goes:
time: 2030 us; the launch traced here: 2020 us
  matrix products  641 us (32%)
  local copies, waits for them, and re-layouts  611 us (30%)
  waiting for transfers between devices  420 us (21%)
  other arithmetic  315 us (16%)
    ppermute x30, waiting for transfers between devices, pass_on(): visitor, accum = lax.ppermute((visitor, accum), 'ep', next_perm)  382 us
    scatter-add x8, other arithmetic, local_share(): jnp.zeros((tok_dev, token_blk.shape[1]), jnp.float32).at[slot_token]  262 us
    dot_general x8, matrix products, local_share(): jnp.einsum('ecf,efd->ecd', hidden, w_down, preferred_element_type=jnp.flo...  216 us
    dot_general x8, matrix products, local_share(): jnp.einsum('ecd,edf->ecf', dispatched, w_gate, preferred_element_type=jnp...  214 us
    dot_general x8, matrix products, local_share(): jnp.einsum('ecd,edf->ecf', dispatched, w_up, preferred_element_type=jnp.f...  210 us
    scatter x8, local copies, waits for them, and re-layouts, local_share(): jnp.full((num_local * shard_cap,), tok_dev, jnp.int32).at[flat_slot]  184 us
    scatter x8, local copies, waits for them, and re-layouts, local_share(): jnp.zeros((num_local * shard_cap,), jnp.float32).at[flat_slot]  184 us
    gather x8, local copies, waits for them, and re-layouts, local_share(): jnp.take(token_blk, slot_token, axis=0, mode='fill', fill_value=0)  126 us
  transfers between devices with their start and end apart: 35, of which 19 were waited for; matrix products, arithmetic and copies ran while one was open for 56% of the time, Pallas kernels for 0%

commit v1 on v0

v1 whole, which is shorter than its diff:
```python
import functools
import jax
import jax.numpy as jnp
from jax import lax
from jax.experimental import pallas as pl
from jax.experimental.pallas import tpu as pltpu
from jax.sharding import PartitionSpec as P

NUM_CHUNKS = 4
MAX_ROWS = 384
ROW_STEP = 128
FF_BLOCK = 512
OUT_BLOCK = 512
ID_RADIX = 64


def expert_kernel(meta, gate, pos, digits, tok_hbm, wg_hbm, wu_hbm, wd_hbm, out_hbm,
                  tok, acc, wg, wu, wd, onehot, x, h, o, idx_v, idx_s, w_sem, tok_sem, idx_sem, out_sem):
    num_tok, d_model = tok.shape
    ff_dim = wg_hbm.shape[2]
    ff_steps = ff_dim // FF_BLOCK
    max_items = meta.shape[0] // 4
    num_items = meta[3 * max_items]

    def weight_copies(step, slot):
        e = meta[step // ff_steps]
        cols = pl.ds(pl.multiple_of((step % ff_steps) * FF_BLOCK, FF_BLOCK), FF_BLOCK)
        return (pltpu.make_async_copy(wg_hbm.at[e, :, cols], wg.at[slot], w_sem.at[slot, 0]),
                pltpu.make_async_copy(wu_hbm.at[e, :, cols], wu.at[slot], w_sem.at[slot, 1]),
                pltpu.make_async_copy(wd_hbm.at[e, cols, :], wd.at[slot], w_sem.at[slot, 2]))

    tok_copy = pltpu.make_async_copy(tok_hbm, tok, tok_sem)
    tok_copy.start()

    @pl.when(num_items > 0)
    def _():
        for cp in weight_copies(0, 0):
            cp.start()

    def zero(i, c):
        acc[pl.ds(pl.multiple_of(i * 8, 8), 8), :] = jnp.zeros((8, d_model), jnp.float32)
        return c

    lax.fori_loop(0, acc.shape[0] // 8, zero, 0)
    tok_copy.wait()

    def process(m, item, e, p0, rows):
        want = lax.broadcasted_iota(jnp.int32, (m, num_tok), 0) + p0
        onehot[:m, :] = jnp.where(want == pos[e], 1.0, 0.0).astype(jnp.bfloat16)
        parts = lax.dot_general(digits[...], onehot[:m, :], (((1,), (1,)), ((), ())), preferred_element_type=jnp.float32)
        idx = parts[0:1] * ID_RADIX + parts[1:2] + (1.0 - parts[2:3]) * num_tok
        idx_v[:, :m] = jnp.broadcast_to(idx.astype(jnp.int32), (8, m))
        idx_copy = pltpu.make_async_copy(idx_v, idx_s, idx_sem)
        idx_copy.start()

        def dispatch(nb, c):
            cols = pl.ds(pl.multiple_of(nb * OUT_BLOCK, OUT_BLOCK), OUT_BLOCK)
            x[:m, cols] = jnp.dot(onehot[:m, :], tok[:, cols], preferred_element_type=jnp.float32).astype(jnp.bfloat16)
            return c

        lax.fori_loop(0, d_model // OUT_BLOCK, dispatch, 0)

        def ff_step(f, c):
            step = item * ff_steps + f
            slot = step % 2

            @pl.when(step + 1 < num_items * ff_steps)
            def _():
                for cp in weight_copies(step + 1, 1 - slot):
                    cp.start()

            for cp in weight_copies(step, slot):
                cp.wait()

            def up(j, c):
                cols = pl.ds(pl.multiple_of(j * 256, 256), 256)
                a = jnp.dot(x[:m, :], wg[slot, :, cols], preferred_element_type=jnp.float32)
                u = jnp.dot(x[:m, :], wu[slot, :, cols], preferred_element_type=jnp.float32)
                h[:m, cols] = (jax.nn.silu(a) * u).astype(jnp.bfloat16)
                return c

            lax.fori_loop(0, FF_BLOCK // 256, up, 0)

            def down(nb, c):
                cols = pl.ds(pl.multiple_of(nb * OUT_BLOCK, OUT_BLOCK), OUT_BLOCK)
                part = jnp.dot(h[:m, :], wd[slot, :, cols], preferred_element_type=jnp.float32)

                @pl.when(f == 0)
                def _():
                    o[:m, cols] = part

                @pl.when(f != 0)
                def _():
                    o[:m, cols] += part

                return c

            lax.fori_loop(0, d_model // OUT_BLOCK, down, 0)
            return c

        lax.fori_loop(0, ff_steps, ff_step, 0)
        idx_copy.wait()

    def scatter(e, rows):
        width = 640

        def eight(i, c):
            base = pl.multiple_of(i * 8, 8)
            for half in range(2):
                t = [idx_s[0, base + half * 4 + k] for k in range(4)]
                g = [gate[e * num_tok + t[k]] for k in range(4)]
                for cb in range(d_model // width):
                    cols = slice(cb * width, (cb + 1) * width)
                    new = [acc[pl.ds(t[k], 1), cols] + o[pl.ds(base + half * 4 + k, 1), cols] * g[k] for k in range(4)]
                    for k in range(4):
                        acc[pl.ds(t[k], 1), cols] = new[k]
            return c

        lax.fori_loop(0, (rows + 7) // 8, eight, 0)

    def item_body(item, c):
        e, p0, rows = meta[item], meta[max_items + item], meta[2 * max_items + item]
        for m in range(ROW_STEP, MAX_ROWS + 1, ROW_STEP):
            @pl.when((rows > m - ROW_STEP) & (rows <= m))
            def _():
                process(m, item, e, p0, rows)

        scatter(e, rows)
        return c

    lax.fori_loop(0, num_items, item_body, 0)
    out_copy = pltpu.make_async_copy(acc.at[pl.ds(0, num_tok), :], out_hbm, out_sem)
    out_copy.start()
    out_copy.wait()


def expert_block(meta, gate, pos, digits, tok, w_gate, w_up, w_down):
    num_tok, d_model = tok.shape
    num_local, _, ff_dim = w_gate.shape
    smem = pl.BlockSpec(memory_space=pltpu.SMEM)
    vmem = pl.BlockSpec(memory_space=pltpu.VMEM)
    anym = pl.BlockSpec(memory_space=pl.ANY)
    rows = num_tok * 3 // 4
    return pl.pallas_call(
        expert_kernel,
        out_shape=jax.ShapeDtypeStruct((num_tok, d_model), jnp.float32),
        in_specs=[smem, smem, vmem, vmem, anym, anym, anym, anym],
        out_specs=anym,
        scratch_shapes=[
            pltpu.VMEM((num_tok, d_model), jnp.bfloat16),
            pltpu.VMEM((num_tok + 8, d_model), jnp.float32),
            pltpu.VMEM((2, d_model, FF_BLOCK), jnp.bfloat16),
            pltpu.VMEM((2, d_model, FF_BLOCK), jnp.bfloat16),
            pltpu.VMEM((2, FF_BLOCK, d_model), jnp.bfloat16),
            pltpu.VMEM((MAX_ROWS, num_tok), jnp.bfloat16),
            pltpu.VMEM((MAX_ROWS, d_model), jnp.bfloat16),
            pltpu.VMEM((MAX_ROWS, FF_BLOCK), jnp.bfloat16),
            pltpu.VMEM((MAX_ROWS, d_model), jnp.float32),
            pltpu.VMEM((8, MAX_ROWS), jnp.int32),
            pltpu.SMEM((8, MAX_ROWS), jnp.int32),
            pltpu.SemaphoreType.DMA((2, 3)),
            pltpu.SemaphoreType.DMA,
            pltpu.SemaphoreType.DMA,
            pltpu.SemaphoreType.DMA,
        ],
        compiler_params=pltpu.CompilerParams(vmem_limit_bytes=66_000_000),
        cost_estimate=pl.CostEstimate(flops=rows * 6 * d_model * ff_dim * 2, transcendentals=rows * ff_dim,
                                      bytes_accessed=num_local * 6 * d_model * ff_dim + num_tok * d_model * 6),
        name='expert_block',
    )(meta, gate, pos, digits, tok, w_gate, w_up, w_down)


def routing_tables(expert_ids, gate_wts, slot_ids, my_rank, num_local, group_size):
    tok_dev, top_k = expert_ids.shape
    tc = tok_dev // NUM_CHUNKS
    num_tok = group_size * tc
    key = jnp.where(slot_ids >= 0, expert_ids, -1).astype(jnp.float32).T
    packed = lax.all_gather(jnp.concatenate([key, gate_wts.T], axis=0), 'ep')
    packed = packed.reshape(group_size, 2, top_k, NUM_CHUNKS, tc).transpose(1, 3, 2, 0, 4)
    keys, gates = packed[0][:, None], packed[1][:, None]
    local = (my_rank * num_local + jnp.arange(num_local)).astype(jnp.float32)[None, :, None, None, None]
    hit = keys == local
    mask = jnp.any(hit, axis=2).reshape(NUM_CHUNKS, num_local, num_tok)
    gate = jnp.sum(jnp.where(hit, gates, 0.0), axis=2).reshape(NUM_CHUNKS, num_local * num_tok)
    gate = jnp.pad(gate, ((0, 0), (0, 128)))

    blocks = mask.astype(jnp.bfloat16).reshape(NUM_CHUNKS, num_local, num_tok // 128, 128)
    before = (jnp.arange(128)[:, None] < jnp.arange(128)[None, :]).astype(jnp.bfloat16)
    inner = jnp.einsum('cebk,kl->cebl', blocks, before, preferred_element_type=jnp.float32)
    sums = jnp.sum(blocks.astype(jnp.float32), axis=3)
    nb = num_tok // 128
    outer = jnp.sum(jnp.where(jnp.arange(nb)[:, None] < jnp.arange(nb)[None, :], sums[..., None], 0.0), axis=2)
    order = (inner + outer[..., None]).reshape(NUM_CHUNKS, num_local, num_tok)
    pos = jnp.where(mask, order, -1.0).astype(jnp.int32)

    count = jnp.sum(sums, axis=2).astype(jnp.int32)
    passes = (count + MAX_ROWS - 1) // MAX_ROWS
    upto = jnp.arange(num_local)[:, None] <= jnp.arange(num_local)[None, :]
    ends = jnp.sum(jnp.where(upto, passes[:, :, None], 0), axis=1)
    starts = ends - passes
    max_items = 32
    item = jnp.arange(max_items)
    mine = (starts[:, :, None] <= item) & (item < ends[:, :, None])
    e = jnp.sum(jnp.where(mine, jnp.arange(num_local)[:, None], 0), axis=1)
    p0 = jnp.sum(jnp.where(mine, (item - starts[:, :, None]) * MAX_ROWS, 0), axis=1)
    rows = jnp.minimum(jnp.sum(jnp.where(mine, count[:, :, None], 0), axis=1) - p0, MAX_ROWS)
    total = jnp.broadcast_to(ends[:, -1:], (NUM_CHUNKS, max_items))
    meta = jnp.concatenate([e, p0, rows, total], axis=1).astype(jnp.int32)
    return meta, gate, pos.reshape(NUM_CHUNKS, num_local, 1, num_tok)


def solution(mesh):
    group_size = mesh.shape['ep']
    row_spec = P(('dp', 'ep'), None)
    expert_spec = P('ep', None, None)

    def per_device(tokens, expert_ids, gate_wts, slot_ids, w_gate, w_up, w_down):
        my_rank = lax.axis_index('ep')
        tc = tokens.shape[0] // NUM_CHUNKS
        num_tok = group_size * tc
        gathered = [lax.all_gather(tokens[c * tc:(c + 1) * tc], 'ep', axis=0, tiled=True) for c in range(NUM_CHUNKS)]
        meta, gate, pos = routing_tables(expert_ids, gate_wts, slot_ids, my_rank, w_gate.shape[0], group_size)
        ids = jnp.arange(num_tok)
        digits = jnp.stack([ids // ID_RADIX, ids % ID_RADIX, jnp.ones_like(ids)] + [jnp.zeros_like(ids)] * 5).astype(jnp.bfloat16)
        outs = []
        for c in range(NUM_CHUNKS):
            part = expert_block(meta[c], gate[c], pos[c], digits, gathered[c], w_gate, w_up, w_down)
            outs.append(lax.psum_scatter(part, 'ep', scatter_dimension=0, tiled=True).astype(jnp.bfloat16))
        return jnp.concatenate(outs, axis=0)

    return jax.shard_map(per_device, mesh=mesh, in_specs=(row_spec, row_spec, row_spec, row_spec, expert_spec, expert_spec, expert_spec), out_specs=row_spec, check_vma=False)
```

time: 2030 us -> 810 us (0.40)
  matrix products: 641 us -> 0.18 us
  local copies, waits for them, and re-layouts: 611 us -> 9.51 us
  Pallas kernels: 0 us -> 569 us
  other arithmetic: 315 us -> 13.7 us
  waiting for transfers between devices: 420 us -> 190 us
    dot_general x24 -> x1, matrix products: 641 us -> 0.18 us  [routing_tables(): jnp.einsum('cebk,kl->cebl', blocks, before, preferred_element_type=jnp.fl...]
    pallas_call x0 -> x4, Pallas kernels: none -> 569 us  [expert_block(): pl.pallas_call(expert_kernel, out_shape=jax.ShapeDtypeStruct((num_tok, d_...]
    ppermute x35 -> x0, waiting for transfers between devices: 420 us -> none  [the longest x30 382 us: pass_on(): visitor, accum = lax.ppermute((visitor, accum), 'ep', next_perm)]
    scatter x16 -> x0, local copies, waits for them, and re-layouts: 368 us -> none  [the longest x8 184 us: local_share(): jnp.full((num_local * shard_cap,), tok_dev, jnp.int32).at[flat_slot]]
    scatter-add x8 -> x0, other arithmetic: 262 us -> none  [local_share(): jnp.zeros((tok_dev, token_blk.shape[1]), jnp.float32).at[slot_token]]
    reduce_scatter x0 -> x4, waiting for transfers between devices: none -> 151 us  [per_device(): lax.psum_scatter(part, 'ep', scatter_dimension=0, tiled=True)]
    gather x8 -> x0, local copies, waits for them, and re-layouts: 126 us -> none  [local_share(): jnp.take(token_blk, slot_token, axis=0, mode='fill', fill_value=0)]
    while x102 -> x0, local copies, waits for them, and re-layouts: 98.5 us -> none
  transfers between devices with their start and end apart: 35 -> 8, of which waited for: 19 -> 2; matrix products, arithmetic and copies ran while one was open for 56% -> 2% of each run, Pallas kernels for 0% -> 70%
where the time goes in v1:
time: 810 us; the launch traced here: 814 us
  Pallas kernels  569 us (70%)
  waiting for transfers between devices  190 us (23%)
  blocking collectives  18 us (2%)
  between operations  13.8 us (2%)
  other arithmetic  13.7 us (2%)
  local copies, waits for them, and re-layouts  9.51 us (1%)
    pallas_call x4, Pallas kernels, expert_block(): pl.pallas_call(expert_kernel, out_shape=jax.ShapeDtypeStruct((num_tok, d_...  569 us
    reduce_scatter x4, waiting for transfers between devices, per_device(): lax.psum_scatter(part, 'ep', scatter_dimension=0, tiled=True)  151 us
    all_gather x4, waiting for transfers between devices, per_device(): lax.all_gather(tokens[c * tc:(c + 1) * tc], 'ep', axis=0, tiled=True)  36.3 us
    all_gather x1, blocking collectives, routing_tables(): packed = lax.all_gather(jnp.concatenate([key, gate_wts.T], axis=0), 'ep')  18 us
  transfers between devices with their start and end apart: 8, of which 2 were waited for; matrix products, arithmetic and copies ran while one was open for 2% of the time, Pallas kernels for 70%

profile of v1, /device:TPU:0, one launch (start us, length us, event | category | flops | bytes accessed | tf_op | source)
XLA Modules:
  0.0 814.0 jit_solution(3737755832572009886)
XLA Ops:
  6.5 5.0 fusion.12
  11.5 0.0 all-gather.9.cloned.1.call-start
  11.6 0.7 all-gather.9.cloned.1.call-update
  12.3 0.0 all-gather.11.cloned.1.call-start
  12.3 0.7 all-gather.11.cloned.1.call-update
  13.0 0.0 all-gather.13.cloned.1.call-start
  13.1 0.5 all-gather.13.cloned.1.call-update
  13.6 0.0 reduce-scatter.5.cloned.1.call-start
  13.7 18.0 %all-gather.1 = f32[8,12,1024]{2,1,0:T(8,128)S(1)} all-gather(f32[1,12,1024]{2,1,0:T(8,128)S(1)} %maximum_bitcast_fusion), channel_id=2, replica_groups=mesh['dp'=1,'ep'=8] {'ep'}, dimensions={0}, use_global_device_ids=true | all-gather | bytes 442368 | tf_op jit(solution)/shard_map/all_gather | solution.py:178
  31.8 0.2 reshape.116
  32.1 0.3 compare_reduce_fusion
  32.4 0.1 reshape.108
  32.5 0.1 reshape.117
  32.6 0.1 convert_reduce_fusion.1
  32.7 0.1 convert_reduce_fusion
  32.9 0.1 select_reduce_fusion
  33.1 0.2 convolution_add_fusion
  33.3 0.2 fusion
  33.6 0.2 copy.48
  33.8 0.7 stack.10.digits
  34.5 1.3 fusion.2
  35.8 0.1 select_reduce_fusion.4
  35.9 0.2 slice_reduce_fusion
  36.1 0.1 select_reduce_fusion.3
  36.2 0.1 broadcast_in_dim.111
  36.3 0.1 pad_add_fusion
  36.4 0.6 slice_bitcast_fusion.9
  37.0 0.3 fusion.1
  37.2 0.9 slice_bitcast_fusion.5
  38.1 36.2 %all-gather.7.cloned.1.call-done.tok_hbm = bf16[2048,2560]{1,0:T(8,128)(2,1)} async-done(((bf16[256,2560]{1,0:T(8,128)(2,1)}), bf16[2048,2560]{1,0:T(8,128)(2,1)}) %all-gather.7.cloned.1.call-update) | async-done | bytes 10485776 | tf_op jit(solution)/shard_map/all_gather | solution.py:221
  74.3 132.8 %expert_block.4 = f32[2048,2560]{1,0:T(8,128)} custom-call(s32[128]{0:T(128)} %get-tuple-element.22.meta, f32[16512]{0:T(1024)} %get-tuple-element.5.gate, s32[8,1,2048]{2,1,0:T(1,128)} %get-tuple-element.18.pos, bf16[8,2048]{1,0:T(8,128)(2,1)} %stack.10.digits, bf16[2048,2560]{1,0:T(8,128)(2,1)} %all-gather.7.cloned.1.call-done.tok_hbm, ...), custom_call_target="tpu_custom_call" | custom-call | flops 72477573120 | bytes 220200960 | tf_op jit(solution)/shard_map/expert_block/pallas_call | solution.py:144
  207.2 0.0 reduce-scatter.7.cloned.1.call-start
  207.3 0.0 all-gather.9.cloned.1.call-done.tok_hbm
  207.3 133.3 %expert_block.5 = f32[2048,2560]{1,0:T(8,128)} custom-call(s32[128]{0:T(128)} %get-tuple-element.25.meta, f32[16512]{0:T(1024)} %get-tuple-element.6.gate, s32[8,1,2048]{2,1,0:T(1,128)} %get-tuple-element.21.pos, bf16[8,2048]{1,0:T(8,128)(2,1)} %stack.10.digits, bf16[2048,2560]{1,0:T(8,128)(2,1)} %all-gather.9.cloned.1.call-done.tok_hbm, ...), custom_call_target="tpu_custom_call" | custom-call | flops 72477573120 | bytes 220200960 | tf_op jit(solution)/shard_map/expert_block/pallas_call | solution.py:144
  340.6 0.0 reduce-scatter.9.cloned.1.call-start
  340.7 148.9 %expert_block.6 = f32[2048,2560]{1,0:T(8,128)} custom-call(s32[128]{0:T(128)} %get-tuple-element.24.meta, f32[16512]{0:T(1024)} %get-tuple-element.7.gate, s32[8,1,2048]{2,1,0:T(1,128)} %get-tuple-element.20.pos, bf16[8,2048]{1,0:T(8,128)(2,1)} %stack.10.digits, bf16[2048,2560]{1,0:T(8,128)(2,1)} %all-gather.11.cloned.1.call-done.tok_hbm, ...), custom_call_target="tpu_custom_call" | custom-call | flops 72477573120 | bytes 220200960 | tf_op jit(solution)/shard_map/expert_block/pallas_call | solution.py:144
  489.7 0.0 reduce-scatter.11.cloned.1.call-start
  489.8 153.7 %expert_block.7 = f32[2048,2560]{1,0:T(8,128)} custom-call(s32[128]{0:T(128)} %get-tuple-element.23.meta, f32[16512]{0:T(1024)} %get-tuple-element.8.gate, s32[8,1,2048]{2,1,0:T(1,128)} %get-tuple-element.19.pos, bf16[8,2048]{1,0:T(8,128)(2,1)} %stack.10.digits, bf16[2048,2560]{1,0:T(8,128)(2,1)} %all-gather.13.cloned.1.call-done.tok_hbm, ...), custom_call_target="tpu_custom_call" | custom-call | flops 72477573120 | bytes 220200960 | tf_op jit(solution)/shard_map/expert_block/pallas_call | solution.py:144
  643.5 0.0 reduce-scatter.5.cloned.1.call-done
  643.6 1.9 convert_element_type.63
  645.4 0.0 reduce-scatter.7.cloned.1.call-done
  645.5 1.9 convert_element_type.64
  647.3 0.0 reduce-scatter.9.cloned.1.call-done
  647.4 2.9 convert_element_type.65
  650.3 151.4 %reduce-scatter.11.cloned.1.call-done = f32[256,2560]{1,0:T(8,128)} async-done(((f32[2048,2560]{1,0:T(8,128)}), f32[256,2560]{1,0:T(8,128)}) %reduce-scatter.11.cloned.1.call-update) | async-done | bytes 2621456 | tf_op jit(solution)/shard_map/reduce_scatter | solution.py:228
  801.7 2.0 convert_element_type.66
  803.7 0.1 copy-done
  803.8 3.4 pad_maximum_fusion
  (33 shorter events, 0.4 us)
Async XLA Ops:
  6.5 67.8 %all-gather.7.cloned.1.call-start = ((), (), s32[]{:S(2)}) async-start(), calls=%async_computation.4 | async-start | bytes 11796480 | tf_op jit(solution)/shard_map/all_gather | solution.py:221
  11.5 2.1 copy-start.1
  11.5 2.2 copy-start.2
  11.5 2.2 copy-start.3
  11.5 195.7 %all-gather.9.cloned.1.call-start = ((), (), s32[]{:S(2)}) async-start(), calls=%async_computation.6 | async-start | bytes 11796480 | tf_op jit(solution)/shard_map/all_gather | solution.py:221
  12.3 328.4 %all-gather.11.cloned.1.call-start = ((), (), s32[]{:S(2)}) async-start(), calls=%async_computation.8 | async-start | bytes 11796480 | tf_op jit(solution)/shard_map/all_gather | solution.py:221
  13.0 476.7 %all-gather.13.cloned.1.call-start = ((), (), s32[]{:S(2)}) async-start(), calls=%async_computation.10 | async-start | bytes 11796480 | tf_op jit(solution)/shard_map/all_gather | solution.py:221
  13.6 630.0 %reduce-scatter.5.cloned.1.call-start = ((), (), s32[]{:S(2)}) async-start(), calls=%async_computation.5 | async-start | bytes 23592960 | tf_op jit(solution)/shard_map/reduce_scatter | solution.py:228
  207.2 438.2 %reduce-scatter.7.cloned.1.call-start = ((), (), s32[]{:S(2)}) async-start(), calls=%async_computation.7 | async-start | bytes 23592960 | tf_op jit(solution)/shard_map/reduce_scatter | solution.py:228
  340.6 306.7 %reduce-scatter.9.cloned.1.call-start = ((), (), s32[]{:S(2)}) async-start(), calls=%async_computation.9 | async-start | bytes 23592960 | tf_op jit(solution)/shard_map/reduce_scatter | solution.py:228
  489.7 312.0 %reduce-scatter.11.cloned.1.call-start = ((), (), s32[]{:S(2)}) async-start(), calls=%async_computation.11 | async-start | bytes 23592960 | tf_op jit(solution)/shard_map/reduce_scatter | solution.py:228
  801.7 2.1 copy-start
Sparse Core Ops, SparseCore 0:
  11.6 62.6 all-gather.6
  76.1 57.5 all-gather.8
  135.5 57.5 all-gather.10
  194.8 57.5 all-gather.12
  255.8 126.9 reduce-scatter.4
  386.2 126.8 reduce-scatter.6
  516.6 127.7 reduce-scatter.8
  648.0 153.6 reduce-scatter.10

commit v2 on v1

v2 whole, which is shorter than its diff:
```python
import jax
import jax.numpy as jnp
from jax import lax
from jax.experimental import pallas as pl
from jax.experimental.pallas import tpu as pltpu
from jax.sharding import PartitionSpec as P

UNIT = 128
CHUNK_UNITS = (1, 2, 2, 2, 1)
GATHERS = ((0,), (1,), (2, 3, 4))
ROW_SIZES = {1: (128, 160, 384), 2: (128, 256, 288, 384)}
MAX_ROWS = 384
MAX_ITEMS = 32
FF_BLOCK = 256
OUT_BLOCK = 512
ID_RADIX = 64
PIECES = 8


def expert_kernel(row0, row_sizes, meta, gate, pos, digits, tok_hbm, wg_hbm, wu_hbm, wd_hbm, keep_hbm, send_hbm,
                  tok, acc, wg, wu, wd, onehot, x, h, o, idx_v, idx_s, up_sem, down_sem, tok_sem, idx_sem, out_sem):
    num_tok, d_model = tok.shape
    shards = tok_hbm.shape[0]
    tc = num_tok // shards
    ff_dim = wg_hbm.shape[2]
    up_steps, down_steps = ff_dim // FF_BLOCK, d_model // OUT_BLOCK
    num_items = meta[3 * MAX_ITEMS]
    parity = meta[3 * MAX_ITEMS + 1]

    def up_copies(item, j):
        cols = pl.ds(pl.multiple_of(j * FF_BLOCK, FF_BLOCK), FF_BLOCK)
        e = meta[item]
        return (pltpu.make_async_copy(wg_hbm.at[e, :, cols], wg.at[j], up_sem.at[j, 0]),
                pltpu.make_async_copy(wu_hbm.at[e, :, cols], wu.at[j], up_sem.at[j, 1]))

    def down_copy(item, j):
        cols = pl.ds(pl.multiple_of(j * OUT_BLOCK, OUT_BLOCK), OUT_BLOCK)
        return pltpu.make_async_copy(wd_hbm.at[meta[item], :, cols], wd.at[j], down_sem.at[j])

    tok_copies = [pltpu.make_async_copy(tok_hbm.at[s, pl.ds(row0, tc), :], tok.at[pl.ds(s * tc, tc), :], tok_sem.at[s])
                  for s in range(shards)]
    for cp in tok_copies:
        cp.start()

    @pl.when(num_items > 0)
    def _():
        for j in range(up_steps):
            for cp in up_copies(0, j):
                cp.start()
        for j in range(down_steps):
            down_copy(0, j).start()

    def zero(i, c):
        acc[pl.ds(pl.multiple_of(i * 8, 8), 8), :] = jnp.zeros((8, d_model), jnp.float32)
        return c

    lax.fori_loop(0, acc.shape[0] // 8, zero, 0)
    for cp in tok_copies:
        cp.wait()

    def process(m, item, e, p0):
        want = lax.broadcasted_iota(jnp.int32, (m, num_tok), 0) + p0
        onehot[:m, :] = jnp.where(want == pos[e], 1.0, 0.0).astype(jnp.bfloat16)
        parts = lax.dot_general(digits[...], onehot[:m, :], (((1,), (1,)), ((), ())), preferred_element_type=jnp.float32)
        idx = parts[0:1] * ID_RADIX + parts[1:2] + (1.0 - parts[2:3]) * num_tok
        idx_v[:, :m] = jnp.broadcast_to(idx.astype(jnp.int32), (8, m))
        idx_copy = pltpu.make_async_copy(idx_v, idx_s, idx_sem)
        idx_copy.start()

        def dispatch(nb, c):
            cols = pl.ds(pl.multiple_of(nb * OUT_BLOCK, OUT_BLOCK), OUT_BLOCK)
            x[:m, cols] = jnp.dot(onehot[:m, :], tok[:, cols], preferred_element_type=jnp.float32).astype(jnp.bfloat16)
            return c

        lax.fori_loop(0, d_model // OUT_BLOCK, dispatch, 0)

        def up(j, c):
            for cp in up_copies(item, j):
                cp.wait()
            a = jnp.dot(x[:m, :], wg[j], preferred_element_type=jnp.float32)
            u = jnp.dot(x[:m, :], wu[j], preferred_element_type=jnp.float32)
            h[:m, pl.ds(pl.multiple_of(j * FF_BLOCK, FF_BLOCK), FF_BLOCK)] = (jax.nn.silu(a) * u).astype(jnp.bfloat16)

            @pl.when(item + 1 < num_items)
            def _():
                for cp in up_copies(item + 1, j):
                    cp.start()

            return c

        lax.fori_loop(0, up_steps, up, 0)

        def down(j, c):
            down_copy(item, j).wait()
            cols = pl.ds(pl.multiple_of(j * OUT_BLOCK, OUT_BLOCK), OUT_BLOCK)
            o[:m, cols] = jnp.dot(h[:m, :], wd[j], preferred_element_type=jnp.float32)

            @pl.when(item + 1 < num_items)
            def _():
                down_copy(item + 1, j).start()

            return c

        lax.fori_loop(0, down_steps, down, 0)
        idx_copy.wait()

    def scatter(e, rows):
        width = 640

        def eight(i, c):
            base = pl.multiple_of(i * 8, 8)
            for half in range(2):
                t = [idx_s[0, base + half * 4 + k] for k in range(4)]
                g = [gate[e * num_tok + t[k]] for k in range(4)]
                for cb in range(d_model // width):
                    cols = slice(cb * width, (cb + 1) * width)
                    new = [acc[pl.ds(t[k], 1), cols] + o[pl.ds(base + half * 4 + k, 1), cols] * g[k] for k in range(4)]
                    for k in range(4):
                        acc[pl.ds(t[k], 1), cols] = new[k]
            return c

        lax.fori_loop(0, (rows + 7) // 8, eight, 0)

    def item_body(item, c):
        e, p0, rows = meta[item], meta[MAX_ITEMS + item], meta[2 * MAX_ITEMS + item]
        low = 0
        for m in row_sizes:
            @pl.when((rows > low) & (rows <= m))
            def _():
                process(m, item, e, p0)

            low = m
        scatter(e, rows)
        return c

    lax.fori_loop(0, num_items, item_body, 0)
    out_copies = []
    for s in range(shards // 2):
        dst = pl.ds(s * tc, tc)
        mine = pl.ds(pl.multiple_of((2 * s + parity) * tc, tc), tc)
        other = pl.ds(pl.multiple_of((2 * s + 1 - parity) * tc, tc), tc)
        out_copies.append(pltpu.make_async_copy(acc.at[other, :], send_hbm.at[dst, :], out_sem.at[s, 0]))
        out_copies.append(pltpu.make_async_copy(acc.at[mine, :], keep_hbm.at[dst, :], out_sem.at[s, 1]))
    for cp in out_copies:
        cp.start()
    for cp in out_copies:
        cp.wait()


def expert_block(row0, units, meta, gate, pos, digits, tok, w_gate, w_up, w_down):
    shards, _, d_model = tok.shape
    num_tok = shards * units * UNIT
    num_local, _, ff_dim = w_gate.shape
    smem = pl.BlockSpec(memory_space=pltpu.SMEM)
    vmem = pl.BlockSpec(memory_space=pltpu.VMEM)
    anym = pl.BlockSpec(memory_space=pl.ANY)
    rows = num_tok * 3 // 4
    half = jax.ShapeDtypeStruct((num_tok // 2, d_model), jnp.float32)
    up_steps, down_steps = ff_dim // FF_BLOCK, d_model // OUT_BLOCK

    def body(*refs):
        expert_kernel(row0, ROW_SIZES[units], *refs)

    return pl.pallas_call(
        body,
        out_shape=(half, half),
        in_specs=[smem, smem, vmem, vmem, anym, anym, anym, anym],
        out_specs=(anym, anym),
        scratch_shapes=[
            pltpu.VMEM((num_tok, d_model), jnp.bfloat16),
            pltpu.VMEM((num_tok + 8, d_model), jnp.float32),
            pltpu.VMEM((up_steps, d_model, FF_BLOCK), jnp.bfloat16),
            pltpu.VMEM((up_steps, d_model, FF_BLOCK), jnp.bfloat16),
            pltpu.VMEM((down_steps, ff_dim, OUT_BLOCK), jnp.bfloat16),
            pltpu.VMEM((MAX_ROWS, num_tok), jnp.bfloat16),
            pltpu.VMEM((MAX_ROWS, d_model), jnp.bfloat16),
            pltpu.VMEM((MAX_ROWS, ff_dim), jnp.bfloat16),
            pltpu.VMEM((MAX_ROWS, d_model), jnp.float32),
            pltpu.VMEM((8, MAX_ROWS), jnp.int32),
            pltpu.SMEM((8, MAX_ROWS), jnp.int32),
            pltpu.SemaphoreType.DMA((up_steps, 2)),
            pltpu.SemaphoreType.DMA((down_steps,)),
            pltpu.SemaphoreType.DMA((shards,)),
            pltpu.SemaphoreType.DMA,
            pltpu.SemaphoreType.DMA((shards // 2, 2)),
        ],
        compiler_params=pltpu.CompilerParams(vmem_limit_bytes=67_000_000),
        cost_estimate=pl.CostEstimate(flops=rows * 6 * d_model * ff_dim * 2, transcendentals=rows * ff_dim,
                                      bytes_accessed=num_local * 6 * d_model * ff_dim + num_tok * d_model * 6),
        name='expert_block',
    )(meta, gate, pos, digits, tok, w_gate, w_up, w_down)


def pair_kernel(keep, send, out, mine, theirs, send_sem, recv_sem, keep_sem, out_sem):
    me = lax.axis_index('ep')
    other = me + 1 - 2 * lax.rem(me, 2)
    barrier = pltpu.get_barrier_semaphore()
    pl.semaphore_signal(barrier, inc=1, device_id={'ep': other}, device_id_type=pl.DeviceIdType.MESH)
    pl.semaphore_wait(barrier, 1)
    size = keep.shape[0] // PIECES
    remote, local, done = [], [], []
    for p in range(PIECES):
        rows = pl.ds(p * size, size)
        remote.append(pltpu.make_async_remote_copy(
            src_ref=send.at[rows, :], dst_ref=theirs.at[rows, :], send_sem=send_sem.at[p], recv_sem=recv_sem.at[p],
            device_id={'ep': other}, device_id_type=pl.DeviceIdType.MESH))
        local.append(pltpu.make_async_copy(keep.at[rows, :], mine.at[rows, :], keep_sem.at[p]))
        done.append(pltpu.make_async_copy(mine.at[rows, :], out.at[rows, :], out_sem.at[p]))
    for p in range(PIECES):
        remote[p].start()
        local[p].start()
    for p in range(PIECES):
        local[p].wait()
        remote[p].wait_recv()

        def add(i, c, p=p):
            at = pl.ds(pl.multiple_of(p * size + i * 8, 8), 8)
            mine[at, :] = mine[at, :] + theirs[at, :]
            return c

        lax.fori_loop(0, size // 8, add, 0)
        done[p].start()
    for p in range(PIECES):
        remote[p].wait_send()
        done[p].wait()


def pair_sum(keep, send, call_id):
    rows, d_model = keep.shape
    anym = pl.BlockSpec(memory_space=pl.ANY)
    return pl.pallas_call(
        pair_kernel,
        out_shape=jax.ShapeDtypeStruct((rows, d_model), jnp.float32),
        in_specs=[anym, anym],
        out_specs=anym,
        scratch_shapes=[
            pltpu.VMEM((rows, d_model), jnp.float32),
            pltpu.VMEM((rows, d_model), jnp.float32),
            pltpu.SemaphoreType.DMA((PIECES,)),
            pltpu.SemaphoreType.DMA((PIECES,)),
            pltpu.SemaphoreType.DMA((PIECES,)),
            pltpu.SemaphoreType.DMA((PIECES,)),
        ],
        compiler_params=pltpu.CompilerParams(collective_id=call_id, has_side_effects=True, vmem_limit_bytes=67_000_000),
        cost_estimate=pl.CostEstimate(flops=rows * d_model * 4000, transcendentals=0, bytes_accessed=rows * d_model * 16),
        name='pair_sum',
    )(keep, send)


def routing_tables(expert_ids, gate_wts, slot_ids, my_rank, num_local, group_size):
    tok_dev, top_k = expert_ids.shape
    units = tok_dev // UNIT
    key = jnp.where(slot_ids >= 0, expert_ids, -1).astype(jnp.float32).T
    packed = lax.all_gather(jnp.concatenate([key, gate_wts.T], axis=0), 'ep')
    packed = packed.reshape(group_size, 2, top_k, units, UNIT).transpose(1, 2, 0, 3, 4)
    local = (my_rank * num_local + jnp.arange(num_local)).astype(jnp.float32)[:, None, None, None, None]
    hit = packed[0][None] == local
    mask = jnp.any(hit, axis=1)
    gate = jnp.sum(jnp.where(hit, packed[1][None], 0.0), axis=1)

    before = (jnp.arange(UNIT)[:, None] < jnp.arange(UNIT)[None, :]).astype(jnp.bfloat16)
    inner = jnp.einsum('erbk,kl->erbl', mask.astype(jnp.bfloat16), before, preferred_element_type=jnp.float32)
    sums = jnp.sum(mask.astype(jnp.float32), axis=3).reshape(num_local, group_size * units)
    chunk_of_unit = [c for c, n in enumerate(CHUNK_UNITS) for _ in range(n)]
    chunk_of = jnp.tile(jnp.array(chunk_of_unit), group_size)
    block = jnp.arange(group_size * units)
    earlier = (block[:, None] < block[None, :]) & (chunk_of[:, None] == chunk_of[None, :])
    outer = jnp.sum(jnp.where(earlier, sums[:, :, None], 0.0), axis=1).reshape(num_local, group_size, units, 1)
    pos = jnp.where(mask, inner + outer, -1.0).astype(jnp.int32)

    chunks = len(CHUNK_UNITS)
    in_chunk = chunk_of[None, :] == jnp.arange(chunks)[:, None]
    count = jnp.sum(jnp.where(in_chunk[:, None, :], sums[None], 0.0), axis=2).astype(jnp.int32)
    passes = (count + MAX_ROWS - 1) // MAX_ROWS
    upto = jnp.arange(num_local)[:, None] <= jnp.arange(num_local)[None, :]
    ends = jnp.sum(jnp.where(upto, passes[:, :, None], 0), axis=1)
    starts = ends - passes
    item = jnp.arange(MAX_ITEMS)
    mine = (starts[:, :, None] <= item) & (item < ends[:, :, None])
    e = jnp.sum(jnp.where(mine, jnp.arange(num_local)[:, None], 0), axis=1)
    p0 = jnp.sum(jnp.where(mine, (item - starts[:, :, None]) * MAX_ROWS, 0), axis=1)
    rows = jnp.minimum(jnp.sum(jnp.where(mine, count[:, :, None], 0), axis=1) - p0, MAX_ROWS)
    extra = jnp.where(item[None, :] == 0, ends[:, -1:], my_rank % 2)
    meta = jnp.concatenate([e, p0, rows, extra], axis=1).astype(jnp.int32)
    tables = []
    unit0 = 0
    for c, n in enumerate(CHUNK_UNITS):
        span = slice(unit0, unit0 + n)
        num_tok = group_size * n * UNIT
        flat_gate = jnp.pad(gate[:, :, span].reshape(num_local * num_tok), (0, 128))
        tables.append((meta[c], flat_gate, pos[:, :, span].reshape(num_local, 1, num_tok)))
        unit0 += n
    return tables


def solution(mesh):
    group_size = mesh.shape['ep']
    row_spec = P(('dp', 'ep'), None)
    expert_spec = P('ep', None, None)
    same_core = [list(range(core, group_size, 2)) for core in range(2)]

    def per_device(tokens, expert_ids, gate_wts, slot_ids, w_gate, w_up, w_down):
        my_rank = lax.axis_index('ep')
        starts = [UNIT * sum(CHUNK_UNITS[:c]) for c in range(len(CHUNK_UNITS) + 1)]
        source = {}
        for members in GATHERS:
            first, last = starts[members[0]], starts[members[-1] + 1]
            whole = lax.all_gather(tokens[first:last], 'ep', axis=0, tiled=False)
            for c in members:
                source[c] = (whole, starts[c] - first)
        tables = routing_tables(expert_ids, gate_wts, slot_ids, my_rank, w_gate.shape[0], group_size)
        outs = []
        last = None
        for c, units in enumerate(CHUNK_UNITS):
            tok, row0 = source[c]
            ids = jnp.arange(group_size * units * UNIT)
            digits = jnp.stack([ids // ID_RADIX, ids % ID_RADIX, jnp.ones_like(ids)] + [jnp.zeros_like(ids)] * 5).astype(jnp.bfloat16)
            meta, gate, pos = tables[c]
            if last is not None:
                meta, last = lax.optimization_barrier((meta, last))
                outs.append(lax.psum_scatter(last, 'ep', scatter_dimension=0, tiled=True, axis_index_groups=same_core))
            keep, send = expert_block(row0, units, meta, gate, pos, digits, tok, w_gate, w_up, w_down)
            last = pair_sum(keep, send, c)
        outs.append(lax.psum_scatter(last, 'ep', scatter_dimension=0, tiled=True, axis_index_groups=same_core))
        return jnp.concatenate([part.astype(jnp.bfloat16) for part in outs], axis=0)

    return jax.shard_map(per_device, mesh=mesh, in_specs=(row_spec, row_spec, row_spec, row_spec, expert_spec, expert_spec, expert_spec), out_specs=row_spec, check_vma=False)
```

time: 810 us -> 744 us (0.919)
  waiting for transfers between devices: 190 us -> 78 us
  Pallas kernels: 569 us -> 598 us
  local copies, waits for them, and re-layouts: 9.51 us -> 21.2 us
    reduce_scatter x4 -> x5, waiting for transfers between devices: 151 us -> 67.6 us  [per_device(): lax.psum_scatter(last, 'ep', scatter_dimension=0, tiled=True, axis_index_...]
    pallas_call x4 -> x10, Pallas kernels: 569 us -> 598 us  [the longest x5 509 us: expert_block(): pl.pallas_call(body, out_shape=(half, half), in_specs=[smem, smem, vmem,...]
    all_gather x4 -> x3, waiting for transfers between devices: 36.3 us -> 10.2 us  [per_device(): whole = lax.all_gather(tokens[first:last], 'ep', axis=0, tiled=False)]
    unnamed x1 -> x5, other arithmetic: 0.01 us -> 11 us
    convert_element_type x6 -> x1, other arithmetic: 8.91 us -> 0.01 us  [routing_tables(): jnp.sum(jnp.where(in_chunk[:, None, :], sums[None], 0.0), axis=2)]
  transfers between devices with their start and end apart: 8 -> 8, of which waited for: 2 -> 3; matrix products, arithmetic and copies ran while one was open for 2% -> 4% of each run, Pallas kernels for 70% -> 81%
where the time goes in v2:
time: 744 us; the launch traced here: 743 us
  Pallas kernels  598 us (80%)
  waiting for transfers between devices  78 us (10%)
  local copies, waits for them, and re-layouts  21.2 us (3%)
  blocking collectives  16.4 us (2%)
  other arithmetic  14.6 us (2%)
  between operations  13.9 us (2%)
    pallas_call x5, Pallas kernels, expert_block(): pl.pallas_call(body, out_shape=(half, half), in_specs=[smem, smem, vmem,...  509 us
    pallas_call x5, Pallas kernels, pair_sum(): pl.pallas_call(pair_kernel, out_shape=jax.ShapeDtypeStruct((rows, d_model...  89.7 us
    reduce_scatter x5, waiting for transfers between devices, per_device(): lax.psum_scatter(last, 'ep', scatter_dimension=0, tiled=True, axis_index_...  67.6 us
    all_gather x1, blocking collectives, routing_tables(): packed = lax.all_gather(jnp.concatenate([key, gate_wts.T], axis=0), 'ep')  16.4 us
  transfers between devices with their start and end apart: 8, of which 3 were waited for; matrix products, arithmetic and copies ran while one was open for 4% of the time, Pallas kernels for 81%

profile of v2, /device:TPU:0, one launch (start us, length us, event | category | flops | bytes accessed | tf_op | source)
XLA Modules:
  0.0 743.0 jit_solution(11261476728534339665)
XLA Ops:
  6.5 2.0 slice.70
  8.6 2.5 slice.74
  11.2 3.9 slice.78
  15.2 16.4 %all-gather.4 = f32[8,12,1024]{2,1,0:T(8,128)S(1)} all-gather(f32[1,12,1024]{2,1,0:T(8,128)S(1)} %maximum_bitcast_fusion), channel_id=2, replica_groups=mesh['dp'=1,'ep'=8] {'ep'}, dimensions={0}, use_global_device_ids=true | all-gather | bytes 442368 | tf_op jit(solution)/shard_map/all_gather | solution.py:254
  31.7 0.3 compare_reduce_fusion
  32.0 0.1 convert_reduce_fusion
  32.3 0.1 select_reduce_fusion.5
  32.5 0.1 select_reduce_fusion
  32.7 0.2 fusion
  33.0 0.7 copy-done
  33.7 0.6 fusion.13
  34.3 0.6 pad.17.refs_1_
  35.0 0.6 stack.6.refs_3_
  35.7 0.2 slice_reduce_fusion
  35.9 0.1 select_reduce_fusion.3
  36.2 0.6 slice_bitcast_fusion.4
  36.8 0.2 fusion.2
  37.0 0.7 copy-done.2
  37.7 0.7 slice_bitcast_fusion.2
  38.4 10.2 %all-gather.9.cloned.1.call-done = bf16[1024,2560]{1,0:T(8,128)(2,1)} async-done(((bf16[128,2560]{1,0:T(8,128)(2,1)}), bf16[1024,2560]{1,0:T(8,128)(2,1)}) %all-gather.9.cloned.1.call-update) | async-done | bytes 5242896 | tf_op jit(solution)/shard_map/all_gather | solution.py:308
  48.6 77.5 %expert_block.5 = (f32[512,2560]{1,0:T(8,128)}, f32[512,2560]{1,0:T(8,128)}) custom-call(s32[128]{0:T(128)} %get-tuple-element.59.refs_0_, f32[8320]{0:T(1024)} %pad.17.refs_1_, s32[8,1,1024]{2,1,0:T(1,128)} %get-tuple-element.47.refs_2_, bf16[8,1024]{1,0:T(8,128)(2,1)} %stack.6.refs_3_, bf16[8,128,2560]{2,1,0:T(8,128)(2,1)} %bitcast.46, ...), custom_call_target="tpu_custom_call" | custom-call | flops 36238786560 | bytes 204472320 | tf_op jit(solution)/shard_map/expert_block/pallas_call | solution.py:164
  126.1 12.9 %pair_sum.5 = f32[512,2560]{1,0:T(8,128)} custom-call(f32[512,2560]{1,0:T(8,128)} %get-tuple-element.23.keep, f32[512,2560]{1,0:T(8,128)} %get-tuple-element.24.send), custom_call_target="tpu_custom_call" | custom-call | flops 5242880000 | bytes 20971520 | tf_op jit(solution)/shard_map/pair_sum/pallas_call | solution.py:231
  139.1 0.9 copy-done.1
  140.0 0.7 fusion.15
  140.7 0.6 pad.18.refs_1_
  141.4 0.7 stack.7.refs_3_
  142.1 0.7 fusion.14
  142.8 116.9 %expert_block.6 = (f32[1024,2560]{1,0:T(8,128)}, f32[1024,2560]{1,0:T(8,128)}) custom-call(s32[128]{0:T(128)} %get-tuple-element.26.refs_0_, f32[16512]{0:T(1024)} %pad.18.refs_1_, s32[8,1,2048]{2,1,0:T(1,128)} %bitcast.55, bf16[8,2048]{1,0:T(8,128)(2,1)} %stack.7.refs_3_, bf16[8,256,2560]{2,1,0:T(8,128)(2,1)} %bitcast.57, bf16[8,2560,1536]{2,1,0:T(8,128)(2,1)} %refs_5_.9, ...), custom_call_target="tpu_custom_call" | custom-call | flops 72477573120 | bytes 220200960 | tf_op jit(solution)/shard_map/expert_block/pallas_call | solution.py:164
  259.8 24.0 %pair_sum.6 = f32[1024,2560]{1,0:T(8,128)} custom-call(f32[1024,2560]{1,0:T(8,128)} %get-tuple-element.27.keep, f32[1024,2560]{1,0:T(8,128)} %get-tuple-element.28.send), custom_call_target="tpu_custom_call" | custom-call | flops 10485760000 | bytes 41943040 | tf_op jit(solution)/shard_map/pair_sum/pallas_call | solution.py:231
  283.9 0.8 copy-done.5
  284.7 0.6 pad.19.refs_1_
  285.3 119.5 %expert_block.7 = (f32[1024,2560]{1,0:T(8,128)}, f32[1024,2560]{1,0:T(8,128)}) custom-call(s32[128]{0:T(128)} %get-tuple-element.30.refs_0_, f32[16512]{0:T(1024)} %pad.19.refs_1_, s32[8,1,2048]{2,1,0:T(1,128)} %bitcast.54, bf16[8,2048]{1,0:T(8,128)(2,1)} %stack.7.refs_3_, bf16[8,640,2560]{2,1,0:T(8,128)(2,1)} %bitcast.43, bf16[8,2560,1536]{2,1,0:T(8,128)(2,1)} %refs_5_.9, ...), custom_call_target="tpu_custom_call" | custom-call | flops 72477573120 | bytes 220200960 | tf_op jit(solution)/shard_map/expert_block/pallas_call | solution.py:164
  404.8 18.0 %pair_sum.7 = f32[1024,2560]{1,0:T(8,128)} custom-call(f32[1024,2560]{1,0:T(8,128)} %get-tuple-element.31.keep, f32[1024,2560]{1,0:T(8,128)} %get-tuple-element.32.send), custom_call_target="tpu_custom_call" | custom-call | flops 10485760000 | bytes 41943040 | tf_op jit(solution)/shard_map/pair_sum/pallas_call | solution.py:231
  422.8 0.8 copy-done.4
  423.6 0.6 pad.20.refs_1_
  424.2 117.4 %expert_block.8 = (f32[1024,2560]{1,0:T(8,128)}, f32[1024,2560]{1,0:T(8,128)}) custom-call(s32[128]{0:T(128)} %get-tuple-element.34.refs_0_, f32[16512]{0:T(1024)} %pad.20.refs_1_, s32[8,1,2048]{2,1,0:T(1,128)} %bitcast.53, bf16[8,2048]{1,0:T(8,128)(2,1)} %stack.7.refs_3_, bf16[8,640,2560]{2,1,0:T(8,128)(2,1)} %bitcast.44, bf16[8,2560,1536]{2,1,0:T(8,128)(2,1)} %refs_5_.9, ...), custom_call_target="tpu_custom_call" | custom-call | flops 72477573120 | bytes 220200960 | tf_op jit(solution)/shard_map/expert_block/pallas_call | solution.py:164
  541.6 22.9 %pair_sum.8 = f32[1024,2560]{1,0:T(8,128)} custom-call(f32[1024,2560]{1,0:T(8,128)} %get-tuple-element.35.keep, f32[1024,2560]{1,0:T(8,128)} %get-tuple-element.36.send), custom_call_target="tpu_custom_call" | custom-call | flops 10485760000 | bytes 41943040 | tf_op jit(solution)/shard_map/pair_sum/pallas_call | solution.py:231
  564.6 0.7 copy-done.6
  565.3 0.6 pad.21.refs_1_
  565.9 77.5 %expert_block.9 = (f32[512,2560]{1,0:T(8,128)}, f32[512,2560]{1,0:T(8,128)}) custom-call(s32[128]{0:T(128)} %get-tuple-element.38.refs_0_, f32[8320]{0:T(1024)} %pad.21.refs_1_, s32[8,1,1024]{2,1,0:T(1,128)} %get-tuple-element.46.refs_2_, bf16[8,1024]{1,0:T(8,128)(2,1)} %stack.6.refs_3_, bf16[8,640,2560]{2,1,0:T(8,128)(2,1)} %bitcast.45, ...), custom_call_target="tpu_custom_call" | custom-call | flops 36238786560 | bytes 204472320 | tf_op jit(solution)/shard_map/expert_block/pallas_call | solution.py:164
  643.4 11.9 %pair_sum.9 = f32[512,2560]{1,0:T(8,128)} custom-call(f32[512,2560]{1,0:T(8,128)} %get-tuple-element.39.keep, f32[512,2560]{1,0:T(8,128)} %get-tuple-element.40.send), custom_call_target="tpu_custom_call" | custom-call | flops 5242880000 | bytes 20971520 | tf_op jit(solution)/shard_map/pair_sum/pallas_call | solution.py:231
  655.3 2.2 convert_dynamic-update-slice_fusion.4
  657.5 2.9 convert_dynamic-update-slice_fusion.2
  660.4 2.9 convert_dynamic-update-slice_fusion.1
  663.4 12.1 %reduce-scatter.12.cloned.1.call-done = f32[256,2560]{1,0:T(8,128)} async-done(((f32[1024,2560]{1,0:T(8,128)}), f32[256,2560]{1,0:T(8,128)}) %reduce-scatter.12.cloned.1.call-update) | async-done | bytes 2621456 | tf_op jit(solution)/shard_map/reduce_scatter | solution.py:321
  675.4 2.9 convert_dynamic-update-slice_fusion
  678.4 55.6 %reduce-scatter.14.cloned.1.call-done = f32[128,2560]{1,0:T(8,128)} async-done(((f32[512,2560]{1,0:T(8,128)}), f32[128,2560]{1,0:T(8,128)}) %reduce-scatter.14.cloned.1.call-update) | async-done | bytes 1310736 | tf_op jit(solution)/shard_map/reduce_scatter | solution.py:324
  733.9 2.2 convert_dynamic-update-slice_fusion.3
  (65 shorter events, 1.3 us)
Async XLA Ops:
  6.5 42.1 %all-gather.9.cloned.1.call-start = ((), (), s32[]{:S(2)}) async-start(), calls=%async_computation.10 | async-start | bytes 5898240 | tf_op jit(solution)/shard_map/all_gather | solution.py:308
  8.5 134.3 %all-gather.11.cloned.1.call-start = ((), (), s32[]{:S(2)}) async-start(), calls=%async_computation.11 | async-start | bytes 11796480 | tf_op jit(solution)/shard_map/all_gather | solution.py:308
  11.1 4.0 copy-start.7
  11.1 4.0 copy-start.8
  11.1 4.1 copy-start.9
  11.1 21.1 %copy-start.10 = (s32[8]{0:T(128)S(1)}, s32[8]{0:T(128)}, u32[]{:S(2)}) copy-start(s32[8]{0:T(128)} %constant.121.clone) | copy-start | bytes 100
  11.1 274.2 %all-gather.13.cloned.1.call-start = ((), (), s32[]{:S(2)}) async-start(), calls=%async_computation.12 | async-start | bytes 29491200 | tf_op jit(solution)/shard_map/all_gather | solution.py:308
  15.1 640.2 %reduce-scatter.6.cloned.1.call-start = ((), (), s32[]{:S(2)}) async-start(), calls=%async_computation.5 | async-start | bytes 6553600 | tf_op jit(solution)/shard_map/reduce_scatter | solution.py:321
  32.9 0.7 copy-start
  37.0 0.7 copy-start.2
  139.0 1.0 copy-start.1
  139.0 3.0 copy-start.3
  139.1 518.5 %reduce-scatter.8.cloned.1.call-start = ((), (), s32[]{:S(2)}) async-start(), calls=%async_computation.6 | async-start | bytes 13107200 | tf_op jit(solution)/shard_map/reduce_scatter | solution.py:321
  283.8 0.8 copy-start.5
  283.9 376.6 %reduce-scatter.10.cloned.1.call-start = ((), (), s32[]{:S(2)}) async-start(), calls=%async_computation.7 | async-start | bytes 13107200 | tf_op jit(solution)/shard_map/reduce_scatter | solution.py:321
  422.7 0.8 copy-start.4
  422.8 252.7 %reduce-scatter.12.cloned.1.call-start = ((), (), s32[]{:S(2)}) async-start(), calls=%async_computation.8 | async-start | bytes 13107200 | tf_op jit(solution)/shard_map/reduce_scatter | solution.py:321
  564.5 0.8 copy-start.6
  564.5 169.4 %reduce-scatter.14.cloned.1.call-start = ((), (), s32[]{:S(2)}) async-start(), calls=%async_computation.9 | async-start | bytes 6553600 | tf_op jit(solution)/shard_map/reduce_scatter | solution.py:324
Sparse Core Ops, SparseCore 0:
  9.1 39.4 all-gather.8
  50.4 57.5 all-gather.10
  109.8 124.0 all-gather.12
  236.7 55.5 reduce-scatter.5
  295.2 97.7 reduce-scatter.7
  422.9 106.7 reduce-scatter.9
  564.7 110.7 reduce-scatter.11
  678.3 55.5 reduce-scatter.13

commit v3 on v2

--- a/solution.py
+++ b/solution.py
@@ -8,22 +8,25 @@
 UNIT = 128
 CHUNK_UNITS = (1, 2, 2, 2, 1)
 GATHERS = ((0,), (1,), (2, 3, 4))
-ROW_SIZES = {1: (128, 160, 384), 2: (128, 256, 288, 384)}
-MAX_ROWS = 384
+ROW_SIZES = {1: (160, 320), 2: (128, 256, 288, 320)}
+MAX_ROWS = 320
 MAX_ITEMS = 32
-FF_BLOCK = 256
+FF_BLOCK = 512
+FF_PART = 256
 OUT_BLOCK = 512
+LANES = 128
 ID_RADIX = 64
 PIECES = 8
 
 
-def expert_kernel(row0, row_sizes, meta, gate, pos, digits, tok_hbm, wg_hbm, wu_hbm, wd_hbm, keep_hbm, send_hbm,
-                  tok, acc, wg, wu, wd, onehot, x, h, o, idx_v, idx_s, up_sem, down_sem, tok_sem, idx_sem, out_sem):
+def expert_kernel(row0, row_sizes, split, meta, gate, pos, digits, tok_hbm, wg_hbm, wu_hbm, wd_hbm, *refs):
+    outs, (tok, acc, wg, wu, wd, onehot, x, h, o, idx_v, idx_s, up_sem, down_sem, tok_sem, idx_sem, out_sem) = refs[:1 + split], refs[1 + split:]
     num_tok, d_model = tok.shape
     shards = tok_hbm.shape[0]
     tc = num_tok // shards
     ff_dim = wg_hbm.shape[2]
     up_steps, down_steps = ff_dim // FF_BLOCK, d_model // OUT_BLOCK
+    lines = d_model // LANES
     num_items = meta[3 * MAX_ITEMS]
     parity = meta[3 * MAX_ITEMS + 1]
 
@@ -33,9 +36,8 @@
         return (pltpu.make_async_copy(wg_hbm.at[e, :, cols], wg.at[j], up_sem.at[j, 0]),
                 pltpu.make_async_copy(wu_hbm.at[e, :, cols], wu.at[j], up_sem.at[j, 1]))
 
-    def down_copy(item, j):
-        cols = pl.ds(pl.multiple_of(j * OUT_BLOCK, OUT_BLOCK), OUT_BLOCK)
-        return pltpu.make_async_copy(wd_hbm.at[meta[item], :, cols], wd.at[j], down_sem.at[j])
+    def down_copy(item):
+        return pltpu.make_async_copy(wd_hbm.at[meta[item]], wd, down_sem)
 
     tok_copies = [pltpu.make_async_copy(tok_hbm.at[s, pl.ds(row0, tc), :], tok.at[pl.ds(s * tc, tc), :], tok_sem.at[s])
                   for s in range(shards)]
@@ -47,20 +49,24 @@
         for j in range(up_steps):
             for cp in up_copies(0, j):
                 cp.start()
-        for j in range(down_steps):
-            down_copy(0, j).start()
+        down_copy(0).start()
 
     def zero(i, c):
-        acc[pl.ds(pl.multiple_of(i * 8, 8), 8), :] = jnp.zeros((8, d_model), jnp.float32)
+        acc[pl.ds(pl.multiple_of(i * 160, 8), 160), :] = jnp.zeros((160, LANES), jnp.float32)
         return c
 
-    lax.fori_loop(0, acc.shape[0] // 8, zero, 0)
+    lax.fori_loop(0, acc.shape[0] // 160, zero, 0)
     for cp in tok_copies:
         cp.wait()
 
     def process(m, item, e, p0):
-        want = lax.broadcasted_iota(jnp.int32, (m, num_tok), 0) + p0
-        onehot[:m, :] = jnp.where(want == pos[e], 1.0, 0.0).astype(jnp.bfloat16)
+        def select(i, c):
+            row = pl.multiple_of(i * 32, 32)
+            want = lax.broadcasted_iota(jnp.int32, (32, num_tok), 0) + (p0 + row)
+            onehot[pl.ds(row, 32), :] = jnp.where(want == pos[e], 1.0, 0.0).astype(jnp.bfloat16)
+            return c
+
+        lax.fori_loop(0, m // 32, select, 0)
         parts = lax.dot_general(digits[...], onehot[:m, :], (((1,), (1,)), ((), ())), preferred_element_type=jnp.float32)
         idx = parts[0:1] * ID_RADIX + parts[1:2] + (1.0 - parts[2:3]) * num_tok
         idx_v[:, :m] = jnp.broadcast_to(idx.astype(jnp.int32), (8, m))
@@ -77,9 +83,16 @@
         def up(j, c):
             for cp in up_copies(item, j):
                 cp.wait()
-            a = jnp.dot(x[:m, :], wg[j], preferred_element_type=jnp.float32)
-            u = jnp.dot(x[:m, :], wu[j], preferred_element_type=jnp.float32)
-            h[:m, pl.ds(pl.multiple_of(j * FF_BLOCK, FF_BLOCK), FF_BLOCK)] = (jax.nn.silu(a) * u).astype(jnp.bfloat16)
+
+            def part(k, c):
+                cols = pl.ds(pl.multiple_of(k * FF_PART, FF_PART), FF_PART)
+                a = jnp.dot(x[:m, :], wg[j, :, cols], preferred_element_type=jnp.float32)
+                u = jnp.dot(x[:m, :], wu[j, :, cols], preferred_element_type=jnp.float32)
+                to = pl.ds(pl.multiple_of(j * FF_BLOCK + k * FF_PART, FF_PART), FF_PART)
+                h[:m, to] = (jax.nn.silu(a) * u).astype(jnp.bfloat16)
+                return c
+
+            lax.fori_loop(0, FF_BLOCK // FF_PART, part, 0)
 
             @pl.when(item + 1 < num_items)
             def _():
@@ -89,34 +102,36 @@
             return c
 
         lax.fori_loop(0, up_steps, up, 0)
+        down_copy(item).wait()
 
         def down(j, c):
-            down_copy(item, j).wait()
             cols = pl.ds(pl.multiple_of(j * OUT_BLOCK, OUT_BLOCK), OUT_BLOCK)
-            o[:m, cols] = jnp.dot(h[:m, :], wd[j], preferred_element_type=jnp.float32)
-
-            @pl.when(item + 1 < num_items)
-            def _():
-                down_copy(item + 1, j).start()
-
+            part = jnp.dot(h[:m, :], wd[:, cols], preferred_element_type=jnp.float32)
+            for k in range(OUT_BLOCK // LANES):
+                o[pl.ds(j * (OUT_BLOCK // LANES) + k, m, stride=lines), :] = part[:, k * LANES:(k + 1) * LANES]
             return c
 
         lax.fori_loop(0, down_steps, down, 0)
+
+        @pl.when(item + 1 < num_items)
+        def _():
+            down_copy(item + 1).start()
+
         idx_copy.wait()
 
     def scatter(e, rows):
-        width = 640
+        spans = [(at, min(8, lines - at)) for at in range(0, lines, 8)]
 
         def eight(i, c):
-            base = pl.multiple_of(i * 8, 8)
+            base = i * 8
             for half in range(2):
                 t = [idx_s[0, base + half * 4 + k] for k in range(4)]
                 g = [gate[e * num_tok + t[k]] for k in range(4)]
-                for cb in range(d_model // width):
-                    cols = slice(cb * width, (cb + 1) * width)
-                    new = [acc[pl.ds(t[k], 1), cols] + o[pl.ds(base + half * 4 + k, 1), cols] * g[k] for k in range(4)]
-                    for k in range(4):
-                        acc[pl.ds(t[k], 1), cols] = new[k]
+                new = [[acc[pl.ds(t[k] * lines + at, n), :] + o[pl.ds((base + half * 4 + k) * lines + at, n), :] * g[k]
+                        for at, n in spans] for k in range(4)]
+                for k in range(4):
+                    for (at, n), value in zip(spans, new[k]):
+                        acc[pl.ds(t[k] * lines + at, n), :] = value
             return c
 
         lax.fori_loop(0, (rows + 7) // 8, eight, 0)
@@ -135,19 +150,23 @@
 
     lax.fori_loop(0, num_items, item_body, 0)
     out_copies = []
-    for s in range(shards // 2):
-        dst = pl.ds(s * tc, tc)
-        mine = pl.ds(pl.multiple_of((2 * s + parity) * tc, tc), tc)
-        other = pl.ds(pl.multiple_of((2 * s + 1 - parity) * tc, tc), tc)
-        out_copies.append(pltpu.make_async_copy(acc.at[other, :], send_hbm.at[dst, :], out_sem.at[s, 0]))
-        out_copies.append(pltpu.make_async_copy(acc.at[mine, :], keep_hbm.at[dst, :], out_sem.at[s, 1]))
+    size = tc * lines
+    if split:
+        for s in range(shards // 2):
+            dst = pl.ds(s * size, size)
+            mine = pl.ds(pl.multiple_of((2 * s + parity) * size, size), size)
+            other = pl.ds(pl.multiple_of((2 * s + 1 - parity) * size, size), size)
+            out_copies.append(pltpu.make_async_copy(acc.at[other, :], outs[1].at[dst, :], out_sem.at[s, 0]))
+            out_copies.append(pltpu.make_async_copy(acc.at[mine, :], outs[0].at[dst, :], out_sem.at[s, 1]))
+    else:
+        out_copies.append(pltpu.make_async_copy(acc.at[pl.ds(0, shards * size), :], outs[0], out_sem.at[0, 0]))
     for cp in out_copies:
         cp.start()
     for cp in out_copies:
         cp.wait()
 
 
-def expert_block(row0, units, meta, gate, pos, digits, tok, w_gate, w_up, w_down):
+def expert_block(row0, units, split, meta, gate, pos, digits, tok, w_gate, w_up, w_down):
     shards, _, d_model = tok.shape
     num_tok = shards * units * UNIT
     num_local, _, ff_dim = w_gate.shape
@@ -155,31 +174,32 @@
     vmem = pl.BlockSpec(memory_space=pltpu.VMEM)
     anym = pl.BlockSpec(memory_space=pl.ANY)
     rows = num_tok * 3 // 4
-    half = jax.ShapeDtypeStruct((num_tok // 2, d_model), jnp.float32)
-    up_steps, down_steps = ff_dim // FF_BLOCK, d_model // OUT_BLOCK
+    lines = d_model // LANES
+    out = jax.ShapeDtypeStruct((num_tok // (1 + split) * lines, LANES), jnp.float32)
+    up_steps = ff_dim // FF_BLOCK
 
     def body(*refs):
-        expert_kernel(row0, ROW_SIZES[units], *refs)
+        expert_kernel(row0, ROW_SIZES[units], split, *refs)
 
     return pl.pallas_call(
         body,
-        out_shape=(half, half),
+        out_shape=(out,) * (1 + split),
         in_specs=[smem, smem, vmem, vmem, anym, anym, anym, anym],
-        out_specs=(anym, anym),
+        out_specs=(anym,) * (1 + split),
         scratch_shapes=[
             pltpu.VMEM((num_tok, d_model), jnp.bfloat16),
-            pltpu.VMEM((num_tok + 8, d_model), jnp.float32),
+            pltpu.VMEM(((num_tok + 8) * lines, LANES), jnp.float32),
             pltpu.VMEM((up_steps, d_model, FF_BLOCK), jnp.bfloat16),
             pltpu.VMEM((up_steps, d_model, FF_BLOCK), jnp.bfloat16),
-            pltpu.VMEM((down_steps, ff_dim, OUT_BLOCK), jnp.bfloat16),
+            pltpu.VMEM((ff_dim, d_model), jnp.bfloat16),
             pltpu.VMEM((MAX_ROWS, num_tok), jnp.bfloat16),
             pltpu.VMEM((MAX_ROWS, d_model), jnp.bfloat16),
             pltpu.VMEM((MAX_ROWS, ff_dim), jnp.bfloat16),
-            pltpu.VMEM((MAX_ROWS, d_model), jnp.float32),
+            pltpu.VMEM((MAX_ROWS * lines, LANES), jnp.float32),
             pltpu.VMEM((8, MAX_ROWS), jnp.int32),
             pltpu.SMEM((8, MAX_ROWS), jnp.int32),
             pltpu.SemaphoreType.DMA((up_steps, 2)),
-            pltpu.SemaphoreType.DMA((down_steps,)),
+            pltpu.SemaphoreType.DMA,
             pltpu.SemaphoreType.DMA((shards,)),
             pltpu.SemaphoreType.DMA,
             pltpu.SemaphoreType.DMA((shards // 2, 2)),
@@ -214,11 +234,11 @@
         remote[p].wait_recv()
 
         def add(i, c, p=p):
-            at = pl.ds(pl.multiple_of(p * size + i * 8, 8), 8)
+            at = pl.ds(pl.multiple_of(p * size + i * 160, 8), 160)
             mine[at, :] = mine[at, :] + theirs[at, :]
             return c
 
-        lax.fori_loop(0, size // 8, add, 0)
+        lax.fori_loop(0, size // 160, add, 0)
         done[p].start()
     for p in range(PIECES):
         remote[p].wait_send()
@@ -299,7 +319,7 @@
     expert_spec = P('ep', None, None)
     same_core = [list(range(core, group_size, 2)) for core in range(2)]
 
-    def per_device(tokens, expert_ids, gate_wts, slot_ids, w_gate, w_up, w_down):
+    def layer(tokens, expert_ids, gate_wts, slot_ids, w_gate, w_up, w_down):
         my_rank = lax.axis_index('ep')
         starts = [UNIT * sum(CHUNK_UNITS[:c]) for c in range(len(CHUNK_UNITS) + 1)]
         source = {}
@@ -311,6 +331,12 @@
         tables = routing_tables(expert_ids, gate_wts, slot_ids, my_rank, w_gate.shape[0], group_size)
         outs = []
         last = None
+
+        def reduce(part, c):
+            groups = same_core if c > 0 else None
+            part = lax.psum_scatter(part, 'ep', scatter_dimension=0, tiled=True, axis_index_groups=groups)
+            return part.reshape(-1, tokens.shape[1]).astype(jnp.bfloat16)
+
         for c, units in enumerate(CHUNK_UNITS):
             tok, row0 = source[c]
             ids = jnp.arange(group_size * units * UNIT)
@@ -318,10 +344,10 @@
             meta, gate, pos = tables[c]
             if last is not None:
                 meta, last = lax.optimization_barrier((meta, last))
-                outs.append(lax.psum_scatter(last, 'ep', scatter_dimension=0, tiled=True, axis_index_groups=same_core))
-            keep, send = expert_block(row0, units, meta, gate, pos, digits, tok, w_gate, w_up, w_down)
-            last = pair_sum(keep, send, c)
-        outs.append(lax.psum_scatter(last, 'ep', scatter_dimension=0, tiled=True, axis_index_groups=same_core))
-        return jnp.concatenate([part.astype(jnp.bfloat16) for part in outs], axis=0)
-
-    return jax.shard_map(per_device, mesh=mesh, in_specs=(row_spec, row_spec, row_spec, row_spec, expert_spec, expert_spec, expert_spec), out_specs=row_spec, check_vma=False)
+                outs.append(reduce(last, c - 1))
+            last = expert_block(row0, units, c > 0, meta, gate, pos, digits, tok, w_gate, w_up, w_down)
+            last = pair_sum(*last, c) if c > 0 else last[0]
+        outs.append(reduce(last, len(CHUNK_UNITS) - 1))
+        return jnp.concatenate(outs, axis=0)
+
+    return jax.shard_map(layer, mesh=mesh, in_specs=(row_spec, row_spec, row_spec, row_spec, expert_spec, expert_spec, expert_spec), out_specs=row_spec, check_vma=False)

time: 744 us -> 918 us (1.23)
  waiting for transfers between devices: 78 us -> 306 us
  Pallas kernels: 598 us -> 537 us
  local copies, waits for them, and re-layouts: 21.2 us -> 31.7 us
    reduce_scatter x5, waiting for transfers between devices: 67.6 us -> 294 us  [reduce(): lax.psum_scatter(part, 'ep', scatter_dimension=0, tiled=True, axis_index_...]
    pallas_call x5, Pallas kernels: 509 us -> 463 us  [expert_block(): pl.pallas_call(body, out_shape=(out,) * (1 + split), in_specs=[smem, smem...]
    pallas_call x5 -> x4, Pallas kernels: 89.7 us -> 73.5 us  [pair_sum(): pl.pallas_call(pair_kernel, out_shape=jax.ShapeDtypeStruct((rows, d_model...]
    unnamed x5 -> x1, other arithmetic: 11 us -> 0.01 us
    convert_element_type x0 -> x5, other arithmetic: none -> 9.43 us  [reduce(): return part.reshape(-1, tokens.shape[1]).astype(jnp.bfloat16)]
  transfers between devices with their start and end apart: 8 -> 8, of which waited for: 3 -> 4; matrix products, arithmetic and copies ran while one was open for 4% -> 3% of each run, Pallas kernels for 81% -> 59%
where the time goes in v3:
time: 918 us; the launch traced here: 917 us
  Pallas kernels  537 us (58%)
  waiting for transfers between devices  306 us (33%)
  local copies, waits for them, and re-layouts  31.7 us (3%)
  blocking collectives  16.6 us (2%)
  between operations  13.9 us (2%)
  other arithmetic  10.8 us (1%)
    pallas_call x5, Pallas kernels, expert_block(): pl.pallas_call(body, out_shape=(out,) * (1 + split), in_specs=[smem, smem...  463 us
    reduce_scatter x5, waiting for transfers between devices, reduce(): lax.psum_scatter(part, 'ep', scatter_dimension=0, tiled=True, axis_index_...  294 us
    pallas_call x4, Pallas kernels, pair_sum(): pl.pallas_call(pair_kernel, out_shape=jax.ShapeDtypeStruct((rows, d_model...  73.5 us
  transfers between devices with their start and end apart: 8, of which 4 were waited for; matrix products, arithmetic and copies ran while one was open for 3% of the time, Pallas kernels for 59%

profile of v3, /device:TPU:0, one launch (start us, length us, event | category | flops | bytes accessed | tf_op | source)
XLA Modules:
  0.0 916.5 jit_solution(12943469777024067306)
XLA Ops:
  6.5 2.0 slice.70
  8.6 2.5 slice.74
  11.2 3.8 slice.78
  15.2 16.6 %all-gather.4 = f32[8,12,1024]{2,1,0:T(8,128)S(1)} all-gather(f32[1,12,1024]{2,1,0:T(8,128)S(1)} %maximum_bitcast_fusion), channel_id=2, replica_groups=mesh['dp'=1,'ep'=8] {'ep'}, dimensions={0}, use_global_device_ids=true | all-gather | bytes 442368 | tf_op jit(solution)/shard_map/all_gather | solution.py:274
  33.2 0.7 copy-done
  33.9 0.6 pad.17.refs_1_
  34.6 0.6 stack.6.refs_3_
  35.8 0.6 slice_bitcast_fusion.4
  36.6 0.7 copy-done.2
  37.3 0.7 slice_bitcast_fusion.2
  38.0 10.9 %all-gather.9.cloned.1.call-done = bf16[1024,2560]{1,0:T(8,128)(2,1)} async-done(((bf16[128,2560]{1,0:T(8,128)(2,1)}), bf16[1024,2560]{1,0:T(8,128)(2,1)}) %all-gather.9.cloned.1.call-update) | async-done | bytes 5242896 | tf_op jit(solution)/shard_map/all_gather | solution.py:328
  48.9 77.9 %expert_block.5 = f32[20480,128]{1,0:T(8,128)} custom-call(s32[128]{0:T(128)} %get-tuple-element.55.refs_0_, f32[8320]{0:T(1024)} %pad.17.refs_1_, s32[8,1,1024]{2,1,0:T(1,128)} %get-tuple-element.43.refs_2_, bf16[8,1024]{1,0:T(8,128)(2,1)} %stack.6.refs_3_, bf16[8,128,2560]{2,1,0:T(8,128)(2,1)} %bitcast.46, bf16[8,2560,1536]{2,1,0:T(8,128)(2,1)} %refs_5_.9, ...), custom_call_target="tpu_custom_call" | custom-call | flops 36238786560 | bytes 204472320 | tf_op jit(solution)/shard_map/expert_block/pallas_call | solution.py:184
  126.9 0.9 copy-done.1
  127.8 0.7 fusion.15
  128.5 0.6 pad.18.refs_1_
  129.2 0.7 stack.7.refs_3_
  129.9 0.7 fusion.14
  130.6 102.9 %expert_block.6 = (f32[20480,128]{1,0:T(8,128)}, f32[20480,128]{1,0:T(8,128)}) custom-call(s32[128]{0:T(128)} %get-tuple-element.22.refs_0_, f32[16512]{0:T(1024)} %pad.18.refs_1_, s32[8,1,2048]{2,1,0:T(1,128)} %bitcast.55, bf16[8,2048]{1,0:T(8,128)(2,1)} %stack.7.refs_3_, bf16[8,256,2560]{2,1,0:T(8,128)(2,1)} %bitcast.57, bf16[8,2560,1536]{2,1,0:T(8,128)(2,1)} %refs_5_.9, ...), custom_call_target="tpu_custom_call" | custom-call | flops 72477573120 | bytes 220200960 | tf_op jit(solution)/shard_map/expert_block/pallas_call | solution.py:184
  233.6 25.4 %pair_sum.4 = f32[20480,128]{1,0:T(8,128)} custom-call(f32[20480,128]{1,0:T(8,128)} %get-tuple-element.23.keep, f32[20480,128]{1,0:T(8,128)} %get-tuple-element.24.send), custom_call_target="tpu_custom_call" | custom-call | flops 10485760000 | bytes 41943040 | tf_op jit(solution)/shard_map/pair_sum/pallas_call | solution.py:251
  259.1 0.7 copy-done.5
  259.8 0.6 pad.19.refs_1_
  260.5 0.6 pad.20.refs_1_
  261.7 103.2 %expert_block.7 = (f32[20480,128]{1,0:T(8,128)}, f32[20480,128]{1,0:T(8,128)}) custom-call(s32[128]{0:T(128)} %get-tuple-element.26.refs_0_, f32[16512]{0:T(1024)} %pad.19.refs_1_, s32[8,1,2048]{2,1,0:T(1,128)} %bitcast.54, bf16[8,2048]{1,0:T(8,128)(2,1)} %stack.7.refs_3_, bf16[8,640,2560]{2,1,0:T(8,128)(2,1)} %bitcast.43, bf16[8,2560,1536]{2,1,0:T(8,128)(2,1)} %refs_5_.9, ...), custom_call_target="tpu_custom_call" | custom-call | flops 72477573120 | bytes 220200960 | tf_op jit(solution)/shard_map/expert_block/pallas_call | solution.py:184
  364.9 17.9 %pair_sum.5 = f32[20480,128]{1,0:T(8,128)} custom-call(f32[20480,128]{1,0:T(8,128)} %get-tuple-element.27.keep, f32[20480,128]{1,0:T(8,128)} %get-tuple-element.28.send), custom_call_target="tpu_custom_call" | custom-call | flops 10485760000 | bytes 41943040 | tf_op jit(solution)/shard_map/pair_sum/pallas_call | solution.py:251
  382.8 101.9 %expert_block.8 = (f32[20480,128]{1,0:T(8,128)}, f32[20480,128]{1,0:T(8,128)}) custom-call(s32[128]{0:T(128)} %get-tuple-element.30.refs_0_, f32[16512]{0:T(1024)} %pad.20.refs_1_, s32[8,1,2048]{2,1,0:T(1,128)} %bitcast.53, bf16[8,2048]{1,0:T(8,128)(2,1)} %stack.7.refs_3_, bf16[8,640,2560]{2,1,0:T(8,128)(2,1)} %bitcast.44, bf16[8,2560,1536]{2,1,0:T(8,128)(2,1)} %refs_5_.9, ...), custom_call_target="tpu_custom_call" | custom-call | flops 72477573120 | bytes 220200960 | tf_op jit(solution)/shard_map/expert_block/pallas_call | solution.py:184
  484.7 20.1 %pair_sum.6 = f32[20480,128]{1,0:T(8,128)} custom-call(f32[20480,128]{1,0:T(8,128)} %get-tuple-element.31.keep, f32[20480,128]{1,0:T(8,128)} %get-tuple-element.32.send), custom_call_target="tpu_custom_call" | custom-call | flops 10485760000 | bytes 41943040 | tf_op jit(solution)/shard_map/pair_sum/pallas_call | solution.py:251
  504.8 77.2 %expert_block.9 = (f32[10240,128]{1,0:T(8,128)}, f32[10240,128]{1,0:T(8,128)}) custom-call(s32[128]{0:T(128)} %get-tuple-element.34.refs_0_, f32[8320]{0:T(1024)} %pad.21.refs_1_, s32[8,1,1024]{2,1,0:T(1,128)} %get-tuple-element.42.refs_2_, bf16[8,1024]{1,0:T(8,128)(2,1)} %stack.6.refs_3_, bf16[8,640,2560]{2,1,0:T(8,128)(2,1)} %bitcast.45, ...), custom_call_target="tpu_custom_call" | custom-call | flops 36238786560 | bytes 204472320 | tf_op jit(solution)/shard_map/expert_block/pallas_call | solution.py:184
  582.0 10.1 %pair_sum.7 = f32[10240,128]{1,0:T(8,128)} custom-call(f32[10240,128]{1,0:T(8,128)} %get-tuple-element.35.keep, f32[10240,128]{1,0:T(8,128)} %get-tuple-element.36.send), custom_call_target="tpu_custom_call" | custom-call | flops 5242880000 | bytes 20971520 | tf_op jit(solution)/shard_map/pair_sum/pallas_call | solution.py:251
  592.1 0.7 reduce-scatter.10.cloned.1.call-update
  592.9 0.7 reduce-scatter.12.cloned.1.call-update
  593.6 1.4 convert_element_type.78
  595.0 0.7 convert_element_type.79
  595.7 0.9 constant_dynamic-update-slice_fusion.4
  596.6 1.9 convert_element_type.80
  598.5 1.5 convert_element_type.81
  600.0 1.1 constant_dynamic-update-slice_fusion.3
  601.1 97.6 %reduce-scatter.14.cloned.1.call-done = f32[2560,128]{1,0:T(8,128)} async-done(((f32[10240,128]{1,0:T(8,128)}), f32[2560,128]{1,0:T(8,128)}) %reduce-scatter.14.cloned.1.call-update) | async-done | bytes 1310736 | tf_op jit(solution)/shard_map/reduce_scatter | solution.py:337
  698.7 1.4 convert_element_type.86
  700.1 0.7 convert_element_type.87
  700.9 98.8 %reduce-scatter.10.cloned.1.call-done = f32[5120,128]{1,0:T(8,128)} async-done(((f32[20480,128]{1,0:T(8,128)}), f32[5120,128]{1,0:T(8,128)}) %reduce-scatter.10.cloned.1.call-update) | async-done | bytes 2621456 | tf_op jit(solution)/shard_map/reduce_scatter | solution.py:337
  799.7 1.9 convert_element_type.82
  801.6 1.5 convert_element_type.83
  803.1 97.6 %reduce-scatter.12.cloned.1.call-done = f32[5120,128]{1,0:T(8,128)} async-done(((f32[20480,128]{1,0:T(8,128)}), f32[5120,128]{1,0:T(8,128)}) %reduce-scatter.12.cloned.1.call-update) | async-done | bytes 2621456 | tf_op jit(solution)/shard_map/reduce_scatter | solution.py:337
  900.7 2.9 convert_element_type.84
  903.6 2.9 convert_element_type.85
  906.5 1.1 constant_dynamic-update-slice_fusion.2
  907.7 1.1 constant_dynamic-update-slice_fusion.1
  908.8 0.9 constant_dynamic-update-slice_fusion
  (72 shorter events, 3.3 us)
Async XLA Ops:
  6.5 42.3 %all-gather.9.cloned.1.call-start = ((), (), s32[]{:S(2)}) async-start(), calls=%async_computation.10 | async-start | bytes 5898240 | tf_op jit(solution)/shard_map/all_gather | solution.py:328
  8.6 122.1 %all-gather.11.cloned.1.call-start = ((), (), s32[]{:S(2)}) async-start(), calls=%async_computation.11 | async-start | bytes 11796480 | tf_op jit(solution)/shard_map/all_gather | solution.py:328
  11.1 4.0 copy-start.6
  11.1 4.0 copy-start.7
  11.1 4.0 copy-start.8
  11.1 21.3 %copy-start.9 = (s32[8]{0:T(128)S(1)}, s32[8]{0:T(128)}, u32[]{:S(2)}) copy-start(s32[8]{0:T(128)} %constant.121.clone) | copy-start | bytes 100
  11.2 250.6 %all-gather.13.cloned.1.call-start = ((), (), s32[]{:S(2)}) async-start(), calls=%async_computation.12 | async-start | bytes 29491200 | tf_op jit(solution)/shard_map/all_gather | solution.py:328
  15.1 578.5 %reduce-scatter.6.cloned.1.call-start = ((), (), s32[]{:S(2)}) async-start(), calls=%async_computation.5 | async-start | bytes 11796480 | tf_op jit(solution)/shard_map/reduce_scatter | solution.py:337
  33.2 0.7 copy-start
  36.6 0.7 copy-start.2
  126.8 1.0 copy-start.1
  126.8 3.0 copy-start.3
  126.9 469.7 %reduce-scatter.8.cloned.1.call-start = ((), (), s32[]{:S(2)}) async-start(), calls=%async_computation.6 | async-start | bytes 13107200 | tf_op jit(solution)/shard_map/reduce_scatter | solution.py:337
  259.0 0.8 copy-start.5
  259.0 1.5 copy-start.4
  259.0 439.7 %reduce-scatter.14.cloned.1.call-start = ((), (), s32[]{:S(2)}) async-start(), calls=%async_computation.9 | async-start | bytes 6553600 | tf_op jit(solution)/shard_map/reduce_scatter | solution.py:337
  592.1 207.6 %reduce-scatter.10.cloned.1.call-start = ((), (), s32[]{:S(2)}) async-start(), calls=%async_computation.7 | async-start | bytes 13107200 | tf_op jit(solution)/shard_map/reduce_scatter | solution.py:337
  592.8 307.8 %reduce-scatter.12.cloned.1.call-start = ((), (), s32[]{:S(2)}) async-start(), calls=%async_computation.8 | async-start | bytes 13107200 | tf_op jit(solution)/shard_map/reduce_scatter | solution.py:337
Sparse Core Ops, SparseCore 0:
  9.1 39.6 all-gather.8
  50.7 57.6 all-gather.10
  110.2 124.2 all-gather.12
  237.8 75.2 reduce-scatter.5
  315.9 97.9 reduce-scatter.7
  592.2 106.4 reduce-scatter.13
  701.8 97.8 reduce-scatter.9
  802.7 97.8 reduce-scatter.11

commit v4 on v3

--- a/solution.py
+++ b/solution.py
@@ -8,9 +8,8 @@
 UNIT = 128
 CHUNK_UNITS = (1, 2, 2, 2, 1)
 GATHERS = ((0,), (1,), (2, 3, 4))
-ROW_SIZES = {1: (160, 320), 2: (128, 256, 288, 320)}
-MAX_ROWS = 320
-MAX_ITEMS = 32
+ROW_SIZES = {1: (160,), 2: (128, 256, 288, 320)}
+MAX_ITEMS = 64
 FF_BLOCK = 512
 FF_PART = 256
 OUT_BLOCK = 512
@@ -19,8 +18,8 @@
 PIECES = 8
 
 
-def expert_kernel(row0, row_sizes, split, meta, gate, pos, digits, tok_hbm, wg_hbm, wu_hbm, wd_hbm, *refs):
-    outs, (tok, acc, wg, wu, wd, onehot, x, h, o, idx_v, idx_s, up_sem, down_sem, tok_sem, idx_sem, out_sem) = refs[:1 + split], refs[1 + split:]
+def expert_kernel(row0, row_sizes, meta, gate, pos, digits, tok_hbm, wg_hbm, wu_hbm, wd_hbm, *refs):
+    outs, (tok, acc, wg, wu, wd, onehot, x, h, o, idx_v, idx_s, up_sem, down_sem, tok_sem, idx_sem, out_sem) = refs[:2], refs[2:]
     num_tok, d_model = tok.shape
     shards = tok_hbm.shape[0]
     tc = num_tok // shards
@@ -36,20 +35,24 @@
         return (pltpu.make_async_copy(wg_hbm.at[e, :, cols], wg.at[j], up_sem.at[j, 0]),
                 pltpu.make_async_copy(wu_hbm.at[e, :, cols], wu.at[j], up_sem.at[j, 1]))
 
-    def down_copy(item):
-        return pltpu.make_async_copy(wd_hbm.at[meta[item]], wd, down_sem)
+    def down_copies(item):
+        half = ff_dim // 2
+        return [pltpu.make_async_copy(wd_hbm.at[meta[item], pl.ds(k * half, half), :], wd.at[pl.ds(k * half, half), :],
+                                      down_sem.at[k]) for k in range(2)]
+
+    def start_all(copies):
+        for k, cp in enumerate(copies):
+            cp.start(priority=k % 2)
 
     tok_copies = [pltpu.make_async_copy(tok_hbm.at[s, pl.ds(row0, tc), :], tok.at[pl.ds(s * tc, tc), :], tok_sem.at[s])
                   for s in range(shards)]
-    for cp in tok_copies:
-        cp.start()
+    start_all(tok_copies)
 
     @pl.when(num_items > 0)
     def _():
         for j in range(up_steps):
-            for cp in up_copies(0, j):
-                cp.start()
-        down_copy(0).start()
+            start_all(up_copies(0, j))
+        start_all(down_copies(0))
 
     def zero(i, c):
         acc[pl.ds(pl.multiple_of(i * 160, 8), 160), :] = jnp.zeros((160, LANES), jnp.float32)
@@ -96,13 +99,13 @@
 
             @pl.when(item + 1 < num_items)
             def _():
-                for cp in up_copies(item + 1, j):
-                    cp.start()
+                start_all(up_copies(item + 1, j))
 
             return c
 
         lax.fori_loop(0, up_steps, up, 0)
-        down_copy(item).wait()
+        for cp in down_copies(item):
+            cp.wait()
 
         def down(j, c):
             cols = pl.ds(pl.multiple_of(j * OUT_BLOCK, OUT_BLOCK), OUT_BLOCK)
@@ -115,7 +118,7 @@
 
         @pl.when(item + 1 < num_items)
         def _():
-            down_copy(item + 1).start()
+            start_all(down_copies(item + 1))
 
         idx_copy.wait()
 
@@ -151,22 +154,18 @@
     lax.fori_loop(0, num_items, item_body, 0)
     out_copies = []
     size = tc * lines
-    if split:
-        for s in range(shards // 2):
-            dst = pl.ds(s * size, size)
-            mine = pl.ds(pl.multiple_of((2 * s + parity) * size, size), size)
-            other = pl.ds(pl.multiple_of((2 * s + 1 - parity) * size, size), size)
-            out_copies.append(pltpu.make_async_copy(acc.at[other, :], outs[1].at[dst, :], out_sem.at[s, 0]))
-            out_copies.append(pltpu.make_async_copy(acc.at[mine, :], outs[0].at[dst, :], out_sem.at[s, 1]))
-    else:
-        out_copies.append(pltpu.make_async_copy(acc.at[pl.ds(0, shards * size), :], outs[0], out_sem.at[0, 0]))
-    for cp in out_copies:
-        cp.start()
+    for s in range(shards // 2):
+        dst = pl.ds(s * size, size)
+        mine = pl.ds(pl.multiple_of((2 * s + parity) * size, size), size)
+        other = pl.ds(pl.multiple_of((2 * s + 1 - parity) * size, size), size)
+        out_copies.append(pltpu.make_async_copy(acc.at[other, :], outs[1].at[dst, :], out_sem.at[s, 0]))
+        out_copies.append(pltpu.make_async_copy(acc.at[mine, :], outs[0].at[dst, :], out_sem.at[s, 1]))
+    start_all(out_copies)
     for cp in out_copies:
         cp.wait()
 
 
-def expert_block(row0, units, split, meta, gate, pos, digits, tok, w_gate, w_up, w_down):
+def expert_block(row0, units, meta, gate, pos, digits, tok, w_gate, w_up, w_down):
     shards, _, d_model = tok.shape
     num_tok = shards * units * UNIT
     num_local, _, ff_dim = w_gate.shape
@@ -174,32 +173,33 @@
     vmem = pl.BlockSpec(memory_space=pltpu.VMEM)
     anym = pl.BlockSpec(memory_space=pl.ANY)
     rows = num_tok * 3 // 4
+    max_rows = ROW_SIZES[units][-1]
     lines = d_model // LANES
-    out = jax.ShapeDtypeStruct((num_tok // (1 + split) * lines, LANES), jnp.float32)
+    out = jax.ShapeDtypeStruct((num_tok // 2 * lines, LANES), jnp.float32)
     up_steps = ff_dim // FF_BLOCK
 
     def body(*refs):
-        expert_kernel(row0, ROW_SIZES[units], split, *refs)
+        expert_kernel(row0, ROW_SIZES[units], *refs)
 
     return pl.pallas_call(
         body,
-        out_shape=(out,) * (1 + split),
+        out_shape=(out, out),
         in_specs=[smem, smem, vmem, vmem, anym, anym, anym, anym],
-        out_specs=(anym,) * (1 + split),
+        out_specs=(anym, anym),
         scratch_shapes=[
             pltpu.VMEM((num_tok, d_model), jnp.bfloat16),
             pltpu.VMEM(((num_tok + 8) * lines, LANES), jnp.float32),
             pltpu.VMEM((up_steps, d_model, FF_BLOCK), jnp.bfloat16),
             pltpu.VMEM((up_steps, d_model, FF_BLOCK), jnp.bfloat16),
             pltpu.VMEM((ff_dim, d_model), jnp.bfloat16),
-            pltpu.VMEM((MAX_ROWS, num_tok), jnp.bfloat16),
-            pltpu.VMEM((MAX_ROWS, d_model), jnp.bfloat16),
-            pltpu.VMEM((MAX_ROWS, ff_dim), jnp.bfloat16),
-            pltpu.VMEM((MAX_ROWS * lines, LANES), jnp.float32),
-            pltpu.VMEM((8, MAX_ROWS), jnp.int32),
-            pltpu.SMEM((8, MAX_ROWS), jnp.int32),
+            pltpu.VMEM((max_rows, num_tok), jnp.bfloat16),
+            pltpu.VMEM((max_rows, d_model), jnp.bfloat16),
+            pltpu.VMEM((max_rows, ff_dim), jnp.bfloat16),
+            pltpu.VMEM((max_rows * lines, LANES), jnp.float32),
+            pltpu.VMEM((8, max_rows), jnp.int32),
+            pltpu.SMEM((8, max_rows), jnp.int32),
             pltpu.SemaphoreType.DMA((up_steps, 2)),
-            pltpu.SemaphoreType.DMA,
+            pltpu.SemaphoreType.DMA((2,)),
             pltpu.SemaphoreType.DMA((shards,)),
             pltpu.SemaphoreType.DMA,
             pltpu.SemaphoreType.DMA((shards // 2, 2)),
@@ -291,15 +291,16 @@
     chunks = len(CHUNK_UNITS)
     in_chunk = chunk_of[None, :] == jnp.arange(chunks)[:, None]
     count = jnp.sum(jnp.where(in_chunk[:, None, :], sums[None], 0.0), axis=2).astype(jnp.int32)
-    passes = (count + MAX_ROWS - 1) // MAX_ROWS
+    limit = jnp.array([ROW_SIZES[n][-1] for n in CHUNK_UNITS])[:, None]
+    passes = (count + limit - 1) // limit
     upto = jnp.arange(num_local)[:, None] <= jnp.arange(num_local)[None, :]
     ends = jnp.sum(jnp.where(upto, passes[:, :, None], 0), axis=1)
     starts = ends - passes
     item = jnp.arange(MAX_ITEMS)
     mine = (starts[:, :, None] <= item) & (item < ends[:, :, None])
     e = jnp.sum(jnp.where(mine, jnp.arange(num_local)[:, None], 0), axis=1)
-    p0 = jnp.sum(jnp.where(mine, (item - starts[:, :, None]) * MAX_ROWS, 0), axis=1)
-    rows = jnp.minimum(jnp.sum(jnp.where(mine, count[:, :, None], 0), axis=1) - p0, MAX_ROWS)
+    p0 = jnp.sum(jnp.where(mine, (item - starts[:, :, None]) * limit[:, :, None], 0), axis=1)
+    rows = jnp.minimum(jnp.sum(jnp.where(mine, count[:, :, None], 0), axis=1) - p0, limit)
     extra = jnp.where(item[None, :] == 0, ends[:, -1:], my_rank % 2)
     meta = jnp.concatenate([e, p0, rows, extra], axis=1).astype(jnp.int32)
     tables = []
@@ -332,9 +333,8 @@
         outs = []
         last = None
 
-        def reduce(part, c):
-            groups = same_core if c > 0 else None
-            part = lax.psum_scatter(part, 'ep', scatter_dimension=0, tiled=True, axis_index_groups=groups)
+        def reduce(part):
+            part = lax.psum_scatter(part, 'ep', scatter_dimension=0, tiled=True, axis_index_groups=same_core)
             return part.reshape(-1, tokens.shape[1]).astype(jnp.bfloat16)
 
         for c, units in enumerate(CHUNK_UNITS):
@@ -344,10 +344,10 @@
             meta, gate, pos = tables[c]
             if last is not None:
                 meta, last = lax.optimization_barrier((meta, last))
-                outs.append(reduce(last, c - 1))
-            last = expert_block(row0, units, c > 0, meta, gate, pos, digits, tok, w_gate, w_up, w_down)
-            last = pair_sum(*last, c) if c > 0 else last[0]
-        outs.append(reduce(last, len(CHUNK_UNITS) - 1))
+                outs.append(reduce(last))
+            last = expert_block(row0, units, meta, gate, pos, digits, tok, w_gate, w_up, w_down)
+            last = pair_sum(*last, c)
+        outs.append(reduce(last))
         return jnp.concatenate(outs, axis=0)
 
     return jax.shard_map(layer, mesh=mesh, in_specs=(row_spec, row_spec, row_spec, row_spec, expert_spec, expert_spec, expert_spec), out_specs=row_spec, check_vma=False)

time: 918 us -> 932 us (1.015)
    pallas_call x4 -> x5, Pallas kernels: 73.5 us -> 76 us  [pair_sum(): pl.pallas_call(pair_kernel, out_shape=jax.ShapeDtypeStruct((rows, d_model...]
where the time goes in v4:
time: 932 us; the launch traced here: 931 us
  Pallas kernels  546 us (59%)
  waiting for transfers between devices  309 us (33%)
  local copies, waits for them, and re-layouts  31.7 us (3%)
  blocking collectives  16.6 us (2%)
  between operations  13.9 us (1%)
  other arithmetic  12.4 us (1%)
    pallas_call x5, Pallas kernels, expert_block(): pl.pallas_call(body, out_shape=(out, out), in_specs=[smem, smem, vmem, vm...  470 us
    reduce_scatter x5, waiting for transfers between devices, reduce(): lax.psum_scatter(part, 'ep', scatter_dimension=0, tiled=True, axis_index_...  298 us
    pallas_call x5, Pallas kernels, pair_sum(): pl.pallas_call(pair_kernel, out_shape=jax.ShapeDtypeStruct((rows, d_model...  76 us
  transfers between devices with their start and end apart: 8, of which 4 were waited for; matrix products, arithmetic and copies ran while one was open for 3% of the time, Pallas kernels for 59%

profile of v4, /device:TPU:0, one launch (start us, length us, event | category | flops | bytes accessed | tf_op | source)
XLA Modules:
  0.0 930.7 jit_solution(17034703323210197063)
XLA Ops:
  6.5 2.0 slice.70
  8.6 2.5 slice.74
  11.2 3.9 slice.78
  15.2 16.6 %all-gather.4 = f32[8,12,1024]{2,1,0:T(8,128)S(1)} all-gather(f32[1,12,1024]{2,1,0:T(8,128)S(1)} %maximum_bitcast_fusion), channel_id=2, replica_groups=mesh['dp'=1,'ep'=8] {'ep'}, dimensions={0}, use_global_device_ids=true | all-gather | bytes 442368 | tf_op jit(solution)/shard_map/all_gather | solution.py:274
  33.2 0.7 copy-done
  33.9 0.6 fusion.13
  35.2 0.6 stack.6.refs_3_
  36.7 0.7 pad_add_fusion.6
  37.4 0.7 pad_add_fusion
  38.3 0.7 copy-done.2
  39.0 0.7 slice_bitcast_fusion.2
  39.6 9.3 all-gather.9.cloned.1.call-done
  48.9 79.8 %expert_block.5 = (f32[10240,128]{1,0:T(8,128)}, f32[10240,128]{1,0:T(8,128)}) custom-call(s32[256]{0:T(256)} %bitcast.53, f32[8320]{0:T(1024)} %pad.17.refs_1_, s32[8,1,1024]{2,1,0:T(1,128)} %get-tuple-element.47.refs_2_, bf16[8,1024]{1,0:T(8,128)(2,1)} %stack.6.refs_3_, bf16[8,128,2560]{2,1,0:T(8,128)(2,1)} %bitcast.41, bf16[8,2560,1536]{2,1,0:T(8,128)(2,1)} %refs_5_.9, ...), custom_call_target="tpu_custom_call" | custom-call | flops 36238786560 | bytes 204472320 | tf_op jit(solution)/shard_map/expert_block/pallas_call | solution.py:184
  128.7 10.1 %pair_sum.5 = f32[10240,128]{1,0:T(8,128)} custom-call(f32[10240,128]{1,0:T(8,128)} %get-tuple-element.23.keep, f32[10240,128]{1,0:T(8,128)} %get-tuple-element.24.send), custom_call_target="tpu_custom_call" | custom-call | flops 5242880000 | bytes 20971520 | tf_op jit(solution)/shard_map/pair_sum/pallas_call | solution.py:251
  138.9 0.9 copy-done.1
  139.8 0.7 fusion.15
  140.5 0.6 pad.18.refs_1_
  141.2 0.7 stack.7.refs_3_
  141.9 0.7 fusion.14
  142.6 104.3 %expert_block.6 = (f32[20480,128]{1,0:T(8,128)}, f32[20480,128]{1,0:T(8,128)}) custom-call(s32[256]{0:T(256)} %bitcast.56, f32[16512]{0:T(1024)} %pad.18.refs_1_, s32[8,1,2048]{2,1,0:T(1,128)} %bitcast.50, bf16[8,2048]{1,0:T(8,128)(2,1)} %stack.7.refs_3_, bf16[8,256,2560]{2,1,0:T(8,128)(2,1)} %bitcast.57, bf16[8,2560,1536]{2,1,0:T(8,128)(2,1)} %refs_5_.9, ...), custom_call_target="tpu_custom_call" | custom-call | flops 72477573120 | bytes 220200960 | tf_op jit(solution)/shard_map/expert_block/pallas_call | solution.py:184
  246.9 17.9 %pair_sum.6 = f32[20480,128]{1,0:T(8,128)} custom-call(f32[20480,128]{1,0:T(8,128)} %get-tuple-element.27.keep, f32[20480,128]{1,0:T(8,128)} %get-tuple-element.28.send), custom_call_target="tpu_custom_call" | custom-call | flops 10485760000 | bytes 41943040 | tf_op jit(solution)/shard_map/pair_sum/pallas_call | solution.py:251
  265.0 0.7 copy-done.5
  267.6 105.0 %expert_block.7 = (f32[20480,128]{1,0:T(8,128)}, f32[20480,128]{1,0:T(8,128)}) custom-call(s32[256]{0:T(256)} %bitcast.55, f32[16512]{0:T(1024)} %pad.19.refs_1_, s32[8,1,2048]{2,1,0:T(1,128)} %bitcast.49, bf16[8,2048]{1,0:T(8,128)(2,1)} %stack.7.refs_3_, bf16[8,640,2560]{2,1,0:T(8,128)(2,1)} %bitcast.38, bf16[8,2560,1536]{2,1,0:T(8,128)(2,1)} %refs_5_.9, ...), custom_call_target="tpu_custom_call" | custom-call | flops 72477573120 | bytes 220200960 | tf_op jit(solution)/shard_map/expert_block/pallas_call | solution.py:184
  372.6 17.9 %pair_sum.7 = f32[20480,128]{1,0:T(8,128)} custom-call(f32[20480,128]{1,0:T(8,128)} %get-tuple-element.31.keep, f32[20480,128]{1,0:T(8,128)} %get-tuple-element.32.send), custom_call_target="tpu_custom_call" | custom-call | flops 10485760000 | bytes 41943040 | tf_op jit(solution)/shard_map/pair_sum/pallas_call | solution.py:251
  390.5 102.9 %expert_block.8 = (f32[20480,128]{1,0:T(8,128)}, f32[20480,128]{1,0:T(8,128)}) custom-call(s32[256]{0:T(256)} %bitcast.54, f32[16512]{0:T(1024)} %pad.20.refs_1_, s32[8,1,2048]{2,1,0:T(1,128)} %bitcast.48, bf16[8,2048]{1,0:T(8,128)(2,1)} %stack.7.refs_3_, bf16[8,640,2560]{2,1,0:T(8,128)(2,1)} %bitcast.39, bf16[8,2560,1536]{2,1,0:T(8,128)(2,1)} %refs_5_.9, ...), custom_call_target="tpu_custom_call" | custom-call | flops 72477573120 | bytes 220200960 | tf_op jit(solution)/shard_map/expert_block/pallas_call | solution.py:184
  493.4 20.0 %pair_sum.8 = f32[20480,128]{1,0:T(8,128)} custom-call(f32[20480,128]{1,0:T(8,128)} %get-tuple-element.35.keep, f32[20480,128]{1,0:T(8,128)} %get-tuple-element.36.send), custom_call_target="tpu_custom_call" | custom-call | flops 10485760000 | bytes 41943040 | tf_op jit(solution)/shard_map/pair_sum/pallas_call | solution.py:251
  513.4 78.4 %expert_block.9 = (f32[10240,128]{1,0:T(8,128)}, f32[10240,128]{1,0:T(8,128)}) custom-call(s32[256]{0:T(256)} %bitcast.52, f32[8320]{0:T(1024)} %pad.21.refs_1_, s32[8,1,1024]{2,1,0:T(1,128)} %get-tuple-element.46.refs_2_, bf16[8,1024]{1,0:T(8,128)(2,1)} %stack.6.refs_3_, bf16[8,640,2560]{2,1,0:T(8,128)(2,1)} %bitcast.40, bf16[8,2560,1536]{2,1,0:T(8,128)(2,1)} %refs_5_.9, ...), custom_call_target="tpu_custom_call" | custom-call | flops 36238786560 | bytes 204472320 | tf_op jit(solution)/shard_map/expert_block/pallas_call | solution.py:184
  591.8 10.1 %pair_sum.9 = f32[10240,128]{1,0:T(8,128)} custom-call(f32[10240,128]{1,0:T(8,128)} %get-tuple-element.39.keep, f32[10240,128]{1,0:T(8,128)} %get-tuple-element.40.send), custom_call_target="tpu_custom_call" | custom-call | flops 5242880000 | bytes 20971520 | tf_op jit(solution)/shard_map/pair_sum/pallas_call | solution.py:251
  602.0 0.7 reduce-scatter.10.cloned.1.call-update
  602.7 0.7 reduce-scatter.12.cloned.1.call-update
  603.5 1.4 convert_element_type.78
  604.8 0.7 convert_element_type.79
  605.6 0.9 constant_dynamic-update-slice_fusion.4
  606.5 1.9 convert_element_type.80
  608.3 1.5 convert_element_type.81
  609.8 1.1 constant_dynamic-update-slice_fusion.3
  611.0 101.9 %reduce-scatter.14.cloned.1.call-done = f32[2560,128]{1,0:T(8,128)} async-done(((f32[10240,128]{1,0:T(8,128)}), f32[2560,128]{1,0:T(8,128)}) %reduce-scatter.14.cloned.1.call-update) | async-done | bytes 1310736 | tf_op jit(solution)/shard_map/reduce_scatter | solution.py:337
  712.9 1.4 convert_element_type.86
  714.2 0.7 convert_element_type.87
  715.0 98.9 %reduce-scatter.10.cloned.1.call-done = f32[5120,128]{1,0:T(8,128)} async-done(((f32[20480,128]{1,0:T(8,128)}), f32[5120,128]{1,0:T(8,128)}) %reduce-scatter.10.cloned.1.call-update) | async-done | bytes 2621456 | tf_op jit(solution)/shard_map/reduce_scatter | solution.py:337
  813.9 1.9 convert_element_type.82
  815.7 1.5 convert_element_type.83
  817.2 97.6 %reduce-scatter.12.cloned.1.call-done = f32[5120,128]{1,0:T(8,128)} async-done(((f32[20480,128]{1,0:T(8,128)}), f32[5120,128]{1,0:T(8,128)}) %reduce-scatter.12.cloned.1.call-update) | async-done | bytes 2621456 | tf_op jit(solution)/shard_map/reduce_scatter | solution.py:337
  914.8 2.9 convert_element_type.84
  917.7 2.9 convert_element_type.85
  920.7 1.1 constant_dynamic-update-slice_fusion.2
  921.8 1.1 constant_dynamic-update-slice_fusion.1
  922.9 0.9 constant_dynamic-update-slice_fusion
  (77 shorter events, 5.4 us)
Async XLA Ops:
  6.5 42.3 %all-gather.9.cloned.1.call-start = ((), (), s32[]{:S(2)}) async-start(), calls=%async_computation.10 | async-start | bytes 5898240 | tf_op jit(solution)/shard_map/all_gather | solution.py:329
  8.5 134.1 %all-gather.11.cloned.1.call-start = ((), (), s32[]{:S(2)}) async-start(), calls=%async_computation.11 | async-start | bytes 11796480 | tf_op jit(solution)/shard_map/all_gather | solution.py:329
  11.1 4.1 copy-start.7
  11.1 4.1 copy-start.8
  11.1 4.1 copy-start.9
  11.1 21.3 %copy-start.11 = (s32[8]{0:T(128)S(1)}, s32[8]{0:T(128)}, u32[]{:S(2)}) copy-start(s32[8]{0:T(128)} %constant.115.clone) | copy-start | bytes 100
  11.1 256.5 %all-gather.13.cloned.1.call-start = ((), (), s32[]{:S(2)}) async-start(), calls=%async_computation.12 | async-start | bytes 29491200 | tf_op jit(solution)/shard_map/all_gather | solution.py:329
  15.1 20.8 %copy-start.10 = (s32[5]{0:T(128)S(1)}, s32[5]{0:T(128)}, u32[]{:S(2)}) copy-start(s32[5]{0:T(128)} %constant.116.clone) | copy-start | bytes 64
  15.1 588.4 %reduce-scatter.6.cloned.1.call-start = ((), (), s32[]{:S(2)}) async-start(), calls=%async_computation.5 | async-start | bytes 6553600 | tf_op jit(solution)/shard_map/reduce_scatter | solution.py:337
  33.2 0.7 copy-start
  38.2 0.7 copy-start.2
  138.8 1.0 copy-start.1
  138.8 3.0 copy-start.3
  138.9 467.6 %reduce-scatter.8.cloned.1.call-start = ((), (), s32[]{:S(2)}) async-start(), calls=%async_computation.6 | async-start | bytes 13107200 | tf_op jit(solution)/shard_map/reduce_scatter | solution.py:337
  264.8 0.8 copy-start.5
  264.9 1.5 copy-start.4
  264.9 2.1 copy-start.6
  264.9 448.0 %reduce-scatter.14.cloned.1.call-start = ((), (), s32[]{:S(2)}) async-start(), calls=%async_computation.9 | async-start | bytes 6553600 | tf_op jit(solution)/shard_map/reduce_scatter | solution.py:337
  601.9 211.9 %reduce-scatter.10.cloned.1.call-start = ((), (), s32[]{:S(2)}) async-start(), calls=%async_computation.7 | async-start | bytes 13107200 | tf_op jit(solution)/shard_map/reduce_scatter | solution.py:337
  602.7 312.1 %reduce-scatter.12.cloned.1.call-start = ((), (), s32[]{:S(2)}) async-start(), calls=%async_computation.8 | async-start | bytes 13107200 | tf_op jit(solution)/shard_map/reduce_scatter | solution.py:337
Sparse Core Ops, SparseCore 0:
  9.1 39.6 all-gather.8
  50.7 57.6 all-gather.10
  110.3 124.1 all-gather.12
  237.3 55.6 reduce-scatter.5
  295.9 97.8 reduce-scatter.7
  602.1 110.7 reduce-scatter.13
  715.9 97.9 reduce-scatter.9
  816.9 97.8 reduce-scatter.11

commit v5 on v4

--- a/solution.py
+++ b/solution.py
@@ -5,10 +5,10 @@
 from jax.experimental.pallas import tpu as pltpu
 from jax.sharding import PartitionSpec as P
 
-UNIT = 128
-CHUNK_UNITS = (1, 2, 2, 2, 1)
+UNIT = 64
+CHUNK_UNITS = (3, 4, 4, 3, 2)
 GATHERS = ((0,), (1,), (2, 3, 4))
-ROW_SIZES = {1: (160,), 2: (128, 256, 288, 320)}
+ROW_SIZES = {2: (160,), 3: (192, 224), 4: (128, 256, 288, 320)}
 MAX_ITEMS = 64
 FF_BLOCK = 512
 FF_PART = 256
@@ -41,8 +41,8 @@
                                       down_sem.at[k]) for k in range(2)]
 
     def start_all(copies):
-        for k, cp in enumerate(copies):
-            cp.start(priority=k % 2)
+        for cp in copies:
+            cp.start()
 
     tok_copies = [pltpu.make_async_copy(tok_hbm.at[s, pl.ds(row0, tc), :], tok.at[pl.ds(s * tc, tc), :], tok_sem.at[s])
                   for s in range(shards)]

time: 932 us -> 927 us (level)
  waiting for transfers between devices: 309 us -> 287 us
    reduce_scatter x5, waiting for transfers between devices: 298 us -> 268 us  [reduce(): lax.psum_scatter(part, 'ep', scatter_dimension=0, tiled=True, axis_index_...]
  transfers between devices with their start and end apart: 8 -> 8, of which waited for: 4 -> 4; matrix products, arithmetic and copies ran while one was open for 3% -> 4% of each run, Pallas kernels for 59% -> 60%
where the time goes in v5:
time: 927 us; the launch traced here: 926 us
  Pallas kernels  555 us (60%)
  waiting for transfers between devices  287 us (31%)
  local copies, waits for them, and re-layouts  39.3 us (4%)
  blocking collectives  18.6 us (2%)
  between operations  13.9 us (1%)
  other arithmetic  12.1 us (1%)
    pallas_call x5, Pallas kernels, expert_block(): pl.pallas_call(body, out_shape=(out, out), in_specs=[smem, smem, vmem, vm...  477 us
    reduce_scatter x5, waiting for transfers between devices, reduce(): lax.psum_scatter(part, 'ep', scatter_dimension=0, tiled=True, axis_index_...  268 us
    pallas_call x5, Pallas kernels, pair_sum(): pl.pallas_call(pair_kernel, out_shape=jax.ShapeDtypeStruct((rows, d_model...  77.2 us
    all_gather x1, blocking collectives, routing_tables(): packed = lax.all_gather(jnp.concatenate([key, gate_wts.T], axis=0), 'ep')  18.6 us
  transfers between devices with their start and end apart: 8, of which 4 were waited for; matrix products, arithmetic and copies ran while one was open for 4% of the time, Pallas kernels for 60%

profile of v5, /device:TPU:0, one launch (start us, length us, event | category | flops | bytes accessed | tf_op | source)
XLA Modules:
  0.0 926.0 jit_solution(387059372771372603)
XLA Ops:
  6.5 2.2 slice.70
  8.8 2.4 slice.74
  11.3 3.6 slice.78
  15.2 18.6 %all-gather.4 = f32[8,12,1024]{2,1,0:T(8,128)S(1)} all-gather(f32[1,12,1024]{2,1,0:T(8,128)S(1)} %maximum_bitcast_fusion), channel_id=2, replica_groups=mesh['dp'=1,'ep'=8] {'ep'}, dimensions={0}, use_global_device_ids=true | all-gather | bytes 442368 | tf_op jit(solution)/shard_map/all_gather | solution.py:274
  36.1 0.8 copy-done
  36.9 0.7 fusion.16
  38.0 0.8 copy-done.2
  38.7 0.7 fusion.15
  39.5 0.7 reshape.380.refs_2_
  43.7 17.9 %all-gather.9.cloned.1.call-done = bf16[1536,2560]{1,0:T(8,128)(2,1)} async-done(((bf16[192,2560]{1,0:T(8,128)(2,1)}), bf16[1536,2560]{1,0:T(8,128)(2,1)}) %all-gather.9.cloned.1.call-update) | async-done | bytes 7864336 | tf_op jit(solution)/shard_map/all_gather | solution.py:329
  61.7 95.4 %expert_block.5 = (f32[15360,128]{1,0:T(8,128)}, f32[15360,128]{1,0:T(8,128)}) custom-call(s32[256]{0:T(256)} %bitcast.35, f32[12416]{0:T(1024)} %pad.18.refs_1_, s32[8,1,1536]{2,1,0:T(1,128)} %reshape.380.refs_2_, bf16[8,1536]{1,0:T(8,128)(2,1)} %stack.11.refs_3_, bf16[8,192,2560]{2,1,0:T(8,128)(2,1)} %bitcast.37, bf16[8,2560,1536]{2,1,0:T(8,128)(2,1)} %refs_5_.9, ...), custom_call_target="tpu_custom_call" | custom-call | flops 54358179840 | bytes 212336640 | tf_op jit(solution)/shard_map/expert_block/pallas_call | solution.py:184
  157.1 15.6 %pair_sum.5 = f32[15360,128]{1,0:T(8,128)} custom-call(f32[15360,128]{1,0:T(8,128)} %get-tuple-element.23.keep, f32[15360,128]{1,0:T(8,128)} %get-tuple-element.24.send), custom_call_target="tpu_custom_call" | custom-call | flops 7864320000 | bytes 31457280 | tf_op jit(solution)/shard_map/pair_sum/pallas_call | solution.py:251
  172.8 0.9 copy-done.1
  173.7 0.7 fusion.18
  175.2 0.7 fusion.17
  175.9 0.8 reshape.364.refs_2_
  177.4 105.6 %expert_block.6 = (f32[20480,128]{1,0:T(8,128)}, f32[20480,128]{1,0:T(8,128)}) custom-call(s32[256]{0:T(256)} %bitcast.34, f32[16512]{0:T(1024)} %pad.19.refs_1_, s32[8,1,2048]{2,1,0:T(1,128)} %reshape.364.refs_2_, bf16[8,2048]{1,0:T(8,128)(2,1)} %stack.12.refs_3_, bf16[8,256,2560]{2,1,0:T(8,128)(2,1)} %bitcast.36, bf16[8,2560,1536]{2,1,0:T(8,128)(2,1)} %refs_5_.9, ...), custom_call_target="tpu_custom_call" | custom-call | flops 72477573120 | bytes 220200960 | tf_op jit(solution)/shard_map/expert_block/pallas_call | solution.py:184
  282.9 18.0 %pair_sum.6 = f32[20480,128]{1,0:T(8,128)} custom-call(f32[20480,128]{1,0:T(8,128)} %get-tuple-element.27.keep, f32[20480,128]{1,0:T(8,128)} %get-tuple-element.28.send), custom_call_target="tpu_custom_call" | custom-call | flops 10485760000 | bytes 41943040 | tf_op jit(solution)/shard_map/pair_sum/pallas_call | solution.py:251
  301.0 1.1 slice.94
  302.1 1.0 slice.95
  305.3 0.7 reshape.370.refs_2_
  306.0 0.7 reshape.381.refs_2_
  306.8 0.7 reshape.366.refs_2_
  308.2 103.2 %expert_block.7 = (f32[20480,128]{1,0:T(8,128)}, f32[20480,128]{1,0:T(8,128)}) custom-call(s32[256]{0:T(256)} %bitcast.33, f32[16512]{0:T(1024)} %pad.20.refs_1_, s32[8,1,2048]{2,1,0:T(1,128)} %reshape.366.refs_2_, bf16[8,2048]{1,0:T(8,128)(2,1)} %stack.12.refs_3_, bf16[8,576,2560]{2,1,0:T(8,128)(2,1)} %bitcast.26, bf16[8,2560,1536]{2,1,0:T(8,128)(2,1)} %refs_5_.9, ...), custom_call_target="tpu_custom_call" | custom-call | flops 72477573120 | bytes 220200960 | tf_op jit(solution)/shard_map/expert_block/pallas_call | solution.py:184
  411.4 18.4 %pair_sum.7 = f32[20480,128]{1,0:T(8,128)} custom-call(f32[20480,128]{1,0:T(8,128)} %get-tuple-element.31.keep, f32[20480,128]{1,0:T(8,128)} %get-tuple-element.32.send), custom_call_target="tpu_custom_call" | custom-call | flops 10485760000 | bytes 41943040 | tf_op jit(solution)/shard_map/pair_sum/pallas_call | solution.py:251
  429.8 94.9 %expert_block.8 = (f32[15360,128]{1,0:T(8,128)}, f32[15360,128]{1,0:T(8,128)}) custom-call(s32[256]{0:T(256)} %bitcast.32, f32[12416]{0:T(1024)} %pad.21.refs_1_, s32[8,1,1536]{2,1,0:T(1,128)} %reshape.381.refs_2_, bf16[8,1536]{1,0:T(8,128)(2,1)} %stack.11.refs_3_, bf16[8,576,2560]{2,1,0:T(8,128)(2,1)} %bitcast.27, bf16[8,2560,1536]{2,1,0:T(8,128)(2,1)} %refs_5_.9, ...), custom_call_target="tpu_custom_call" | custom-call | flops 54358179840 | bytes 212336640 | tf_op jit(solution)/shard_map/expert_block/pallas_call | solution.py:184
  524.7 15.2 %pair_sum.8 = f32[15360,128]{1,0:T(8,128)} custom-call(f32[15360,128]{1,0:T(8,128)} %get-tuple-element.35.keep, f32[15360,128]{1,0:T(8,128)} %get-tuple-element.36.send), custom_call_target="tpu_custom_call" | custom-call | flops 7864320000 | bytes 31457280 | tf_op jit(solution)/shard_map/pair_sum/pallas_call | solution.py:251
  539.9 78.2 %expert_block.9 = (f32[10240,128]{1,0:T(8,128)}, f32[10240,128]{1,0:T(8,128)}) custom-call(s32[256]{0:T(256)} %bitcast.31, f32[8320]{0:T(1024)} %pad.22.refs_1_, s32[8,1,1024]{2,1,0:T(1,128)} %reshape.370.refs_2_, bf16[8,1024]{1,0:T(8,128)(2,1)} %stack.14.refs_3_, bf16[8,576,2560]{2,1,0:T(8,128)(2,1)} %bitcast.28, bf16[8,2560,1536]{2,1,0:T(8,128)(2,1)} %refs_5_.9, ...), custom_call_target="tpu_custom_call" | custom-call | flops 36238786560 | bytes 204472320 | tf_op jit(solution)/shard_map/expert_block/pallas_call | solution.py:184
  618.2 10.1 %pair_sum.9 = f32[10240,128]{1,0:T(8,128)} custom-call(f32[10240,128]{1,0:T(8,128)} %get-tuple-element.39.keep, f32[10240,128]{1,0:T(8,128)} %get-tuple-element.40.send), custom_call_target="tpu_custom_call" | custom-call | flops 5242880000 | bytes 20971520 | tf_op jit(solution)/shard_map/pair_sum/pallas_call | solution.py:251
  628.3 0.7 reduce-scatter.12.cloned.1.call-update
  629.8 1.6 convert_element_type.79
  631.5 1.1 convert_element_type.80
  632.6 1.0 constant_dynamic-update-slice_fusion.4
  633.6 1.9 convert_element_type.81
  635.4 1.5 convert_element_type.82
  636.9 1.1 constant_dynamic-update-slice_fusion.3
  638.1 92.0 %reduce-scatter.14.cloned.1.call-done = f32[2560,128]{1,0:T(8,128)} async-done(((f32[10240,128]{1,0:T(8,128)}), f32[2560,128]{1,0:T(8,128)}) %reduce-scatter.14.cloned.1.call-update) | async-done | bytes 1310736 | tf_op jit(solution)/shard_map/reduce_scatter | solution.py:337
  730.1 1.4 convert_element_type.87
  731.5 0.7 convert_element_type.88
  732.2 78.4 %reduce-scatter.12.cloned.1.call-done = f32[3840,128]{1,0:T(8,128)} async-done(((f32[15360,128]{1,0:T(8,128)}), f32[3840,128]{1,0:T(8,128)}) %reduce-scatter.12.cloned.1.call-update) | async-done | bytes 1966096 | tf_op jit(solution)/shard_map/reduce_scatter | solution.py:337
  810.5 1.6 convert_element_type.85
  812.2 2.1 convert_element_type.86
  814.3 97.3 %reduce-scatter.10.cloned.1.call-done = f32[5120,128]{1,0:T(8,128)} async-done(((f32[20480,128]{1,0:T(8,128)}), f32[5120,128]{1,0:T(8,128)}) %reduce-scatter.10.cloned.1.call-update) | async-done | bytes 2621456 | tf_op jit(solution)/shard_map/reduce_scatter | solution.py:337
  911.5 1.9 convert_element_type.83
  913.4 1.5 convert_element_type.84
  914.9 1.1 constant_dynamic-update-slice_fusion.2
  916.1 2.2 constant_dynamic-update-slice_fusion.1
  918.3 0.9 constant_dynamic-update-slice_fusion
  (96 shorter events, 11.7 us)
Async XLA Ops:
  6.5 55.1 %all-gather.9.cloned.1.call-start = ((), (), s32[]{:S(2)}) async-start(), calls=%async_computation.10 | async-start | bytes 8847360 | tf_op jit(solution)/shard_map/all_gather | solution.py:329
  8.8 168.6 %all-gather.11.cloned.1.call-start = ((), (), s32[]{:S(2)}) async-start(), calls=%async_computation.11 | async-start | bytes 11796480 | tf_op jit(solution)/shard_map/all_gather | solution.py:329
  11.2 3.8 copy-start.12
  11.2 3.9 copy-start.8
  11.2 3.9 copy-start.9
  11.2 3.9 copy-start.10
  11.3 296.9 %all-gather.13.cloned.1.call-start = ((), (), s32[]{:S(2)}) async-start(), calls=%async_computation.12 | async-start | bytes 26542080 | tf_op jit(solution)/shard_map/all_gather | solution.py:329
  15.0 26.6 %copy-start.11 = (s32[5]{0:T(128)S(1)}, s32[5]{0:T(128)}, u32[]{:S(2)}) copy-start(s32[5]{0:T(128)} %constant.134.clone) | copy-start | bytes 64
  15.0 614.8 %reduce-scatter.6.cloned.1.call-start = ((), (), s32[]{:S(2)}) async-start(), calls=%async_computation.5 | async-start | bytes 9830400 | tf_op jit(solution)/shard_map/reduce_scatter | solution.py:337
  36.1 0.8 copy-start
  37.9 0.8 copy-start.2
  172.7 1.0 copy-start.1
  172.7 2.5 copy-start.3
  172.7 460.9 %reduce-scatter.8.cloned.1.call-start = ((), (), s32[]{:S(2)}) async-start(), calls=%async_computation.6 | async-start | bytes 13107200 | tf_op jit(solution)/shard_map/reduce_scatter | solution.py:337
  300.9 2.9 copy-start.5
  300.9 3.0 copy-start.7
  300.9 5.1 copy-start.4
  300.9 5.8 copy-start.6
  301.0 429.1 %reduce-scatter.14.cloned.1.call-start = ((), (), s32[]{:S(2)}) async-start(), calls=%async_computation.9 | async-start | bytes 6553600 | tf_op jit(solution)/shard_map/reduce_scatter | solution.py:337
  628.3 182.3 %reduce-scatter.12.cloned.1.call-start = ((), (), s32[]{:S(2)}) async-start(), calls=%async_computation.8 | async-start | bytes 9830400 | tf_op jit(solution)/shard_map/reduce_scatter | solution.py:337
  629.0 282.5 %reduce-scatter.10.cloned.1.call-start = ((), (), s32[]{:S(2)}) async-start(), calls=%async_computation.7 | async-start | bytes 13107200 | tf_op jit(solution)/shard_map/reduce_scatter | solution.py:337
Sparse Core Ops, SparseCore 0:
  9.1 52.4 all-gather.8
  63.5 57.5 all-gather.10
  122.9 113.2 all-gather.12
  238.9 77.5 reduce-scatter.5
  319.5 101.0 reduce-scatter.7
  628.4 101.6 reduce-scatter.13
  733.0 77.5 reduce-scatter.11
  813.6 97.9 reduce-scatter.9

commit v6 on v4

--- a/solution.py
+++ b/solution.py
@@ -15,6 +15,7 @@
 OUT_BLOCK = 512
 LANES = 128
 ID_RADIX = 64
+WINDOW = 10
 PIECES = 8
 
 
@@ -41,8 +42,8 @@
                                       down_sem.at[k]) for k in range(2)]
 
     def start_all(copies):
-        for k, cp in enumerate(copies):
-            cp.start(priority=k % 2)
+        for cp in copies:
+            cp.start()
 
     tok_copies = [pltpu.make_async_copy(tok_hbm.at[s, pl.ds(row0, tc), :], tok.at[pl.ds(s * tc, tc), :], tok_sem.at[s])
                   for s in range(shards)]
@@ -62,27 +63,42 @@
     for cp in tok_copies:
         cp.wait()
 
-    def process(m, item, e, p0):
+    max_rows = row_sizes[-1]
+    blocks = num_tok // UNIT
+
+    def block_of(e, p):
+        found = -1
+        for k in range(blocks):
+            found = found + jnp.where(meta[4 * MAX_ITEMS + e * blocks + k] <= p, 1, 0)
+        return found
+
+    def dispatch(rows, e, row0, p0, half, first, width):
+        start = pl.multiple_of(first * UNIT, UNIT)
+
         def select(i, c):
-            row = pl.multiple_of(i * 32, 32)
-            want = lax.broadcasted_iota(jnp.int32, (32, num_tok), 0) + (p0 + row)
-            onehot[pl.ds(row, 32), :] = jnp.where(want == pos[e], 1.0, 0.0).astype(jnp.bfloat16)
-            return c
-
-        lax.fori_loop(0, m // 32, select, 0)
-        parts = lax.dot_general(digits[...], onehot[:m, :], (((1,), (1,)), ((), ())), preferred_element_type=jnp.float32)
-        idx = parts[0:1] * ID_RADIX + parts[1:2] + (1.0 - parts[2:3]) * num_tok
-        idx_v[:, :m] = jnp.broadcast_to(idx.astype(jnp.int32), (8, m))
-        idx_copy = pltpu.make_async_copy(idx_v, idx_s, idx_sem)
-        idx_copy.start()
-
-        def dispatch(nb, c):
+            row = pl.multiple_of(i * 16, 16)
+            want = lax.broadcasted_iota(jnp.int32, (16, width), 0) + (p0 + row)
+            here = pos[e, :, pl.ds(start, width)]
+            onehot[pl.ds(row, 16), :width] = jnp.where(want == here, 1.0, 0.0).astype(jnp.bfloat16)
+            return c
+
+        lax.fori_loop(0, rows // 16, select, 0)
+        parts = lax.dot_general(digits[:, :width], onehot[:rows, :width], (((1,), (1,)), ((), ())), preferred_element_type=jnp.float32)
+        here = parts[0:1] * ID_RADIX + parts[1:2] + (parts[2:3] * start.astype(jnp.float32) + (1.0 - parts[2:3]) * num_tok)
+        idx_v[pl.ds(pl.multiple_of(half * 8, 8), 8), :rows] = jnp.broadcast_to(here.astype(jnp.int32), (8, rows))
+
+        def columns(nb, c):
             cols = pl.ds(pl.multiple_of(nb * OUT_BLOCK, OUT_BLOCK), OUT_BLOCK)
-            x[:m, cols] = jnp.dot(onehot[:m, :], tok[:, cols], preferred_element_type=jnp.float32).astype(jnp.bfloat16)
-            return c
-
-        lax.fori_loop(0, d_model // OUT_BLOCK, dispatch, 0)
-
+            x[pl.ds(pl.multiple_of(row0, 16), rows), cols] = jnp.dot(
+                onehot[:rows, :width], tok[pl.ds(start, width), cols], preferred_element_type=jnp.float32).astype(jnp.bfloat16)
+            return c
+
+        lax.fori_loop(0, d_model // OUT_BLOCK, columns, 0)
+
+    idx_copy = pltpu.make_async_copy(idx_v, idx_s, idx_sem)
+    zero_block = jnp.int32(0)
+
+    def process(m, item):
         def up(j, c):
             for cp in up_copies(item, j):
                 cp.wait()
@@ -120,15 +136,15 @@
         def _():
             start_all(down_copies(item + 1))
 
-        idx_copy.wait()
-
-    def scatter(e, rows):
+    def scatter(e, rows, half_rows):
         spans = [(at, min(8, lines - at)) for at in range(0, lines, 8)]
 
         def eight(i, c):
             base = i * 8
+            upper = jnp.where(base >= half_rows, 1, 0)
+            at0 = base - upper * half_rows
             for half in range(2):
-                t = [idx_s[0, base + half * 4 + k] for k in range(4)]
+                t = [idx_s[upper * 8, at0 + half * 4 + k] for k in range(4)]
                 g = [gate[e * num_tok + t[k]] for k in range(4)]
                 new = [[acc[pl.ds(t[k] * lines + at, n), :] + o[pl.ds((base + half * 4 + k) * lines + at, n), :] * g[k]
                         for at, n in spans] for k in range(4)]
@@ -141,14 +157,51 @@
 
     def item_body(item, c):
         e, p0, rows = meta[item], meta[MAX_ITEMS + item], meta[2 * MAX_ITEMS + item]
+        half_rows = max_rows
+        windowed = False
+        starts = (zero_block, zero_block)
         low = 0
+        if blocks > WINDOW:
+            for m in row_sizes[1:]:
+                half_rows = jnp.where(rows <= m, jnp.minimum(half_rows, m // 2), half_rows)
+            fits = rows > row_sizes[0]
+            starts = []
+            for half in range(2):
+                begin = p0 + half * half_rows
+                end = jnp.minimum(begin + half_rows, p0 + rows) - 1
+                first = jnp.minimum(block_of(e, begin), blocks - WINDOW)
+                fits = fits & (block_of(e, end) < first + WINDOW)
+                starts.append(first)
+            windowed = fits
+            half_rows = jnp.where(fits, half_rows, max_rows)
+            for m in row_sizes[1:]:
+                @pl.when(windowed & (half_rows == m // 2))
+                def _():
+                    def half_step(half, c):
+                        first = jnp.where(half == 0, starts[0], starts[1])
+                        dispatch(m // 2, e, half * (m // 2), p0 + half * (m // 2), half, first, WINDOW * UNIT)
+                        return c
+
+                    lax.fori_loop(0, 2, half_step, 0)
+
+            @pl.when(rows <= row_sizes[0])
+            def _():
+                dispatch(row_sizes[0], e, 0, p0, 0, zero_block, num_tok)
+
+            @pl.when((rows > row_sizes[0]) & jnp.logical_not(windowed))
+            def _():
+                dispatch(max_rows, e, 0, p0, 0, zero_block, num_tok)
+        else:
+            dispatch(max_rows, e, 0, p0, 0, zero_block, num_tok)
+        idx_copy.start()
         for m in row_sizes:
             @pl.when((rows > low) & (rows <= m))
             def _():
-                process(m, item, e, p0)
+                process(m, item)
 
             low = m
-        scatter(e, rows)
+        idx_copy.wait()
+        scatter(e, rows, half_rows)
         return c
 
     lax.fori_loop(0, num_items, item_body, 0)
@@ -196,8 +249,8 @@
             pltpu.VMEM((max_rows, d_model), jnp.bfloat16),
             pltpu.VMEM((max_rows, ff_dim), jnp.bfloat16),
             pltpu.VMEM((max_rows * lines, LANES), jnp.float32),
-            pltpu.VMEM((8, max_rows), jnp.int32),
-            pltpu.SMEM((8, max_rows), jnp.int32),
+            pltpu.VMEM((16, max_rows), jnp.int32),
+            pltpu.SMEM((16, max_rows), jnp.int32),
             pltpu.SemaphoreType.DMA((up_steps, 2)),
             pltpu.SemaphoreType.DMA((2,)),
             pltpu.SemaphoreType.DMA((shards,)),
@@ -309,7 +362,8 @@
         span = slice(unit0, unit0 + n)
         num_tok = group_size * n * UNIT
         flat_gate = jnp.pad(gate[:, :, span].reshape(num_local * num_tok), (0, 128))
-        tables.append((meta[c], flat_gate, pos[:, :, span].reshape(num_local, 1, num_tok)))
+        base = outer[:, :, span, 0].reshape(num_local * group_size * n).astype(jnp.int32)
+        tables.append((jnp.concatenate([meta[c], base]), flat_gate, pos[:, :, span].reshape(num_local, 1, num_tok)))
         unit0 += n
     return tables
 

time: 932 us -> 943 us (1.012)
  Pallas kernels: 546 us -> 556 us
    pallas_call x5, Pallas kernels: 470 us -> 480 us  [expert_block(): pl.pallas_call(body, out_shape=(out, out), in_specs=[smem, smem, vmem, vm...]
  transfers between devices with their start and end apart: 8 -> 8, of which waited for: 4 -> 4; matrix products, arithmetic and copies ran while one was open for 3% -> 4% of each run, Pallas kernels for 59% -> 59%
where the time goes in v6:
time: 943 us; the launch traced here: 942 us
  Pallas kernels  556 us (59%)
  waiting for transfers between devices  306 us (32%)
  local copies, waits for them, and re-layouts  32.1 us (3%)
  blocking collectives  16.6 us (2%)
  other arithmetic  16.4 us (2%)
  between operations  14 us (1%)
    pallas_call x5, Pallas kernels, expert_block(): pl.pallas_call(body, out_shape=(out, out), in_specs=[smem, smem, vmem, vm...  480 us
    reduce_scatter x5, waiting for transfers between devices, reduce(): lax.psum_scatter(part, 'ep', scatter_dimension=0, tiled=True, axis_index_...  298 us
    pallas_call x5, Pallas kernels, pair_sum(): pl.pallas_call(pair_kernel, out_shape=jax.ShapeDtypeStruct((rows, d_model...  75.6 us
  transfers between devices with their start and end apart: 8, of which 4 were waited for; matrix products, arithmetic and copies ran while one was open for 4% of the time, Pallas kernels for 59%

profile of v6, /device:TPU:0, one launch (start us, length us, event | category | flops | bytes accessed | tf_op | source)
XLA Modules:
  0.0 941.8 jit_solution(2760529152106674136)
XLA Ops:
  6.5 2.0 slice.87
  8.6 2.5 slice.92
  11.2 3.9 slice.97
  15.2 16.6 %all-gather.4 = f32[8,12,1024]{2,1,0:T(8,128)S(1)} all-gather(f32[1,12,1024]{2,1,0:T(8,128)S(1)} %maximum_bitcast_fusion), channel_id=2, replica_groups=mesh['dp'=1,'ep'=8] {'ep'}, dimensions={0}, use_global_device_ids=true | all-gather | bytes 442368 | tf_op jit(solution)/shard_map/all_gather | solution.py:327
  32.9 0.7 slice_convert_fusion.1
  33.9 0.9 fusion.5
  35.1 0.7 copy-done
  35.8 0.6 fusion.15
  37.1 0.6 stack.6.refs_3_
  39.2 0.7 pad_add_fusion.5
  40.7 0.7 copy-done.2
  41.4 0.7 slice_bitcast_fusion.2
  42.1 6.8 all-gather.9.cloned.1.call-done
  48.9 80.7 %expert_block.5 = (f32[10240,128]{1,0:T(8,128)}, f32[10240,128]{1,0:T(8,128)}) custom-call(s32[320]{0:T(512)} %pad_add_fusion.1.refs_0_, f32[8320]{0:T(1024)} %pad.17.refs_1_, s32[8,1,1024]{2,1,0:T(1,128)} %get-tuple-element.49.refs_2_, bf16[8,1024]{1,0:T(8,128)(2,1)} %stack.6.refs_3_, bf16[8,128,2560]{2,1,0:T(8,128)(2,1)} %bitcast.53, ...), custom_call_target="tpu_custom_call" | custom-call | flops 36238786560 | bytes 204472320 | tf_op jit(solution)/shard_map/expert_block/pallas_call | solution.py:237
  129.5 10.1 %pair_sum.5 = f32[10240,128]{1,0:T(8,128)} custom-call(f32[10240,128]{1,0:T(8,128)} %get-tuple-element.23.keep, f32[10240,128]{1,0:T(8,128)} %get-tuple-element.24.send), custom_call_target="tpu_custom_call" | custom-call | flops 5242880000 | bytes 20971520 | tf_op jit(solution)/shard_map/pair_sum/pallas_call | solution.py:304
  139.9 0.7 copy-done.1
  140.6 0.7 fusion.17
  142.0 0.7 stack.7.refs_3_
  143.3 0.7 fusion.16
  144.0 107.1 %expert_block.6 = (f32[20480,128]{1,0:T(8,128)}, f32[20480,128]{1,0:T(8,128)}) custom-call(s32[384]{0:T(512)} %pad_add_fusion.refs_0_, f32[16512]{0:T(1024)} %pad.18.refs_1_, s32[8,1,2048]{2,1,0:T(1,128)} %bitcast.62, bf16[8,2048]{1,0:T(8,128)(2,1)} %stack.7.refs_3_, bf16[8,256,2560]{2,1,0:T(8,128)(2,1)} %bitcast.69, bf16[8,2560,1536]{2,1,0:T(8,128)(2,1)} %refs_5_.9, ...), custom_call_target="tpu_custom_call" | custom-call | flops 72477573120 | bytes 220200960 | tf_op jit(solution)/shard_map/expert_block/pallas_call | solution.py:237
  251.1 17.9 %pair_sum.6 = f32[20480,128]{1,0:T(8,128)} custom-call(f32[20480,128]{1,0:T(8,128)} %get-tuple-element.27.keep, f32[20480,128]{1,0:T(8,128)} %get-tuple-element.28.send), custom_call_target="tpu_custom_call" | custom-call | flops 10485760000 | bytes 41943040 | tf_op jit(solution)/shard_map/pair_sum/pallas_call | solution.py:304
  269.9 0.6 pad.19.refs_1_
  273.1 107.5 %expert_block.7 = (f32[20480,128]{1,0:T(8,128)}, f32[20480,128]{1,0:T(8,128)}) custom-call(s32[384]{0:T(512)} %pad_add_fusion.2.refs_0_, f32[16512]{0:T(1024)} %pad.19.refs_1_, s32[8,1,2048]{2,1,0:T(1,128)} %bitcast.61, bf16[8,2048]{1,0:T(8,128)(2,1)} %stack.7.refs_3_, bf16[8,640,2560]{2,1,0:T(8,128)(2,1)} %bitcast.50, bf16[8,2560,1536]{2,1,0:T(8,128)(2,1)} %refs_5_.9, ...), custom_call_target="tpu_custom_call" | custom-call | flops 72477573120 | bytes 220200960 | tf_op jit(solution)/shard_map/expert_block/pallas_call | solution.py:237
  380.6 17.9 %pair_sum.7 = f32[20480,128]{1,0:T(8,128)} custom-call(f32[20480,128]{1,0:T(8,128)} %get-tuple-element.31.keep, f32[20480,128]{1,0:T(8,128)} %get-tuple-element.32.send), custom_call_target="tpu_custom_call" | custom-call | flops 10485760000 | bytes 41943040 | tf_op jit(solution)/shard_map/pair_sum/pallas_call | solution.py:304
  398.5 105.9 %expert_block.8 = (f32[20480,128]{1,0:T(8,128)}, f32[20480,128]{1,0:T(8,128)}) custom-call(s32[384]{0:T(512)} %pad_add_fusion.3.refs_0_, f32[16512]{0:T(1024)} %pad.20.refs_1_, s32[8,1,2048]{2,1,0:T(1,128)} %bitcast.60, bf16[8,2048]{1,0:T(8,128)(2,1)} %stack.7.refs_3_, bf16[8,640,2560]{2,1,0:T(8,128)(2,1)} %bitcast.51, bf16[8,2560,1536]{2,1,0:T(8,128)(2,1)} %refs_5_.9, ...), custom_call_target="tpu_custom_call" | custom-call | flops 72477573120 | bytes 220200960 | tf_op jit(solution)/shard_map/expert_block/pallas_call | solution.py:237
  504.3 19.6 %pair_sum.8 = f32[20480,128]{1,0:T(8,128)} custom-call(f32[20480,128]{1,0:T(8,128)} %get-tuple-element.35.keep, f32[20480,128]{1,0:T(8,128)} %get-tuple-element.36.send), custom_call_target="tpu_custom_call" | custom-call | flops 10485760000 | bytes 41943040 | tf_op jit(solution)/shard_map/pair_sum/pallas_call | solution.py:304
  524.0 79.3 %expert_block.9 = (f32[10240,128]{1,0:T(8,128)}, f32[10240,128]{1,0:T(8,128)}) custom-call(s32[320]{0:T(512)} %pad_add_fusion.4.refs_0_, f32[8320]{0:T(1024)} %pad.21.refs_1_, s32[8,1,1024]{2,1,0:T(1,128)} %get-tuple-element.48.refs_2_, bf16[8,1024]{1,0:T(8,128)(2,1)} %stack.6.refs_3_, bf16[8,640,2560]{2,1,0:T(8,128)(2,1)} %bitcast.52, ...), custom_call_target="tpu_custom_call" | custom-call | flops 36238786560 | bytes 204472320 | tf_op jit(solution)/shard_map/expert_block/pallas_call | solution.py:237
  603.3 10.1 %pair_sum.9 = f32[10240,128]{1,0:T(8,128)} custom-call(f32[10240,128]{1,0:T(8,128)} %get-tuple-element.39.keep, f32[10240,128]{1,0:T(8,128)} %get-tuple-element.40.send), custom_call_target="tpu_custom_call" | custom-call | flops 5242880000 | bytes 20971520 | tf_op jit(solution)/shard_map/pair_sum/pallas_call | solution.py:304
  613.4 0.7 reduce-scatter.10.cloned.1.call-update
  614.2 0.7 reduce-scatter.12.cloned.1.call-update
  614.9 1.4 convert_element_type.112
  616.3 0.7 convert_element_type.113
  617.0 0.9 constant_dynamic-update-slice_fusion.4
  617.9 1.9 convert_element_type.116
  619.8 1.5 convert_element_type.117
  621.3 1.1 constant_dynamic-update-slice_fusion.3
  622.4 101.6 %reduce-scatter.14.cloned.1.call-done = f32[2560,128]{1,0:T(8,128)} async-done(((f32[10240,128]{1,0:T(8,128)}), f32[2560,128]{1,0:T(8,128)}) %reduce-scatter.14.cloned.1.call-update) | async-done | bytes 1310736 | tf_op jit(solution)/shard_map/reduce_scatter | solution.py:391
  724.1 1.4 convert_element_type.126
  725.5 0.7 convert_element_type.127
  726.2 98.8 %reduce-scatter.10.cloned.1.call-done = f32[5120,128]{1,0:T(8,128)} async-done(((f32[20480,128]{1,0:T(8,128)}), f32[5120,128]{1,0:T(8,128)}) %reduce-scatter.10.cloned.1.call-update) | async-done | bytes 2621456 | tf_op jit(solution)/shard_map/reduce_scatter | solution.py:391
  825.0 1.9 convert_element_type.120
  826.9 1.5 convert_element_type.121
  828.4 97.6 %reduce-scatter.12.cloned.1.call-done = f32[5120,128]{1,0:T(8,128)} async-done(((f32[20480,128]{1,0:T(8,128)}), f32[5120,128]{1,0:T(8,128)}) %reduce-scatter.12.cloned.1.call-update) | async-done | bytes 2621456 | tf_op jit(solution)/shard_map/reduce_scatter | solution.py:391
  926.0 2.9 convert_element_type.124
  928.9 2.9 convert_element_type.125
  931.8 1.1 constant_dynamic-update-slice_fusion.2
  933.0 1.1 constant_dynamic-update-slice_fusion.1
  934.1 0.9 constant_dynamic-update-slice_fusion
  (98 shorter events, 9.6 us)
Async XLA Ops:
  6.5 42.3 %all-gather.9.cloned.1.call-start = ((), (), s32[]{:S(2)}) async-start(), calls=%async_computation.10 | async-start | bytes 5898240 | tf_op jit(solution)/shard_map/all_gather | solution.py:383
  8.5 135.5 %all-gather.11.cloned.1.call-start = ((), (), s32[]{:S(2)}) async-start(), calls=%async_computation.11 | async-start | bytes 11796480 | tf_op jit(solution)/shard_map/all_gather | solution.py:383
  11.1 4.1 copy-start.8
  11.1 4.1 copy-start.9
  11.1 4.1 copy-start.10
  11.1 21.3 %copy-start.15 = (s32[8]{0:T(128)S(1)}, s32[8]{0:T(128)}, u32[]{:S(2)}) copy-start(s32[8]{0:T(128)} %constant.115.clone) | copy-start | bytes 100
  11.1 261.9 %all-gather.13.cloned.1.call-start = ((), (), s32[]{:S(2)}) async-start(), calls=%async_computation.12 | async-start | bytes 29491200 | tf_op jit(solution)/shard_map/all_gather | solution.py:383
  15.1 22.7 %copy-start.12 = (s32[5]{0:T(128)S(1)}, s32[5]{0:T(128)}, u32[]{:S(2)}) copy-start(s32[5]{0:T(128)} %constant.116.clone) | copy-start | bytes 64
  15.1 599.8 %reduce-scatter.6.cloned.1.call-start = ((), (), s32[]{:S(2)}) async-start(), calls=%async_computation.5 | async-start | bytes 6553600 | tf_op jit(solution)/shard_map/reduce_scatter | solution.py:391
  35.0 0.7 copy-start
  40.7 0.7 copy-start.2
  139.6 1.0 copy-start.1
  139.7 3.6 copy-start.3
  139.7 478.2 %reduce-scatter.8.cloned.1.call-start = ((), (), s32[]{:S(2)}) async-start(), calls=%async_computation.6 | async-start | bytes 13107200 | tf_op jit(solution)/shard_map/reduce_scatter | solution.py:391
  269.0 0.8 copy-start.6
  269.0 0.9 copy-start.5
  269.0 1.5 copy-start.11
  269.1 1.6 copy-start.4
  269.1 2.2 copy-start.7
  269.1 2.8 copy-start.14
  269.1 3.4 copy-start.13
  269.1 455.0 %reduce-scatter.14.cloned.1.call-start = ((), (), s32[]{:S(2)}) async-start(), calls=%async_computation.9 | async-start | bytes 6553600 | tf_op jit(solution)/shard_map/reduce_scatter | solution.py:391
  613.4 211.6 %reduce-scatter.10.cloned.1.call-start = ((), (), s32[]{:S(2)}) async-start(), calls=%async_computation.7 | async-start | bytes 13107200 | tf_op jit(solution)/shard_map/reduce_scatter | solution.py:391
  614.1 311.8 %reduce-scatter.12.cloned.1.call-start = ((), (), s32[]{:S(2)}) async-start(), calls=%async_computation.8 | async-start | bytes 13107200 | tf_op jit(solution)/shard_map/reduce_scatter | solution.py:391
Sparse Core Ops, SparseCore 0:
  9.1 39.6 all-gather.8
  50.7 57.5 all-gather.10
  110.1 124.2 all-gather.12
  237.2 55.7 reduce-scatter.5
  295.9 97.9 reduce-scatter.7
  613.5 110.5 reduce-scatter.13
  727.1 97.8 reduce-scatter.9
  828.0 97.8 reduce-scatter.11

commit v7 on v6

--- a/solution.py
+++ b/solution.py
@@ -19,8 +19,8 @@
 PIECES = 8
 
 
-def expert_kernel(row0, row_sizes, meta, gate, pos, digits, tok_hbm, wg_hbm, wu_hbm, wd_hbm, *refs):
-    outs, (tok, acc, wg, wu, wd, onehot, x, h, o, idx_v, idx_s, up_sem, down_sem, tok_sem, idx_sem, out_sem) = refs[:2], refs[2:]
+def expert_kernel(row0, row_sizes, split, meta, gate, pos, digits, tok_hbm, wg_hbm, wu_hbm, wd_hbm, *refs):
+    outs, (tok, acc, wg, wu, wd, onehot, x, h, o, idx_v, idx_s, up_sem, down_sem, tok_sem, idx_sem, out_sem) = refs[:1 + split], refs[1 + split:]
     num_tok, d_model = tok.shape
     shards = tok_hbm.shape[0]
     tc = num_tok // shards
@@ -74,15 +74,16 @@
 
     def dispatch(rows, e, row0, p0, half, first, width):
         start = pl.multiple_of(first * UNIT, UNIT)
+        step = 16 if rows % 32 else 32
 
         def select(i, c):
-            row = pl.multiple_of(i * 16, 16)
-            want = lax.broadcasted_iota(jnp.int32, (16, width), 0) + (p0 + row)
+            row = pl.multiple_of(i * step, step)
+            want = lax.broadcasted_iota(jnp.int32, (step, width), 0) + (p0 + row)
             here = pos[e, :, pl.ds(start, width)]
-            onehot[pl.ds(row, 16), :width] = jnp.where(want == here, 1.0, 0.0).astype(jnp.bfloat16)
-            return c
-
-        lax.fori_loop(0, rows // 16, select, 0)
+            onehot[pl.ds(row, step), :width] = jnp.where(want == here, 1.0, 0.0).astype(jnp.bfloat16)
+            return c
+
+        lax.fori_loop(0, rows // step, select, 0)
         parts = lax.dot_general(digits[:, :width], onehot[:rows, :width], (((1,), (1,)), ((), ())), preferred_element_type=jnp.float32)
         here = parts[0:1] * ID_RADIX + parts[1:2] + (parts[2:3] * start.astype(jnp.float32) + (1.0 - parts[2:3]) * num_tok)
         idx_v[pl.ds(pl.multiple_of(half * 8, 8), 8), :rows] = jnp.broadcast_to(here.astype(jnp.int32), (8, rows))
@@ -207,18 +208,21 @@
     lax.fori_loop(0, num_items, item_body, 0)
     out_copies = []
     size = tc * lines
-    for s in range(shards // 2):
-        dst = pl.ds(s * size, size)
-        mine = pl.ds(pl.multiple_of((2 * s + parity) * size, size), size)
-        other = pl.ds(pl.multiple_of((2 * s + 1 - parity) * size, size), size)
-        out_copies.append(pltpu.make_async_copy(acc.at[other, :], outs[1].at[dst, :], out_sem.at[s, 0]))
-        out_copies.append(pltpu.make_async_copy(acc.at[mine, :], outs[0].at[dst, :], out_sem.at[s, 1]))
+    if split:
+        for s in range(shards // 2):
+            dst = pl.ds(s * size, size)
+            mine = pl.ds(pl.multiple_of((2 * s + parity) * size, size), size)
+            other = pl.ds(pl.multiple_of((2 * s + 1 - parity) * size, size), size)
+            out_copies.append(pltpu.make_async_copy(acc.at[other, :], outs[1].at[dst, :], out_sem.at[s, 0]))
+            out_copies.append(pltpu.make_async_copy(acc.at[mine, :], outs[0].at[dst, :], out_sem.at[s, 1]))
+    else:
+        out_copies.append(pltpu.make_async_copy(acc.at[pl.ds(0, shards * size), :], outs[0], out_sem.at[0, 0]))
     start_all(out_copies)
     for cp in out_copies:
         cp.wait()
 
 
-def expert_block(row0, units, meta, gate, pos, digits, tok, w_gate, w_up, w_down):
+def expert_block(row0, units, split, meta, gate, pos, digits, tok, w_gate, w_up, w_down):
     shards, _, d_model = tok.shape
     num_tok = shards * units * UNIT
     num_local, _, ff_dim = w_gate.shape
@@ -228,17 +232,17 @@
     rows = num_tok * 3 // 4
     max_rows = ROW_SIZES[units][-1]
     lines = d_model // LANES
-    out = jax.ShapeDtypeStruct((num_tok // 2 * lines, LANES), jnp.float32)
+    out = jax.ShapeDtypeStruct((num_tok // (1 + split) * lines, LANES), jnp.float32)
     up_steps = ff_dim // FF_BLOCK
 
     def body(*refs):
-        expert_kernel(row0, ROW_SIZES[units], *refs)
+        expert_kernel(row0, ROW_SIZES[units], split, *refs)
 
     return pl.pallas_call(
         body,
-        out_shape=(out, out),
+        out_shape=(out,) * (1 + split),
         in_specs=[smem, smem, vmem, vmem, anym, anym, anym, anym],
-        out_specs=(anym, anym),
+        out_specs=(anym,) * (1 + split),
         scratch_shapes=[
             pltpu.VMEM((num_tok, d_model), jnp.bfloat16),
             pltpu.VMEM(((num_tok + 8) * lines, LANES), jnp.float32),
@@ -387,8 +391,8 @@
         outs = []
         last = None
 
-        def reduce(part):
-            part = lax.psum_scatter(part, 'ep', scatter_dimension=0, tiled=True, axis_index_groups=same_core)
+        def reduce(part, c):
+            part = lax.psum_scatter(part, 'ep', scatter_dimension=0, tiled=True, axis_index_groups=same_core if c > 0 else None)
             return part.reshape(-1, tokens.shape[1]).astype(jnp.bfloat16)
 
         for c, units in enumerate(CHUNK_UNITS):
@@ -398,10 +402,10 @@
             meta, gate, pos = tables[c]
             if last is not None:
                 meta, last = lax.optimization_barrier((meta, last))
-                outs.append(reduce(last))
-            last = expert_block(row0, units, meta, gate, pos, digits, tok, w_gate, w_up, w_down)
-            last = pair_sum(*last, c)
-        outs.append(reduce(last))
+                outs.append(reduce(last, c - 1))
+            last = expert_block(row0, units, c > 0, meta, gate, pos, digits, tok, w_gate, w_up, w_down)
+            last = pair_sum(*last, c) if c > 0 else last[0]
+        outs.append(reduce(last, len(CHUNK_UNITS) - 1))
         return jnp.concatenate(outs, axis=0)
 
     return jax.shard_map(layer, mesh=mesh, in_specs=(row_spec, row_spec, row_spec, row_spec, expert_spec, expert_spec, expert_spec), out_specs=row_spec, check_vma=False)

time: 943 us -> 931 us (0.987)
    pallas_call x5 -> x4, Pallas kernels: 75.6 us -> 71.9 us  [pair_sum(): pl.pallas_call(pair_kernel, out_shape=jax.ShapeDtypeStruct((rows, d_model...]
where the time goes in v7:
time: 931 us; the launch traced here: 930 us
  Pallas kernels  551 us (59%)
  waiting for transfers between devices  300 us (32%)
  local copies, waits for them, and re-layouts  32 us (3%)
  blocking collectives  16.6 us (2%)
  other arithmetic  15.7 us (2%)
  between operations  14 us (2%)
    pallas_call x5, Pallas kernels, expert_block(): pl.pallas_call(body, out_shape=(out,) * (1 + split), in_specs=[smem, smem...  479 us
    reduce_scatter x5, waiting for transfers between devices, reduce(): lax.psum_scatter(part, 'ep', scatter_dimension=0, tiled=True, axis_index_...  291 us
    pallas_call x4, Pallas kernels, pair_sum(): pl.pallas_call(pair_kernel, out_shape=jax.ShapeDtypeStruct((rows, d_model...  71.9 us
  transfers between devices with their start and end apart: 8, of which 4 were waited for; matrix products, arithmetic and copies ran while one was open for 4% of the time, Pallas kernels for 59%

profile of v7, /device:TPU:0, one launch (start us, length us, event | category | flops | bytes accessed | tf_op | source)
XLA Modules:
  0.0 929.8 jit_solution(5540752342958020983)
XLA Ops:
  6.5 2.0 slice.87
  8.6 2.5 slice.92
  11.2 3.8 slice.97
  15.2 16.6 %all-gather.4 = f32[8,12,1024]{2,1,0:T(8,128)S(1)} all-gather(f32[1,12,1024]{2,1,0:T(8,128)S(1)} %maximum_bitcast_fusion), channel_id=2, replica_groups=mesh['dp'=1,'ep'=8] {'ep'}, dimensions={0}, use_global_device_ids=true | all-gather | bytes 442368 | tf_op jit(solution)/shard_map/all_gather | solution.py:331
  32.9 0.7 slice_convert_fusion.1
  34.6 0.7 copy-done
  35.3 0.6 fusion.15
  36.6 0.6 stack.6.refs_3_
  38.8 0.6 pad_add_fusion.5
  40.2 0.7 copy-done.2
  40.9 0.7 slice_bitcast_fusion.2
  41.5 7.3 all-gather.9.cloned.1.call-done
  48.8 80.3 %expert_block.5 = f32[20480,128]{1,0:T(8,128)} custom-call(s32[320]{0:T(512)} %pad_add_fusion.1.refs_0_, f32[8320]{0:T(1024)} %pad.17.refs_1_, s32[8,1,1024]{2,1,0:T(1,128)} %get-tuple-element.45.refs_2_, bf16[8,1024]{1,0:T(8,128)(2,1)} %stack.6.refs_3_, bf16[8,128,2560]{2,1,0:T(8,128)(2,1)} %bitcast.53, bf16[8,2560,1536]{2,1,0:T(8,128)(2,1)} %refs_5_.9, ...), custom_call_target="tpu_custom_call" | custom-call | flops 36238786560 | bytes 204472320 | tf_op jit(solution)/shard_map/expert_block/pallas_call | solution.py:241
  129.2 0.6 copy-done.7
  130.1 0.7 fusion.17
  130.8 0.6 pad.18.refs_1_
  131.5 0.7 stack.7.refs_3_
  132.7 0.7 fusion.16
  133.5 106.7 %expert_block.6 = (f32[20480,128]{1,0:T(8,128)}, f32[20480,128]{1,0:T(8,128)}) custom-call(s32[384]{0:T(512)} %pad_add_fusion.refs_0_, f32[16512]{0:T(1024)} %pad.18.refs_1_, s32[8,1,2048]{2,1,0:T(1,128)} %bitcast.62, bf16[8,2048]{1,0:T(8,128)(2,1)} %stack.7.refs_3_, bf16[8,256,2560]{2,1,0:T(8,128)(2,1)} %bitcast.69, bf16[8,2560,1536]{2,1,0:T(8,128)(2,1)} %refs_5_.9, ...), custom_call_target="tpu_custom_call" | custom-call | flops 72477573120 | bytes 220200960 | tf_op jit(solution)/shard_map/expert_block/pallas_call | solution.py:241
  240.2 24.2 %pair_sum.4 = f32[20480,128]{1,0:T(8,128)} custom-call(f32[20480,128]{1,0:T(8,128)} %get-tuple-element.23.keep, f32[20480,128]{1,0:T(8,128)} %get-tuple-element.24.send), custom_call_target="tpu_custom_call" | custom-call | flops 10485760000 | bytes 41943040 | tf_op jit(solution)/shard_map/pair_sum/pallas_call | solution.py:308
  265.2 0.6 pad.19.refs_1_
  265.9 0.6 pad.20.refs_1_
  268.2 107.5 %expert_block.7 = (f32[20480,128]{1,0:T(8,128)}, f32[20480,128]{1,0:T(8,128)}) custom-call(s32[384]{0:T(512)} %pad_add_fusion.2.refs_0_, f32[16512]{0:T(1024)} %pad.19.refs_1_, s32[8,1,2048]{2,1,0:T(1,128)} %bitcast.61, bf16[8,2048]{1,0:T(8,128)(2,1)} %stack.7.refs_3_, bf16[8,640,2560]{2,1,0:T(8,128)(2,1)} %bitcast.50, bf16[8,2560,1536]{2,1,0:T(8,128)(2,1)} %refs_5_.9, ...), custom_call_target="tpu_custom_call" | custom-call | flops 72477573120 | bytes 220200960 | tf_op jit(solution)/shard_map/expert_block/pallas_call | solution.py:241
  375.7 17.9 %pair_sum.5 = f32[20480,128]{1,0:T(8,128)} custom-call(f32[20480,128]{1,0:T(8,128)} %get-tuple-element.27.keep, f32[20480,128]{1,0:T(8,128)} %get-tuple-element.28.send), custom_call_target="tpu_custom_call" | custom-call | flops 10485760000 | bytes 41943040 | tf_op jit(solution)/shard_map/pair_sum/pallas_call | solution.py:308
  393.6 105.7 %expert_block.8 = (f32[20480,128]{1,0:T(8,128)}, f32[20480,128]{1,0:T(8,128)}) custom-call(s32[384]{0:T(512)} %pad_add_fusion.3.refs_0_, f32[16512]{0:T(1024)} %pad.20.refs_1_, s32[8,1,2048]{2,1,0:T(1,128)} %bitcast.60, bf16[8,2048]{1,0:T(8,128)(2,1)} %stack.7.refs_3_, bf16[8,640,2560]{2,1,0:T(8,128)(2,1)} %bitcast.51, bf16[8,2560,1536]{2,1,0:T(8,128)(2,1)} %refs_5_.9, ...), custom_call_target="tpu_custom_call" | custom-call | flops 72477573120 | bytes 220200960 | tf_op jit(solution)/shard_map/expert_block/pallas_call | solution.py:241
  499.4 19.8 %pair_sum.6 = f32[20480,128]{1,0:T(8,128)} custom-call(f32[20480,128]{1,0:T(8,128)} %get-tuple-element.31.keep, f32[20480,128]{1,0:T(8,128)} %get-tuple-element.32.send), custom_call_target="tpu_custom_call" | custom-call | flops 10485760000 | bytes 41943040 | tf_op jit(solution)/shard_map/pair_sum/pallas_call | solution.py:308
  519.1 79.0 %expert_block.9 = (f32[10240,128]{1,0:T(8,128)}, f32[10240,128]{1,0:T(8,128)}) custom-call(s32[320]{0:T(512)} %pad_add_fusion.4.refs_0_, f32[8320]{0:T(1024)} %pad.21.refs_1_, s32[8,1,1024]{2,1,0:T(1,128)} %get-tuple-element.44.refs_2_, bf16[8,1024]{1,0:T(8,128)(2,1)} %stack.6.refs_3_, bf16[8,640,2560]{2,1,0:T(8,128)(2,1)} %bitcast.52, ...), custom_call_target="tpu_custom_call" | custom-call | flops 36238786560 | bytes 204472320 | tf_op jit(solution)/shard_map/expert_block/pallas_call | solution.py:241
  598.1 10.1 %pair_sum.7 = f32[10240,128]{1,0:T(8,128)} custom-call(f32[10240,128]{1,0:T(8,128)} %get-tuple-element.35.keep, f32[10240,128]{1,0:T(8,128)} %get-tuple-element.36.send), custom_call_target="tpu_custom_call" | custom-call | flops 5242880000 | bytes 20971520 | tf_op jit(solution)/shard_map/pair_sum/pallas_call | solution.py:308
  608.3 0.7 reduce-scatter.10.cloned.1.call-update
  609.1 0.7 reduce-scatter.12.cloned.1.call-update
  609.8 1.4 convert_element_type.112
  611.2 0.7 convert_element_type.113
  611.9 0.9 constant_dynamic-update-slice_fusion.4
  612.8 1.9 convert_element_type.116
  614.7 1.5 convert_element_type.117
  616.2 1.1 constant_dynamic-update-slice_fusion.3
  617.3 94.6 %reduce-scatter.14.cloned.1.call-done = f32[2560,128]{1,0:T(8,128)} async-done(((f32[10240,128]{1,0:T(8,128)}), f32[2560,128]{1,0:T(8,128)}) %reduce-scatter.14.cloned.1.call-update) | async-done | bytes 1310736 | tf_op jit(solution)/shard_map/reduce_scatter | solution.py:395
  711.9 1.4 convert_element_type.126
  713.3 0.7 convert_element_type.127
  714.1 98.9 %reduce-scatter.10.cloned.1.call-done = f32[5120,128]{1,0:T(8,128)} async-done(((f32[20480,128]{1,0:T(8,128)}), f32[5120,128]{1,0:T(8,128)}) %reduce-scatter.10.cloned.1.call-update) | async-done | bytes 2621456 | tf_op jit(solution)/shard_map/reduce_scatter | solution.py:395
  812.9 1.9 convert_element_type.120
  814.8 1.5 convert_element_type.121
  816.3 97.6 %reduce-scatter.12.cloned.1.call-done = f32[5120,128]{1,0:T(8,128)} async-done(((f32[20480,128]{1,0:T(8,128)}), f32[5120,128]{1,0:T(8,128)}) %reduce-scatter.12.cloned.1.call-update) | async-done | bytes 2621456 | tf_op jit(solution)/shard_map/reduce_scatter | solution.py:395
  913.9 2.9 convert_element_type.124
  916.9 2.9 convert_element_type.125
  919.8 1.1 constant_dynamic-update-slice_fusion.2
  920.9 1.1 constant_dynamic-update-slice_fusion.1
  922.1 0.9 constant_dynamic-update-slice_fusion
  (95 shorter events, 8.7 us)
Async XLA Ops:
  6.5 42.3 %all-gather.9.cloned.1.call-start = ((), (), s32[]{:S(2)}) async-start(), calls=%async_computation.10 | async-start | bytes 5898240 | tf_op jit(solution)/shard_map/all_gather | solution.py:387
  8.5 124.9 %all-gather.11.cloned.1.call-start = ((), (), s32[]{:S(2)}) async-start(), calls=%async_computation.11 | async-start | bytes 11796480 | tf_op jit(solution)/shard_map/all_gather | solution.py:387
  11.1 4.0 copy-start.8
  11.1 4.0 copy-start.9
  11.1 4.0 copy-start.10
  11.1 21.3 %copy-start.14 = (s32[8]{0:T(128)S(1)}, s32[8]{0:T(128)}, u32[]{:S(2)}) copy-start(s32[8]{0:T(128)} %constant.115.clone) | copy-start | bytes 100
  11.1 257.1 %all-gather.13.cloned.1.call-start = ((), (), s32[]{:S(2)}) async-start(), calls=%async_computation.12 | async-start | bytes 29491200 | tf_op jit(solution)/shard_map/all_gather | solution.py:387
  15.0 22.2 %copy-start.11 = (s32[5]{0:T(128)S(1)}, s32[5]{0:T(128)}, u32[]{:S(2)}) copy-start(s32[5]{0:T(128)} %constant.116.clone) | copy-start | bytes 64
  15.0 594.7 %reduce-scatter.6.cloned.1.call-start = ((), (), s32[]{:S(2)}) async-start(), calls=%async_computation.5 | async-start | bytes 11796480 | tf_op jit(solution)/shard_map/reduce_scatter | solution.py:395
  34.6 0.7 copy-start
  40.2 0.7 copy-start.2
  129.1 0.8 copy-start.7
  129.1 1.0 copy-start.1
  129.1 3.1 copy-start.13
  129.1 3.6 copy-start.3
  129.2 483.6 %reduce-scatter.8.cloned.1.call-start = ((), (), s32[]{:S(2)}) async-start(), calls=%async_computation.6 | async-start | bytes 13107200 | tf_op jit(solution)/shard_map/reduce_scatter | solution.py:395
  264.4 0.8 copy-start.5
  264.4 1.5 copy-start.4
  264.4 2.2 copy-start.6
  264.4 2.8 copy-start.12
  264.4 447.5 %reduce-scatter.14.cloned.1.call-start = ((), (), s32[]{:S(2)}) async-start(), calls=%async_computation.9 | async-start | bytes 6553600 | tf_op jit(solution)/shard_map/reduce_scatter | solution.py:395
  608.3 204.7 %reduce-scatter.10.cloned.1.call-start = ((), (), s32[]{:S(2)}) async-start(), calls=%async_computation.7 | async-start | bytes 13107200 | tf_op jit(solution)/shard_map/reduce_scatter | solution.py:395
  609.0 304.9 %reduce-scatter.12.cloned.1.call-start = ((), (), s32[]{:S(2)}) async-start(), calls=%async_computation.8 | async-start | bytes 13107200 | tf_op jit(solution)/shard_map/reduce_scatter | solution.py:395
Sparse Core Ops, SparseCore 0:
  9.1 39.6 all-gather.8
  50.6 57.5 all-gather.10
  110.0 124.2 all-gather.12
  237.7 73.6 reduce-scatter.5
  314.3 97.8 reduce-scatter.7
  608.4 103.5 reduce-scatter.13
  715.0 97.9 reduce-scatter.9
  816.0 97.9 reduce-scatter.11
